TPU v7x, 32 devices: a whole 2x2x4 slice. The times are simulated.
32 devices in a mesh: fsdp: 8 (over z, x), tp: 4 (over y, core).
Axes of the slice: x: 2, y: 2, z: 4, core: 2. Of those that a mesh axis runs over, the one named last changes fastest.
Arguments:
- hidden_in: bfloat16 [3, 2048, 2048], P(None, ('fsdp', 'tp')), may hold values from -6 to 6
- cotangent: float32 [3, 2048, 2048], P(None, ('fsdp', 'tp')), may hold values from -6 to 6
- gain_attn: float32 [2048], P(('fsdp', 'tp')), may hold values from 0.1 to 1.9
- w_query: bfloat16 [2048, 2048], P('fsdp', 'tp'), may hold values from -0.125 to 0.125
- w_key: bfloat16 [2048, 256], P('fsdp', 'tp'), may hold values from -0.125 to 0.125
- w_value: bfloat16 [2048, 256], P('fsdp', 'tp'), may hold values from -0.125 to 0.125
- w_out: bfloat16 [2048, 2048], P('tp', 'fsdp'), may hold values from -3 to 3
- gain_mlp: float32 [2048], P(('fsdp', 'tp')), may hold values from 0.1 to 1.9
- w_gate: bfloat16 [2048, 5632], P('fsdp', 'tp'), may hold values from -0.125 to 0.125
- w_up: bfloat16 [2048, 5632], P('fsdp', 'tp'), may hold values from -0.125 to 0.125
- w_down: bfloat16 [5632, 2048], P('tp', 'fsdp'), may hold values from -0.078125 to 0.078125
- prefix: int32 [3], replicated, may hold values from 204 to 1024
- block_order: int32 [3, 8], replicated, may hold values from 0 to 7, each once within a row
Outputs:
- layer_out: float32 [3, 2048, 2048], P(None, ('fsdp', 'tp'))
- grad_in: float32 [3, 2048, 2048], P(None, ('fsdp', 'tp'))
- grad_attn: float32 [2048], P(('fsdp', 'tp'))
- grad_query: float32 [2048, 2048], P('fsdp', 'tp')
- grad_key: float32 [2048, 256], P('fsdp', 'tp')
- grad_value: float32 [2048, 256], P('fsdp', 'tp')
- grad_out: float32 [2048, 2048], P('tp', 'fsdp')
- grad_mlp: float32 [2048], P(('fsdp', 'tp'))
- grad_gate: float32 [2048, 5632], P('fsdp', 'tp')
- grad_up: float32 [2048, 5632], P('fsdp', 'tp')
- grad_down: float32 [5632, 2048], P('tp', 'fsdp')
Inputs may be any that keep to these rules, and one draw needn't show every extreme that they name: `prefix`: the number of leading positions of each sequence that attend to one another in both directions. `block_order`: row s names, for each stored block of 256 rows of sequence s in order, which block of positions it holds; each block once.
All inputs are finite; a program needn't handle non-finite values.
Results may differ from a plain program's by a relative error of at most 0.02.
Values may be sent and summed in bfloat16 or wider, within the bound.
A program may use at most 832 MiB of HBM per device.

v0:
```python
import jax
import jax.numpy as jnp
from jax import lax
from jax.sharding import PartitionSpec as P

HD = 64


EPS = 1e-05
THETA = 10000.0
NEG = -1000000000.0


def inverse_rms(values):
    return lax.rsqrt(jnp.mean(values * values, axis=-1, keepdims=True) + EPS)


def norm_back(upstream, values, gain_vec, inv_rms):
    weighted = upstream * gain_vec
    inner_mean = jnp.mean(weighted * values, axis=-1, keepdims=True)
    return (
        inv_rms * weighted - values * (inv_rms * inv_rms * inv_rms) * inner_mean,
        jnp.sum(upstream * values * inv_rms, axis=(0, 1)),
    )


def rope_tables(positions, head_width):
    halfway = head_width // 2
    frequency = THETA ** (-(jnp.arange(halfway, dtype=jnp.float32) * 2.0 / head_width))
    angles = positions.astype(jnp.float32)[..., None] * frequency
    cos_half = jnp.cos(angles)
    sin_half = jnp.sin(angles)
    return (
        jnp.concatenate([cos_half, cos_half], -1)[..., None, :],
        jnp.concatenate([sin_half, sin_half], -1)[..., None, :],
    )


def rotate(values, cos_part, sin_part):
    halfway = values.shape[-1] // 2
    turned = jnp.concatenate([-values[..., halfway:], values[..., :halfway]], -1)
    return values * cos_part + turned * sin_part


def rotate_back(upstream, cos_part, sin_part):
    halfway = upstream.shape[-1] // 2
    moved = upstream * sin_part
    return upstream * cos_part + jnp.concatenate([moved[..., halfway:], -moved[..., :halfway]], -1)


def spread_rows(values):
    return lax.all_gather(values, "tp", axis=1, tiled=True)


def collect_rows(values):
    return lax.psum_scatter(values, "tp", scatter_dimension=1, tiled=True)


def attn_rows(w_query, w_key, w_value):
    return (
        lax.all_gather(w_query, "fsdp", axis=0, tiled=True),
        lax.all_gather(w_key, "fsdp", axis=0, tiled=True),
        lax.all_gather(w_value, "fsdp", axis=0, tiled=True),
    )


def mlp_rows(w_gate, w_up):
    return (
        lax.all_gather(w_gate, "fsdp", axis=0, tiled=True),
        lax.all_gather(w_up, "fsdp", axis=0, tiled=True),
    )


def out_cols(weight):
    return lax.all_gather(weight, "fsdp", axis=1, tiled=True)


def transposed_product(operand, partner):
    return lax.dot_general(
        operand, partner, (((1,), (1,)), ((), ())), preferred_element_type=jnp.float32
    )


def grad_term(operand, partner):

    def term_rows(row_start, row_count):
        return lax.dot_general(
            operand, partner, (((0,), (0,)), ((), ())), preferred_element_type=jnp.float32
        )

    return term_rows


def reduce_grads(term_rows, row_count):
    return lax.psum_scatter(
        term_rows(jnp.int32(0), row_count * lax.axis_size("fsdp")).astype(jnp.bfloat16),
        "fsdp",
        scatter_dimension=0,
        tiled=True,
    ).astype(jnp.float32)


def on_device(
    hidden_in,
    cotangent,
    gain_attn,
    w_query,
    w_key,
    w_value,
    w_out,
    gain_mlp,
    w_gate,
    w_up,
    w_down,
    prefix,
    block_order,
):
    seq_count, own_rows, model_width = hidden_in.shape
    tp_count = lax.axis_size("tp")
    fsdp_count = lax.axis_size("fsdp")
    block_len = own_rows * tp_count
    seq_len = block_len * fsdp_count
    heads_here = w_query.shape[1] // HD
    kv_here = w_key.shape[1] // HD
    group_size = heads_here // kv_here
    kv_width = kv_here * HD
    query_width = heads_here * HD
    token_count = seq_count * block_len
    grad_rows = model_width // fsdp_count
    scale_factor = HD ** (-0.5)
    full_gains = (
        lax.all_gather(gain_attn, ("fsdp", "tp"), axis=0, tiled=True),
        lax.all_gather(gain_mlp, ("fsdp", "tp"), axis=0, tiled=True),
    )
    gain_first = full_gains[0]
    gain_second = full_gains[1]
    fsdp_index = lax.axis_index("fsdp")
    indices = jnp.arange(fsdp_count, dtype=jnp.int32)
    own_block = jnp.sum(jnp.where(indices[None, :] == fsdp_index, block_order, 0), axis=1)
    offsets = jnp.arange(block_len, dtype=jnp.int32)
    query_pos = own_block[:, None] * block_len + offsets[None, :]
    key_pos = (block_order[:, :, None] * block_len + offsets[None, None, :]).reshape(
        seq_count, seq_len
    )
    cos_part, sin_part = rope_tables(query_pos, HD)
    input_f = hidden_in.astype(jnp.float32)
    rms_first = inverse_rms(input_f)
    h_first = spread_rows((input_f * rms_first * gain_first).astype(jnp.bfloat16))
    flat_first = h_first.reshape(token_count, model_width)
    full_query, full_key, full_value = attn_rows(w_query, w_key, w_value)
    query_raw = jnp.dot(flat_first, full_query, preferred_element_type=jnp.float32).reshape(
        seq_count, block_len, heads_here, HD
    )
    key_raw = jnp.dot(flat_first, full_key, preferred_element_type=jnp.float32).reshape(
        seq_count, block_len, kv_here, HD
    )
    value_raw = jnp.dot(flat_first, full_value, preferred_element_type=jnp.float32)
    queries = rotate(query_raw, cos_part, sin_part).astype(jnp.bfloat16)
    keys_own = (
        rotate(key_raw, cos_part, sin_part)
        .astype(jnp.bfloat16)
        .reshape(seq_count, block_len, kv_width)
    )
    values_own = value_raw.astype(jnp.bfloat16).reshape(seq_count, block_len, kv_width)
    pairs = lax.all_gather(jnp.concatenate([keys_own, values_own], -1), "fsdp", axis=1, tiled=True)

    def split_pair(pair_block):
        key_block = pair_block[:, :kv_width].reshape(seq_len, kv_here, HD)
        value_block = pair_block[:, kv_width:].reshape(seq_len, kv_here, HD)
        return (key_block, value_block)

    def masked_scores(grouped, key_block, row_pos, col_pos, prefix_len):
        scores = (
            jnp.einsum("qcgd,kcd->cgqk", grouped, key_block, preferred_element_type=jnp.float32)
            * scale_factor
        )
        allowed = (col_pos[None, :] <= row_pos[:, None]) | (col_pos[None, :] < prefix_len)
        return jnp.where(allowed, scores, NEG)

    def forward_one(inputs):
        query_block, pair_block, row_pos, col_pos, prefix_len = inputs
        key_block, value_block = split_pair(pair_block)
        grouped = query_block.reshape(block_len, kv_here, group_size, HD)
        scores = masked_scores(grouped, key_block, row_pos, col_pos, prefix_len)
        highest = jnp.max(scores, axis=-1, keepdims=True)
        shifted = jnp.exp(scores - highest)
        totals = jnp.sum(shifted, axis=-1, keepdims=True)
        weights = (shifted / totals).astype(jnp.bfloat16)
        mixed = jnp.einsum(
            "cgqk,kcd->qcgd", weights, value_block, preferred_element_type=jnp.float32
        )
        return (mixed.reshape(block_len, query_width), (highest + jnp.log(totals))[..., 0])

    attn_mixed, log_totals = lax.map(forward_one, (queries, pairs, query_pos, key_pos, prefix))
    attended = attn_mixed.astype(jnp.bfloat16).reshape(token_count, query_width)
    full_out = out_cols(w_out)
    middle = input_f + collect_rows(
        jnp.dot(attended, full_out, preferred_element_type=jnp.float32).reshape(
            seq_count, block_len, model_width
        )
    )
    rms_second = inverse_rms(middle)
    h_second = spread_rows((middle * rms_second * gain_second).astype(jnp.bfloat16))
    flat_second = h_second.reshape(token_count, model_width)
    full_gate, full_up = mlp_rows(w_gate, w_up)
    gate_act = jnp.dot(flat_second, full_gate, preferred_element_type=jnp.float32)
    up_act = jnp.dot(flat_second, full_up, preferred_element_type=jnp.float32)
    gate_sigmoid = jax.nn.sigmoid(gate_act)
    hidden = (gate_act * gate_sigmoid * up_act).astype(jnp.bfloat16)
    full_down = out_cols(w_down)
    layer_out = middle + collect_rows(
        jnp.dot(hidden, full_down, preferred_element_type=jnp.float32).reshape(
            seq_count, block_len, model_width
        )
    )
    back_gate, back_up = mlp_rows(w_gate, w_up)
    back_down = out_cols(w_down)
    grad_mlp_out = spread_rows(cotangent.astype(jnp.bfloat16)).reshape(token_count, model_width)
    down_term = reduce_grads(grad_term(grad_mlp_out, hidden), grad_rows)
    grad_hidden = transposed_product(grad_mlp_out, back_down)
    grad_gate_act = (
        grad_hidden * up_act * gate_sigmoid * (1.0 + gate_act * (1.0 - gate_sigmoid))
    ).astype(jnp.bfloat16)
    grad_up_act = (grad_hidden * gate_act * gate_sigmoid).astype(jnp.bfloat16)
    mlp_cat = jnp.concatenate([grad_gate_act, grad_up_act], -1)
    mlp_term = reduce_grads(grad_term(flat_second, mlp_cat), grad_rows)
    grad_h_second = transposed_product(grad_gate_act, back_gate) + transposed_product(
        grad_up_act, back_up
    )
    grad_h_second = collect_rows(grad_h_second.reshape(seq_count, block_len, model_width))
    grad_middle_norm, gain_second_sum = norm_back(grad_h_second, middle, gain_second, rms_second)
    grad_middle = cotangent + grad_middle_norm
    back_query, back_key, back_value = attn_rows(w_query, w_key, w_value)
    back_out = out_cols(w_out)
    grad_attn_out = spread_rows(grad_middle.astype(jnp.bfloat16)).reshape(token_count, model_width)
    out_term = reduce_grads(grad_term(grad_attn_out, attended), grad_rows)
    grad_mixed = (
        transposed_product(grad_attn_out, back_out)
        .astype(jnp.bfloat16)
        .reshape(seq_count, block_len, query_width)
    )

    def backward_one(inputs):
        query_block, pair_block, row_pos, col_pos, prefix_len, log_block, grad_block = inputs
        key_block, value_block = split_pair(pair_block)
        grouped = query_block.reshape(block_len, kv_here, group_size, HD)
        scores = masked_scores(grouped, key_block, row_pos, col_pos, prefix_len)
        probs = jnp.exp(scores - log_block[..., None])
        grad_grouped = grad_block.reshape(block_len, kv_here, group_size, HD)
        grad_values = jnp.einsum(
            "cgqk,qcgd->kcd",
            probs.astype(jnp.bfloat16),
            grad_grouped,
            preferred_element_type=jnp.float32,
        )
        grad_probs = jnp.einsum(
            "qcgd,kcd->cgqk", grad_grouped, value_block, preferred_element_type=jnp.float32
        )
        grad_scores = (
            probs * (grad_probs - jnp.sum(probs * grad_probs, axis=-1, keepdims=True))
        ).astype(jnp.bfloat16)
        grad_queries = (
            jnp.einsum("cgqk,kcd->qcgd", grad_scores, key_block, preferred_element_type=jnp.float32)
            * scale_factor
        )
        grad_keys = (
            jnp.einsum("cgqk,qcgd->kcd", grad_scores, grouped, preferred_element_type=jnp.float32)
            * scale_factor
        )
        grad_pair = jnp.concatenate(
            [grad_keys.reshape(seq_len, kv_width), grad_values.reshape(seq_len, kv_width)], -1
        )
        return (grad_queries.reshape(block_len, heads_here, HD), grad_pair)

    grad_queries, grad_pairs = lax.map(
        backward_one, (queries, pairs, query_pos, key_pos, prefix, log_totals, grad_mixed)
    )
    grad_pairs = lax.psum_scatter(
        grad_pairs.astype(jnp.bfloat16), "fsdp", scatter_dimension=1, tiled=True
    ).astype(jnp.float32)
    grad_query_pre = (
        rotate_back(grad_queries, cos_part, sin_part)
        .astype(jnp.bfloat16)
        .reshape(token_count, query_width)
    )
    grad_key_pre = (
        rotate_back(
            grad_pairs[..., :kv_width].reshape(seq_count, block_len, kv_here, HD),
            cos_part,
            sin_part,
        )
        .astype(jnp.bfloat16)
        .reshape(token_count, kv_width)
    )
    grad_value_pre = grad_pairs[..., kv_width:].astype(jnp.bfloat16).reshape(token_count, kv_width)
    attn_cat = jnp.concatenate([grad_query_pre, grad_key_pre, grad_value_pre], -1)
    attn_term = reduce_grads(grad_term(flat_first, attn_cat), grad_rows)
    grad_h_first = (
        transposed_product(grad_query_pre, back_query)
        + transposed_product(grad_key_pre, back_key)
        + transposed_product(grad_value_pre, back_value)
    )
    grad_h_first = collect_rows(grad_h_first.reshape(seq_count, block_len, model_width))
    grad_input_norm, gain_first_sum = norm_back(grad_h_first, input_f, gain_first, rms_first)
    grad_in = grad_middle + grad_input_norm
    gain_sums = (
        lax.psum_scatter(gain_first_sum, ("fsdp", "tp"), scatter_dimension=0, tiled=True),
        lax.psum_scatter(gain_second_sum, ("fsdp", "tp"), scatter_dimension=0, tiled=True),
    )
    ff_here = w_gate.shape[1]
    grad_query = attn_term[:, :query_width]
    grad_key = attn_term[:, query_width : query_width + kv_width]
    grad_value = attn_term[:, query_width + kv_width :]
    grad_out = out_term.T
    grad_gate = mlp_term[:, :ff_here]
    grad_up = mlp_term[:, ff_here:]
    grad_down = down_term.T
    return (
        layer_out,
        grad_in,
        gain_sums[0],
        grad_query,
        grad_key,
        grad_value,
        grad_out,
        gain_sums[1],
        grad_gate,
        grad_up,
        grad_down,
    )


def solution(mesh):
    return jax.shard_map(
        on_device,
        mesh=mesh,
        in_specs=(
            P(None, ("fsdp", "tp"), None),
            P(None, ("fsdp", "tp"), None),
            P(("fsdp", "tp")),
            P("fsdp", "tp"),
            P("fsdp", "tp"),
            P("fsdp", "tp"),
            P("tp", "fsdp"),
            P(("fsdp", "tp")),
            P("fsdp", "tp"),
            P("fsdp", "tp"),
            P("tp", "fsdp"),
            P(),
            P(),
        ),
        out_specs=(
            P(None, ("fsdp", "tp"), None),
            P(None, ("fsdp", "tp"), None),
            P(("fsdp", "tp")),
            P("fsdp", "tp"),
            P("fsdp", "tp"),
            P("fsdp", "tp"),
            P("tp", "fsdp"),
            P(("fsdp", "tp")),
            P("fsdp", "tp"),
            P("fsdp", "tp"),
            P("tp", "fsdp"),
        ),
        check_vma=False,
    )
```

profile of v0, /device:TPU:8, one launch (start us, length us, event | category | flops | bytes accessed | tf_op | source)
XLA Modules:
  0.0 1742.9 jit_solution(14243952794122991051)
XLA Ops:
  10.9 40.5 %all-reduce.5 = (f32[2048]{0:T(1024)S(1)}, f32[2048]{0:T(1024)}) all-reduce(f32[2048]{0:T(1024)S(1)} %dynamic-update-slice, f32[2048]{0:T(1024)S(1)} %dynamic-update-slice.1), channel_id=1, replica_groups=mesh['fsdp'=8,'tp'=4] {'fsdp','tp'}, use_global_device_ids=true, to_apply=%add | all-reduce | flops 4096 | bytes 32768
  54.6 30.2 %all_gather.51 = bf16[2048,64]{0,1:T(8,128)(2,1)} all-gather(bf16[256,64]{0,1:T(8,128)(2,1)S(1)} %copy-done.28), channel_id=1, replica_groups=mesh['fsdp'=8,'tp'=4] {'fsdp'}, dimensions={0}, use_global_device_ids=true | all-gather | bytes 294912 | tf_op jit(solution)/shard_map/all_gather | solution.py:62
  84.8 31.6 %all_gather.52 = bf16[2048,64]{0,1:T(8,128)(2,1)S(1)} all-gather(bf16[256,64]{0,1:T(8,128)(2,1)S(1)} %copy-done.29), channel_id=1, replica_groups=mesh['fsdp'=8,'tp'=4] {'fsdp'}, dimensions={0}, use_global_device_ids=true | all-gather | bytes 294912 | tf_op jit(solution)/shard_map/all_gather | solution.py:63
  144.5 40.6 %all-gather.13.cloned.1.call-done = bf16[3,2048,128]{1,0,2:T(4,128)(2,1)} async-done(((bf16[3,256,128]{1,0,2:T(4,128)(2,1)}), bf16[3,2048,128]{1,0,2:T(4,128)(2,1)}) %all-gather.13.cloned.1.call-update) | async-done | bytes 1572880 | tf_op jit(solution)/shard_map/all_gather | solution.py:165
  187.9 88.8 %while.24 = (s32[]{:T(128)}, bf16[3,256,512]{1,2,0:T(8,128)(2,1)}, f32[3,1,8,256]{3,2,1,0:T(8,128)}, bf16[3,2048,128]{1,2,0:T(8,128)(2,1)S(1)}, s32[3,2048]{1,0:...) while((s32[]{:T(128)}, bf16[3,256,512]{1,2,0:T(8,128)(2,1)}, ...), condition=%wide.region_5.6_spmd, body=%wide.region_2.5_spmd.sunk | while | flops 1125122048 | bytes 55147660 | solution.py:194
  191.5 7.4 fusion.141
  198.8 9.2 fusion.142
  208.0 8.1 fusion.143
  221.1 7.2 fusion.141
  228.2 9.2 fusion.142
  237.5 8.1 fusion.143
  250.5 7.2 fusion.141
  257.7 9.2 fusion.142
  266.9 8.1 fusion.143
  283.8 57.5 %reduce-scatter.12.cloned.1.call-done = f32[3,64,2048]{2,1,0:T(8,128)} async-done(((f32[3,256,2048]{2,1,0:T(8,128)}), f32[3,64,2048]{2,1,0:T(8,128)}) %reduce-scatter.12.cloned.1.call-update) | async-done | bytes 1572880 | tf_op jit(solution)/shard_map/reduce_scatter | solution.py:56
  349.1 85.6 %all-gather.23.cloned.1.call-done = bf16[2048,1408]{1,0:T(8,128)(2,1)} async-done(((bf16[256,1408]{1,0:T(8,128)(2,1)}), bf16[2048,1408]{1,0:T(8,128)(2,1)}) %all-gather.23.cloned.1.call-update) | async-done | bytes 5767184 | tf_op jit(solution)/shard_map/all_gather | solution.py:70
  434.6 29.9 %all-gather.19.cloned.1.call-done = bf16[3,256,2048]{2,1,0:T(8,128)(2,1)} async-done(((bf16[3,64,2048]{2,1,0:T(8,128)(2,1)}), bf16[3,256,2048]{2,1,0:T(8,128)(2,1)}) %all-gather.19.cloned.1.call-update) | async-done | bytes 3145744 | tf_op jit(solution)/shard_map/all_gather | solution.py:52
  464.5 9.7 fusion.82
  474.2 83.8 %all-gather.21.cloned.1.call-done = bf16[2048,1408]{1,0:T(8,128)(2,1)} async-done(((bf16[256,1408]{1,0:T(8,128)(2,1)}), bf16[2048,1408]{1,0:T(8,128)(2,1)}) %all-gather.21.cloned.1.call-update) | async-done | bytes 5767184 | tf_op jit(solution)/shard_map/all_gather | solution.py:69
  558.0 9.7 fusion.81
  567.7 20.2 %all-gather.27.cloned.1.call-done = bf16[3,256,2048]{2,1,0:T(8,128)(2,1)} async-done(((bf16[3,64,2048]{2,1,0:T(8,128)(2,1)}), bf16[3,256,2048]{2,1,0:T(8,128)(2,1)}) %all-gather.27.cloned.1.call-update) | async-done | bytes 3145744 | tf_op jit(solution)/shard_map/all_gather | solution.py:52
  587.9 93.2 %all-gather.25.cloned.1.call-done = bf16[1408,2048]{1,0:T(8,128)(2,1)} async-done(((bf16[1408,256]{1,0:T(8,128)(2,1)}), bf16[1408,2048]{1,0:T(8,128)(2,1)}) %all-gather.25.cloned.1.call-update) | async-done | bytes 5767184 | tf_op jit(solution)/shard_map/all_gather | solution.py:75
  681.1 13.0 multiply_convert_fusion
  694.1 7.5 fusion.84
  701.6 9.8 convolution_add_fusion
  711.5 10.0 fusion.83
  721.6 48.0 %reduce-scatter.16.cloned.1.call-done = f32[3,64,2048]{2,1,0:T(8,128)} async-done(((f32[3,256,2048]{2,1,0:T(8,128)}), f32[3,64,2048]{2,1,0:T(8,128)}) %reduce-scatter.16.cloned.1.call-update) | async-done | bytes 1572880 | tf_op jit(solution)/shard_map/reduce_scatter | solution.py:56
  772.4 57.5 %reduce-scatter.14.cloned.1.call-done = f32[3,64,2048]{2,1,0:T(8,128)} async-done(((f32[3,256,2048]{2,1,0:T(8,128)}), f32[3,64,2048]{2,1,0:T(8,128)}) %reduce-scatter.14.cloned.1.call-update) | async-done | bytes 1572880 | tf_op jit(solution)/shard_map/reduce_scatter | solution.py:56
  835.3 28.6 %all-gather.29.cloned.1.call-done = bf16[3,256,2048]{2,1,0:T(8,128)(2,1)} async-done(((bf16[3,64,2048]{2,1,0:T(8,128)(2,1)}), bf16[3,256,2048]{2,1,0:T(8,128)(2,1)}) %all-gather.29.cloned.1.call-update) | async-done | bytes 3145744 | tf_op jit(solution)/shard_map/all_gather | solution.py:52
  869.1 122.0 %while.25 = (s32[]{:T(128)}, f32[3,256,8,64]{1,3,2,0:T(8,128)}, bf16[3,2048,128]{2,1,0:T(8,128)(2,1)}, bf16[3,2048,128]{1,2,0:T(8,128)(2,1)S(1)}, s32[3,2048]{1,...) while((s32[]{:T(128)}, f32[3,256,8,64]{1,3,2,0:T(8,128)}, ...), condition=%wide.region_13.14_spmd, body=%wide.region_11.13_spmd.sunk | while | flops 2749759488 | bytes 143482128 | solution.py:275
  884.7 9.5 fusion.152
  894.2 8.4 fusion.153
  925.4 9.5 fusion.152
  934.9 8.4 fusion.153
  966.0 9.5 fusion.152
  975.6 8.4 fusion.153
  991.1 42.5 %copy.98 = bf16[3,2048,128]{0,2,1:T(8,128)(2,1)} copy(bf16[3,2048,128]{2,1,0:T(8,128)(2,1)} %get-tuple-element.110) | data formatting | bytes 3145728
  1033.6 78.5 %reshape.337 = bf16[2048,384]{1,0:T(8,128)(2,1)} reshape(bf16[2048,128,3]{2,1,0:T(8,128)(2,1)} %bitcast.66) | data formatting | bytes 3145728
  1112.2 8.2 fusion.38
  1126.7 14.1 convolution_convert_fusion
  1145.2 32.1 %reduce-scatter.28.cloned.1.call-done = bf16[256,384]{1,0:T(8,128)(2,1)} async-done(((bf16[2048,384]{1,0:T(8,128)(2,1)}), bf16[256,384]{1,0:T(8,128)(2,1)}) %reduce-scatter.28.cloned.1.call-update) | async-done | bytes 196624
  1177.3 18.7 %reshape.338 = bf16[256,128,3]{2,1,0:T(8,128)(2,1)} reshape(bf16[256,384]{1,0:T(8,128)(2,1)} %reduce-scatter.28.cloned.1.call-done) | data formatting | bytes 393216
  1229.0 61.9 %reduce-scatter.26.cloned.1.call-done = bf16[256,1408]{0,1:T(8,128)(2,1)} async-done(((bf16[2048,1408]{0,1:T(8,128)(2,1)}), bf16[256,1408]{0,1:T(8,128)(2,1)}) %reduce-scatter.26.cloned.1.call-update) | async-done | bytes 720912 | tf_op jit(solution)/shard_map/reduce_scatter | solution.py:95
  1293.2 68.5 %reduce-scatter.22.cloned.1.call-done = bf16[256,512]{1,0:T(8,128)(2,1)} async-done(((bf16[2048,512]{1,0:T(8,128)(2,1)}), bf16[256,512]{1,0:T(8,128)(2,1)}) %reduce-scatter.22.cloned.1.call-update) | async-done | bytes 262160 | tf_op jit(solution)/shard_map/reduce_scatter | solution.py:95
  1363.7 192.4 %reduce-scatter.24.cloned.1.call-done = bf16[256,2816]{1,0:T(8,128)(2,1)} async-done(((bf16[2048,2816]{1,0:T(8,128)(2,1)}), bf16[256,2816]{1,0:T(8,128)(2,1)}) %reduce-scatter.24.cloned.1.call-update) | async-done | bytes 1441808 | tf_op jit(solution)/shard_map/reduce_scatter | solution.py:95
  1559.2 71.3 %reduce-scatter.20.cloned.1.call-done = bf16[256,640]{1,0:T(8,128)(2,1)} async-done(((bf16[2048,640]{1,0:T(8,128)(2,1)}), bf16[256,640]{1,0:T(8,128)(2,1)}) %reduce-scatter.20.cloned.1.call-update) | async-done | bytes 327696 | tf_op jit(solution)/shard_map/reduce_scatter | solution.py:95
  1634.7 55.9 %reduce-scatter.18.cloned.1.call-done = f32[3,64,2048]{2,1,0:T(8,128)} async-done(((f32[3,256,2048]{2,1,0:T(8,128)}), f32[3,64,2048]{2,1,0:T(8,128)}) %reduce-scatter.18.cloned.1.call-update) | async-done | bytes 1572880 | tf_op jit(solution)/shard_map/reduce_scatter | solution.py:56
  1692.6 39.5 %all-reduce.4 = (f32[2048]{0:T(1024)S(1)}, f32[2048]{0:T(1024)S(1)}) all-reduce(f32[2048]{0:T(1024)S(1)} %get-tuple-element.221, f32[2048]{0:T(1024)S(1)} %copy-done.27), channel_id=7, replica_groups=mesh['fsdp'=8,'tp'=4] {'fsdp','tp'}, use_global_device_ids=true, to_apply=%region_18.19.clone | all-reduce | flops 4096 | bytes 32768
  (270 shorter events, 209.7 us)
Async XLA Ops:
  7.2 47.4 %copy-start.28 = (bf16[256,64]{0,1:T(8,128)(2,1)S(1)}, bf16[256,64]{0,1:T(8,128)(2,1)}, u32[]{:S(2)}) copy-start(bf16[256,64]{0,1:T(8,128)(2,1)} %param.21) | copy-start | bytes 98308
  7.2 77.6 %copy-start.29 = (bf16[256,64]{0,1:T(8,128)(2,1)S(1)}, bf16[256,64]{0,1:T(8,128)(2,1)}, u32[]{:S(2)}) copy-start(bf16[256,64]{0,1:T(8,128)(2,1)} %param.22) | copy-start | bytes 98308
  7.2 109.2 %copy-start.31 = (s32[3,8]{1,0:T(4,128)S(1)}, s32[3,8]{1,0:T(4,128)}, u32[]{:S(2)}) copy-start(s32[3,8]{1,0:T(4,128)} %param.29) | copy-start | bytes 292
  7.2 111.1 %all-gather.11.cloned.1.call-start = ((), (), s32[]{:S(2)}) async-start(), calls=%async_computation.9 | async-start | bytes 3932160 | tf_op jit(solution)/shard_map/all_gather | solution.py:52
  9.2 109.1 %copy-start.25 = (f32[3,64]{1,0:T(4,128)}, f32[3,64]{1,0:T(4,128)S(1)}, u32[]{:S(2)}) copy-start(f32[3,64]{1,0:T(4,128)S(1)} %get-tuple-element.299) | copy-start | bytes 2308
  51.5 66.9 %copy-start.22 = (f32[2048]{0:T(1024)}, f32[2048]{0:T(1024)S(1)}, u32[]{:S(2)}) copy-start(f32[2048]{0:T(1024)S(1)} %get-tuple-element.261) | copy-start | bytes 24580
  53.8 81.6 %all-gather.15.cloned.1.call-start = ((), (), s32[]{:S(2)}) async-start(), calls=%async_computation.11 | async-start | bytes 2359296 | tf_op jit(solution)/shard_map/all_gather | solution.py:61
  54.5 130.6 %all-gather.13.cloned.1.call-start = ((), (), s32[]{:S(2)}) async-start(), calls=%async_computation.10 | async-start | bytes 2359296 | tf_op jit(solution)/shard_map/all_gather | solution.py:165
  116.4 11.0 copy-start.10
  118.3 11.7 copy-start.17
  118.4 7.3 copy-start.3
  133.8 142.9 %all-gather.17.cloned.1.call-start = ((), (), s32[]{:S(2)}) async-start(), calls=%async_computation.12 | async-start | bytes 2359296 | tf_op jit(solution)/shard_map/all_gather | solution.py:75
  134.4 206.9 %reduce-scatter.12.cloned.1.call-start = ((), (), s32[]{:S(2)}) async-start(), calls=%async_computation.13 | async-start | bytes 7864320 | tf_op jit(solution)/shard_map/reduce_scatter | solution.py:56
  140.3 3.8 copy-start.13
  144.1 43.7 %copy-start.34 = (s32[3]{0:T(128)S(1)}, s32[3]{0:T(128)}, u32[]{:S(2)}) copy-start(s32[3]{0:T(128)} %param.28) | copy-start | bytes 40
  283.1 58.2 %copy-start.5 = (bf16[3,64,2048]{2,1,0:T(8,128)(2,1)S(1)}, bf16[3,64,2048]{2,1,0:T(8,128)(2,1)}, u32[]{:S(2)}) copy-start(bf16[3,64,2048]{2,1,0:T(8,128)(2,1)} %param.17) | copy-start | bytes 2359300
  283.1 61.0 %copy-start.24 = (f32[2048]{0:T(1024)S(1)}, f32[2048]{0:T(1024)}, u32[]{:S(2)}) copy-start(f32[2048]{0:T(1024)} %get-tuple-element.262) | copy-start | bytes 24580
  283.1 151.5 %all-gather.23.cloned.1.call-start = ((), (), s32[]{:S(2)}) async-start(), calls=%async_computation.16 | async-start | bytes 6488064 | tf_op jit(solution)/shard_map/all_gather | solution.py:70
  283.7 180.8 %all-gather.19.cloned.1.call-start = ((), (), s32[]{:S(2)}) async-start(), calls=%async_computation.14 | async-start | bytes 3932160 | tf_op jit(solution)/shard_map/all_gather | solution.py:52
  345.2 212.8 %all-gather.21.cloned.1.call-start = ((), (), s32[]{:S(2)}) async-start(), calls=%async_computation.15 | async-start | bytes 6488064 | tf_op jit(solution)/shard_map/all_gather | solution.py:69
  345.9 241.9 %all-gather.27.cloned.1.call-start = ((), (), s32[]{:S(2)}) async-start(), calls=%async_computation.19 | async-start | bytes 3932160 | tf_op jit(solution)/shard_map/all_gather | solution.py:52
  348.4 332.7 %all-gather.25.cloned.1.call-start = ((), (), s32[]{:S(2)}) async-start(), calls=%async_computation.17 | async-start | bytes 6488064 | tf_op jit(solution)/shard_map/all_gather | solution.py:75
  349.0 420.6 %reduce-scatter.16.cloned.1.call-start = ((), (), s32[]{:S(2)}) async-start(), calls=%async_computation.20 | async-start | bytes 7864320 | tf_op jit(solution)/shard_map/reduce_scatter | solution.py:56
  681.1 13.1 copy-start.32
  694.1 7.5 copy-start.35
  711.4 118.5 %reduce-scatter.14.cloned.1.call-start = ((), (), s32[]{:S(2)}) async-start(), calls=%async_computation.18 | async-start | bytes 7864320 | tf_op jit(solution)/shard_map/reduce_scatter | solution.py:56
  721.5 142.4 %all-gather.29.cloned.1.call-start = ((), (), s32[]{:S(2)}) async-start(), calls=%async_computation.21 | async-start | bytes 3932160 | tf_op jit(solution)/shard_map/all_gather | solution.py:52
  835.2 342.1 %reduce-scatter.28.cloned.1.call-start = ((), (), s32[]{:S(2)}) async-start(), calls=%async_computation.27 | async-start | bytes 1769472
  869.1 6.1 copy-start
  909.8 6.1 copy-start
  950.5 6.1 copy-start
  1033.6 78.6 %copy-start.33 = (bf16[3,256,2048]{2,1,0:T(8,128)(2,1)S(1)}, bf16[3,256,2048]{2,1,0:T(8,128)(2,1)}, u32[]{:S(2)}) copy-start(bf16[3,256,2048]{2,1,0:T(8,128)(2,1)} %all-gather.27.cloned.1.call-done) | copy-start | bytes 9437188
  1112.1 178.8 %reduce-scatter.26.cloned.1.call-start = ((), (), s32[]{:S(2)}) async-start(), calls=%async_computation.26 | async-start | bytes 6488064 | tf_op jit(solution)/shard_map/reduce_scatter | solution.py:95
  1120.4 6.3 copy-start.36
  1120.4 241.3 %reduce-scatter.22.cloned.1.call-start = ((), (), s32[]{:S(2)}) async-start(), calls=%async_computation.24 | async-start | bytes 2359296 | tf_op jit(solution)/shard_map/reduce_scatter | solution.py:95
  1126.6 429.5 %reduce-scatter.24.cloned.1.call-start = ((), (), s32[]{:S(2)}) async-start(), calls=%async_computation.25 | async-start | bytes 12976128 | tf_op jit(solution)/shard_map/reduce_scatter | solution.py:95
  1140.8 489.7 %reduce-scatter.20.cloned.1.call-start = ((), (), s32[]{:S(2)}) async-start(), calls=%async_computation.23 | async-start | bytes 2949120 | tf_op jit(solution)/shard_map/reduce_scatter | solution.py:95
  1208.4 6.6 copy-start.19
  1208.4 6.7 copy-start.18
  1209.0 6.2 copy-start.4
  1220.5 3.8 copy-start.12
  1220.5 470.2 %reduce-scatter.18.cloned.1.call-start = ((), (), s32[]{:S(2)}) async-start(), calls=%async_computation.22 | async-start | bytes 7864320 | tf_op jit(solution)/shard_map/reduce_scatter | solution.py:56
  1363.7 326.9 %copy-start.6 = (bf16[3,64,2048]{2,1,0:T(8,128)(2,1)S(1)}, bf16[3,64,2048]{2,1,0:T(8,128)(2,1)}, u32[]{:S(2)}) copy-start(bf16[3,64,2048]{2,1,0:T(8,128)(2,1)} %param.17) | copy-start | bytes 2359300
  1363.7 326.9 %copy-start.23 = (f32[2048]{0:T(1024)S(1)}, f32[2048]{0:T(1024)}, u32[]{:S(2)}) copy-start(f32[2048]{0:T(1024)} %copy-done.22) | copy-start | bytes 24580
  1363.7 326.9 %copy-start.26 = (f32[3,64]{1,0:T(4,128)S(1)}, f32[3,64]{1,0:T(4,128)}, u32[]{:S(2)}) copy-start(f32[3,64]{1,0:T(4,128)} %copy-done.25) | copy-start | bytes 2308
  1559.2 133.4 %copy-start.27 = (f32[2048]{0:T(1024)S(1)}, f32[2048]{0:T(1024)}, u32[]{:S(2)}) copy-start(f32[2048]{0:T(1024)} %get-tuple-element.219) | copy-start | bytes 24580
  1559.2 174.0 %copy-start.30 = (f32[3,64]{1,0:T(4,128)S(1)}, f32[3,64]{1,0:T(4,128)}, u32[]{:S(2)}) copy-start(f32[3,64]{1,0:T(4,128)} %get-tuple-element.298) | copy-start | bytes 2308
  1690.6 42.6 %copy-start.8 = (f32[3,64,2048]{2,1,0:T(8,128)S(1)}, f32[3,64,2048]{2,1,0:T(8,128)}, u32[]{:S(2)}) copy-start(f32[3,64,2048]{2,1,0:T(8,128)} %reduce-scatter.18.cloned.1.call-done) | copy-start | bytes 4718596
  (14 other events, 22.4 us)
Sparse Core Ops, SparseCore 0:
  53.9 28.8 all-gather.10
  84.9 50.1 all-gather.14
  137.7 47.3 all-gather.12
  187.0 48.5 all-gather.16
  283.2 57.9 reduce-scatter.11
  343.3 91.2 all-gather.22
  436.8 27.6 all-gather.18
  466.7 91.2 all-gather.20
  560.1 27.6 all-gather.26
  589.8 91.2 all-gather.24
  711.5 57.9 reduce-scatter.15
  771.9 57.9 reduce-scatter.13
  835.4 28.4 all-gather.28
  1112.2 65.0 reduce-scatter.27
  1180.9 109.9 reduce-scatter.25
  1294.3 67.3 reduce-scatter.21
  1365.1 190.9 reduce-scatter.23
  1559.5 70.9 reduce-scatter.19
  1633.0 57.5 reduce-scatter.17
where the time goes:
time: 1760 us; the launch traced here: 1740 us
  waiting for transfers between devices  1030 us (59%)
  matrix products  242 us (14%)
  local copies, waits for them, and re-layouts  206 us (12%)
  blocking collectives  142 us (8%)
  other arithmetic  107 us (6%)
    reduce_scatter x4, waiting for transfers between devices, reduce_grads(): lax.psum_scatter(term_rows(jnp.int32(0), row_count * lax.axis_size('fsdp'...  394 us
    reduce_scatter x4, waiting for transfers between devices, collect_rows(): return lax.psum_scatter(values, 'tp', scatter_dimension=1, tiled=True)  219 us
    unnamed x89, local copies, waits for them, and re-layouts  163 us
    all_gather x2, waiting for transfers between devices, out_cols(): return lax.all_gather(weight, 'fsdp', axis=1, tiled=True)  93.2 us
    all_gather x1, waiting for transfers between devices, mlp_rows(): lax.all_gather(w_up, 'fsdp', axis=0, tiled=True)  85.6 us
    all_gather x1, waiting for transfers between devices, mlp_rows(): lax.all_gather(w_gate, 'fsdp', axis=0, tiled=True)  83.8 us
    unnamed x2, blocking collectives  80 us
    all_gather x4, waiting for transfers between devices, spread_rows(): return lax.all_gather(values, 'tp', axis=1, tiled=True)  78.6 us
  transfers between devices with their start and end apart: 19, of which 16 were waited for; matrix products, arithmetic and copies ran while one was open for 14% of the time, Pallas kernels for 0%

commit v1 on v0

v1 whole, which is shorter than its diff:
```python
import functools

import jax
import jax.numpy as jnp
from jax import lax
from jax.experimental import pallas as pl
from jax.experimental.pallas import tpu as pltpu
from jax.sharding import PartitionSpec as P

HD = 64
EPS = 1e-05
THETA = 10000.0
NEG = -1000000000.0
F32 = jnp.float32
BF16 = jnp.bfloat16


def inverse_rms(values):
    return lax.rsqrt(jnp.mean(values * values, axis=-1, keepdims=True) + EPS)


def norm_back(upstream, values, gain_vec, inv_rms):
    weighted = upstream * gain_vec
    inner_mean = jnp.mean(weighted * values, axis=-1, keepdims=True)
    return (
        inv_rms * weighted - values * (inv_rms * inv_rms * inv_rms) * inner_mean,
        jnp.sum(upstream * values * inv_rms, axis=(0, 1)),
    )


def dot(a, b, ca, cb):
    return lax.dot_general(a, b, (((ca,), (cb,)), ((), ())), preferred_element_type=F32)


def swap_b(v):
    n = lax.axis_size("fsdp")
    return lax.ppermute(v, "fsdp", [(i, i ^ 1) for i in range(n)])


def a_groups():
    n = lax.axis_size("fsdp")
    return [[b + 2 * a for a in range(n // 2)] for b in range(2)]


def gather_halves(shard):
    own = lax.all_gather(shard, "fsdp", axis=0, tiled=True, axis_index_groups=a_groups())
    return own, swap_b(own)


def scatter_halves(send, keep_fn):
    other = swap_b(send.astype(BF16))
    total = (keep_fn() + other.astype(F32)).astype(BF16)
    return lax.psum_scatter(
        total, "fsdp", scatter_dimension=0, tiled=True, axis_index_groups=a_groups()
    )


def swap_tp(v, bit):
    n = lax.axis_size("tp")
    return lax.ppermute(v, "tp", [(i, i ^ bit) for i in range(n)])


def spread_rows(v):
    pair = jnp.concatenate([v, swap_tp(v, 2)], axis=1)
    return jnp.concatenate([pair, swap_tp(pair, 1)], axis=1)


def collect_rows(halves):
    out = []
    for part in halves:
        half = part.shape[1] // 2
        got = swap_tp(part[:, half:].astype(BF16), 1)
        part = part[:, :half] + got.astype(F32)
        half = half // 2
        got = swap_tp(part[:, half:].astype(BF16), 2)
        out.append(part[:, :half] + got.astype(F32))
    return jnp.concatenate(out, axis=-1)


def row_offsets(idx, rows, y, c):
    ec = idx // (2 * rows)
    ey = (idx // rows) % 2
    return ((ey ^ y) * 2 + (ec ^ c)) * rows + idx % rows


def fill_bias(bias_ref, tab_ref, s, n_blocks, block, rows):
    y = tab_ref[s, n_blocks + 2]
    c = tab_ref[s, n_blocks + 3]
    prefix = tab_ref[s, n_blocks + 1]
    koff = row_offsets(lax.broadcasted_iota(jnp.int32, (block, block), 0), rows, y, c)
    qoff = row_offsets(lax.broadcasted_iota(jnp.int32, (block, block), 1), rows, y, c)
    qpos = qoff + tab_ref[s, n_blocks] * block
    for kb in range(n_blocks):
        kpos = koff + tab_ref[s, kb] * block
        ok = (kpos <= qpos) | (kpos < prefix)
        bias_ref[kb * block : (kb + 1) * block, :] = jnp.where(ok, 0.0, NEG)


def fwd_kernel(n_blocks, block, rows, step, tab_ref, q_ref, kv_ref, vt_ref, o_ref, lse_ref, bias_ref):
    s = pl.program_id(0)

    @pl.when(pl.program_id(1) == 0)
    def _():
        fill_bias(bias_ref, tab_ref, s, n_blocks, block, rows)

    q = q_ref[...]
    qz = jnp.concatenate([q, jnp.zeros_like(q)], axis=0)
    seq = n_blocks * block
    m = jnp.full((1, block), -jnp.inf, F32)
    l = jnp.zeros((1, block), F32)
    acc = jnp.zeros((HD, block), F32)
    for k0 in range(0, seq, step):
        sc = dot(kv_ref[k0 : k0 + step, :], qz, 1, 0) + bias_ref[k0 : k0 + step, :]
        m_new = jnp.maximum(m, jnp.max(sc, axis=0, keepdims=True))
        alpha = jnp.exp(m - m_new)
        p = jnp.exp(sc - m_new)
        l = l * alpha + jnp.sum(p, axis=0, keepdims=True)
        acc = acc * alpha + dot(vt_ref[:, k0 : k0 + step], p.astype(BF16), 1, 0)
        m = m_new
    o_ref[...] = (acc / l).astype(BF16)
    lse_ref[0] = m + jnp.log(l)


def bwd_kernel(
    n_blocks, block, rows, step, tab_ref, q_ref, kv_ref, kt_ref, go_ref, o_ref, lse_ref,
    dq_ref, dkv_ref, bias_ref, dkv_acc,
):
    s = pl.program_id(0)
    h = pl.program_id(1)

    @pl.when(h == 0)
    def _():
        fill_bias(bias_ref, tab_ref, s, n_blocks, block, rows)
        dkv_acc[...] = jnp.zeros_like(dkv_acc)

    q = q_ref[...]
    go = go_ref[...]
    zero = jnp.zeros_like(q)
    qz = jnp.concatenate([q, zero], axis=0)
    gz = jnp.concatenate([zero, go], axis=0)
    lse = lse_ref[0]
    delta = jnp.sum(go.astype(F32) * o_ref[...].astype(F32), axis=0, keepdims=True)
    seq = n_blocks * block
    dq = jnp.zeros((HD, block), F32)
    for k0 in range(0, seq, step):
        ks = slice(k0, k0 + step)
        kv = kv_ref[ks, :]
        p = jnp.exp(dot(kv, qz, 1, 0) + bias_ref[ks, :] - lse)
        ds = (p * (dot(kv, gz, 1, 0) - delta)).astype(BF16)
        dkv_acc[HD:, ks] += dot(go, p.astype(BF16), 1, 1)
        dkv_acc[:HD, ks] += dot(q, ds, 1, 1)
        dq = dq + dot(kt_ref[:, ks], ds, 1, 0)
    dq_ref[...] = dq

    @pl.when(h == pl.num_programs(1) - 1)
    def _():
        dkv_ref[...] = dkv_acc[...].T.astype(BF16)


def attention_specs(n_blocks, block):
    seq = n_blocks * block
    q_spec = pl.BlockSpec((HD, block), lambda s, h, t: (h, s))
    kv_spec = pl.BlockSpec((seq, 2 * HD), lambda s, h, t: (0, s))
    lse_spec = pl.BlockSpec((1, 1, block), lambda s, h, t: (h, 0, s))

    def half_spec(which):
        return pl.BlockSpec((HD, seq), lambda s, h, t: (2 * s + which, 0))

    return q_spec, kv_spec, lse_spec, half_spec


def attention_forward(tab, q_t, kv, kv_t, n_blocks, block, rows):
    heads, seqs, seq = q_t.shape[0] // HD, q_t.shape[1] // block, n_blocks * block
    q_spec, kv_spec, lse_spec, half_spec = attention_specs(n_blocks, block)
    return pl.pallas_call(
        functools.partial(fwd_kernel, n_blocks, block, rows, min(512, seq)),
        name="attn_fwd",
        out_shape=(
            jax.ShapeDtypeStruct(q_t.shape, BF16),
            jax.ShapeDtypeStruct((heads, 1, seqs * block), F32),
        ),
        grid_spec=pltpu.PrefetchScalarGridSpec(
            num_scalar_prefetch=1,
            grid=(seqs, heads),
            in_specs=[q_spec, kv_spec, half_spec(1)],
            out_specs=[q_spec, lse_spec],
            scratch_shapes=[pltpu.VMEM((seq, block), F32)],
        ),
        compiler_params=pltpu.CompilerParams(
            dimension_semantics=("arbitrary", "arbitrary"), vmem_limit_bytes=48 << 20
        ),
        cost_estimate=pl.CostEstimate(
            flops=16 * heads * seqs * block * seq * HD,
            bytes_accessed=4 * seqs * seq * 2 * HD,
            transcendentals=heads * seqs * block * seq,
        ),
    )(tab, q_t, kv, kv_t)


def attention_backward(tab, q_t, kv, kv_t, go_t, o_t, lse, n_blocks, block, rows):
    heads, seqs, seq = q_t.shape[0] // HD, q_t.shape[1] // block, n_blocks * block
    q_spec, kv_spec, lse_spec, half_spec = attention_specs(n_blocks, block)
    return pl.pallas_call(
        functools.partial(bwd_kernel, n_blocks, block, rows, min(512, seq)),
        name="attn_bwd",
        out_shape=(
            jax.ShapeDtypeStruct(q_t.shape, F32),
            jax.ShapeDtypeStruct((seq, seqs * 2 * HD), BF16),
        ),
        grid_spec=pltpu.PrefetchScalarGridSpec(
            num_scalar_prefetch=1,
            grid=(seqs, heads),
            in_specs=[q_spec, kv_spec, half_spec(0), q_spec, q_spec, lse_spec],
            out_specs=[q_spec, kv_spec],
            scratch_shapes=[pltpu.VMEM((seq, block), F32), pltpu.VMEM((2 * HD, seq), F32)],
        ),
        compiler_params=pltpu.CompilerParams(
            dimension_semantics=("arbitrary", "arbitrary"), vmem_limit_bytes=48 << 20
        ),
        cost_estimate=pl.CostEstimate(
            flops=40 * heads * seqs * block * seq * HD,
            bytes_accessed=8 * seqs * seq * 2 * HD,
            transcendentals=heads * seqs * block * seq,
        ),
    )(tab, q_t, kv, kv_t, go_t, o_t, lse)


def on_device(
    hidden_in, cotangent, gain_attn, w_query, w_key, w_value, w_out, gain_mlp, w_gate, w_up,
    w_down, prefix, block_order,
):
    seqs, rows, width = hidden_in.shape
    n_tp = lax.axis_size("tp")
    n_fsdp = lax.axis_size("fsdp")
    if n_tp != 4 or n_fsdp % 2 or w_key.shape[1] != HD:
        raise ValueError("unsupported mesh")
    n_a = n_fsdp // 2
    block = rows * n_tp
    tokens = seqs * block
    half = width // 2
    chunk = width // n_fsdp
    q_width = w_query.shape[1]
    ff = w_gate.shape[1]
    fsdp_index = lax.axis_index("fsdp")
    a_idx, b_idx = fsdp_index // 2, fsdp_index % 2
    tp_index = lax.axis_index("tp")
    y_idx, c_idx = tp_index // 2, tp_index % 2
    first = b_idx == 0

    def to_rel(v):
        v = v.reshape(v.shape[:-1] + (n_a, 2, chunk))
        even, odd = v[..., 0, :], v[..., 1, :]
        lo = jnp.where(first, even, odd).reshape(v.shape[:-3] + (half,))
        hi = jnp.where(first, odd, even).reshape(v.shape[:-3] + (half,))
        return jnp.concatenate([lo, hi], axis=-1)

    def from_rel(v):
        lo = v[..., :half].reshape(v.shape[:-1] + (n_a, chunk))
        hi = v[..., half:].reshape(v.shape[:-1] + (n_a, chunk))
        even, odd = jnp.where(first, lo, hi), jnp.where(first, hi, lo)
        return jnp.stack([even, odd], axis=-2).reshape(v.shape[:-1] + (width,))

    gains = lax.all_gather(
        jnp.stack([gain_attn, gain_mlp]), ("fsdp", "tp"), axis=1, tiled=True
    )
    gains = to_rel(gains)
    gain_first, gain_second = gains[0], gains[1]
    own_block = jnp.sum(
        jnp.where(jnp.arange(n_fsdp)[None, :] == fsdp_index, block_order, 0), axis=1
    )
    by_b = block_order.reshape(seqs, n_a, 2)
    even, odd = by_b[:, :, 0], by_b[:, :, 1]
    key_blocks = jnp.concatenate(
        [jnp.where(first, even, odd), jnp.where(first, odd, even)], axis=1
    )
    tab = jnp.concatenate(
        [
            key_blocks,
            own_block[:, None],
            prefix[:, None],
            jnp.broadcast_to(y_idx, (seqs, 1)),
            jnp.broadcast_to(c_idx, (seqs, 1)),
        ],
        axis=1,
    ).astype(jnp.int32)
    lane = jnp.arange(block, dtype=jnp.int32)
    offs = row_offsets(lane, rows, y_idx, c_idx)
    pos = (own_block[:, None] * block + offs[None, :]).reshape(tokens)
    frequency = THETA ** (-(jnp.arange(HD // 2, dtype=F32) * 2.0 / HD))
    angles = frequency[:, None] * pos.astype(F32)[None, :]
    cos_t = jnp.cos(angles)[None]
    sin_t = jnp.sin(angles)[None]

    def rotate_t(v):
        v = v.reshape(-1, HD, tokens)
        u1, u2 = v[:, : HD // 2], v[:, HD // 2 :]
        return jnp.concatenate(
            [u1 * cos_t - u2 * sin_t, u2 * cos_t + u1 * sin_t], axis=1
        ).reshape(-1, tokens)

    def rotate_back_t(v):
        v = v.reshape(-1, HD, tokens)
        u1, u2 = v[:, : HD // 2], v[:, HD // 2 :]
        return jnp.concatenate(
            [u1 * cos_t + u2 * sin_t, u2 * cos_t - u1 * sin_t], axis=1
        ).reshape(-1, tokens)

    qkv_a, qkv_b = gather_halves(jnp.concatenate([w_query, w_key, w_value], axis=1))
    out_a, out_b = gather_halves(w_out.T)
    gu_a, gu_b = gather_halves(jnp.concatenate([w_gate, w_up], axis=1))
    down_a, down_b = gather_halves(w_down.T)

    x_rel = to_rel(hidden_in)
    x_all = spread_rows(x_rel).astype(F32)
    h_first = (x_all * inverse_rms(x_all) * gain_first).astype(BF16).reshape(tokens, width)
    gm = spread_rows(to_rel(cotangent).astype(BF16)).reshape(tokens, width)
    qkv_t = dot(qkv_a, h_first[:, :half], 0, 1) + dot(qkv_b, h_first[:, half:], 0, 1)
    q_t = (rotate_t(qkv_t[:q_width]).astype(BF16) * (HD**-0.5)).astype(BF16)
    kv_t = jnp.concatenate(
        [rotate_t(qkv_t[q_width : q_width + HD]), qkv_t[q_width + HD :]], axis=0
    ).astype(BF16)
    kv_own = (
        kv_t.reshape(2 * HD, seqs, block).transpose(2, 1, 0).reshape(block, seqs * 2 * HD)
    )
    kv = jnp.concatenate(gather_halves(kv_own), axis=0)
    kv_all_t = kv.T
    o_t, lse = attention_forward(tab, q_t, kv, kv_all_t, n_fsdp, block, rows)

    x_own = x_rel.astype(F32)
    rms_first = inverse_rms(x_own)

    def rows3(v):
        return v.reshape(seqs, block, half)

    middle = x_own + collect_rows(
        [rows3(dot(o_t, out_a, 0, 1)), rows3(dot(o_t, out_b, 0, 1))]
    )
    rms_second = inverse_rms(middle)
    h_second = spread_rows((middle * rms_second * gain_second).astype(BF16)).reshape(
        tokens, width
    )

    gu = dot(h_second[:, :half], gu_a, 1, 0) + dot(h_second[:, half:], gu_b, 1, 0)
    gate, up = gu[:, :ff], gu[:, ff:]
    sig = jax.nn.sigmoid(gate)
    hidden = (gate * sig * up).astype(BF16)
    g_hidden = dot(gm[:, :half], down_a, 1, 0) + dot(gm[:, half:], down_b, 1, 0)
    g_cat = jnp.concatenate(
        [
            (g_hidden * up * sig * (1.0 + gate * (1.0 - sig))).astype(BF16),
            (g_hidden * gate * sig).astype(BF16),
        ],
        axis=1,
    )
    g_h2 = collect_rows([rows3(dot(g_cat, gu_a, 1, 1)), rows3(dot(g_cat, gu_b, 1, 1))])
    down_g = scatter_halves(
        dot(gm[:, half:], hidden, 0, 0), lambda: dot(gm[:, :half], hidden, 0, 0)
    )
    gu_g = scatter_halves(
        dot(h_second[:, half:], g_cat, 0, 0), lambda: dot(h_second[:, :half], g_cat, 0, 0)
    )
    layer_out = middle + collect_rows(
        [rows3(dot(hidden, down_a, 1, 1)), rows3(dot(hidden, down_b, 1, 1))]
    )
    g_mid_norm, gain_second_sum = norm_back(g_h2, middle, gain_second, rms_second)
    g_mid = to_rel(cotangent) + g_mid_norm

    ga = spread_rows(g_mid.astype(BF16)).reshape(tokens, width)
    go_t = (dot(out_a, ga[:, :half], 0, 1) + dot(out_b, ga[:, half:], 0, 1)).astype(BF16)
    dq_t, dkv = attention_backward(
        tab, q_t, kv, kv_all_t, go_t, o_t, lse, n_fsdp, block, rows
    )
    out_g = scatter_halves(dot(ga[:, half:], o_t, 0, 1), lambda: dot(ga[:, :half], o_t, 0, 1))
    seq_half = n_a * block
    dkv_own = scatter_halves(
        dkv[seq_half:], lambda: dkv[:seq_half].astype(F32)
    ).astype(F32)
    dkv_t = dkv_own.reshape(block, seqs, 2 * HD).transpose(2, 1, 0).reshape(2 * HD, tokens)
    gq_t = rotate_back_t(dq_t * (HD**-0.5)).astype(BF16)
    gk_t = rotate_back_t(dkv_t[:HD]).astype(BF16)
    g_qkv_t = jnp.concatenate([gq_t, gk_t, dkv_t[HD:].astype(BF16)], axis=0)
    qkv_g = scatter_halves(
        dot(h_first[:, half:], g_qkv_t, 0, 1), lambda: dot(h_first[:, :half], g_qkv_t, 0, 1)
    )
    g_h1 = collect_rows([rows3(dot(g_qkv_t, qkv_a, 0, 1)), rows3(dot(g_qkv_t, qkv_b, 0, 1))])
    g_in_norm, gain_first_sum = norm_back(g_h1, x_own, gain_first, rms_first)
    g_in = g_mid + g_in_norm
    gain_sums = lax.psum_scatter(
        from_rel(jnp.stack([gain_first_sum, gain_second_sum])),
        ("fsdp", "tp"),
        scatter_dimension=1,
        tiled=True,
    )
    qkv_g = qkv_g.astype(F32)
    gu_g = gu_g.astype(F32)
    return (
        from_rel(layer_out),
        from_rel(g_in),
        gain_sums[0],
        qkv_g[:, :q_width],
        qkv_g[:, q_width : q_width + HD],
        qkv_g[:, q_width + HD :],
        out_g.astype(F32).T,
        gain_sums[1],
        gu_g[:, :ff],
        gu_g[:, ff:],
        down_g.astype(F32).T,
    )


def solution(mesh):
    rows = P(None, ("fsdp", "tp"), None)
    gain = P(("fsdp", "tp"))
    col = P("fsdp", "tp")
    row = P("tp", "fsdp")
    return jax.shard_map(
        on_device,
        mesh=mesh,
        in_specs=(rows, rows, gain, col, col, col, row, gain, col, col, row, P(), P()),
        out_specs=(rows, rows, gain, col, col, col, row, gain, col, col, row),
        check_vma=False,
    )
```

time: 1760 us -> 1070 us (0.61)
  waiting for transfers between devices: 1030 us -> 631 us
  local copies, waits for them, and re-layouts: 206 us -> 61 us
  matrix products: 242 us -> 116 us
  Pallas kernels: 0 us -> 87.8 us
  other arithmetic: 107 us -> 40.4 us
  blocking collectives: 142 us -> 80.3 us
  starting transfers between devices: 0.95 us -> 25.5 us
    reduce_scatter x8 -> x5, waiting for transfers between devices: 613 us -> 129 us  [scatter_halves(): lax.psum_scatter(total, 'fsdp', scatter_dimension=0, tiled=True, axis_ind...]
    ppermute x0 -> x34, waiting for transfers between devices: none -> 479 us  [the longest x10 393 us: swap_b(): return lax.ppermute(v, 'fsdp', [(i, i ^ 1) for i in range(n)])]
    all_gather x10 -> x4, waiting for transfers between devices: 382 us -> 22.9 us  [gather_halves(): lax.all_gather(shard, 'fsdp', axis=0, tiled=True, axis_index_groups=a_gro...]
    unnamed x89 -> x123, local copies, waits for them, and re-layouts: 163 us -> 17.2 us
    dot_general x39 -> x24, matrix products: 242 us -> 116 us  [dot(): lax.dot_general(a, b, (((ca,), (cb,)), ((), ())), preferred_element_type=...]
    pallas_call x0 -> x2, Pallas kernels: none -> 87.8 us  [the longest x1 44.6 us: attention_backward(): pl.pallas_call(functools.partial(bwd_kernel, n_blocks, block, rows, min(5...]
    unnamed x2 -> x0, blocking collectives: 80 us -> none
    unnamed x20 -> x11, waiting for transfers between devices: 35.3 us -> 0.84 us
  transfers between devices with their start and end apart: 19 -> 44, of which waited for: 16 -> 20; matrix products, arithmetic and copies ran while one was open for 14% -> 15% of each run, Pallas kernels for 0% -> 4%
where the time goes in v1:
time: 1070 us; the launch traced here: 1060 us
  waiting for transfers between devices  631 us (59%)
  matrix products  116 us (11%)
  Pallas kernels  87.8 us (8%)
  blocking collectives  80.3 us (8%)
  local copies, waits for them, and re-layouts  61 us (6%)
  other arithmetic  40.4 us (4%)
  starting transfers between devices  25.5 us (2%)
  between operations  16.2 us (2%)
    ppermute x10, waiting for transfers between devices, swap_b(): return lax.ppermute(v, 'fsdp', [(i, i ^ 1) for i in range(n)])  393 us
    reduce_scatter x5, waiting for transfers between devices, scatter_halves(): lax.psum_scatter(total, 'fsdp', scatter_dimension=0, tiled=True, axis_ind...  129 us
    dot_general x24, matrix products, dot(): lax.dot_general(a, b, (((ca,), (cb,)), ((), ())), preferred_element_type=...  116 us
    ppermute x24, waiting for transfers between devices, swap_tp(): return lax.ppermute(v, 'tp', [(i, i ^ bit) for i in range(n)])  85.8 us
    all_gather x1, blocking collectives, on_device(): lax.all_gather(jnp.stack([gain_attn, gain_mlp]), ('fsdp', 'tp'), axis=1,...  45.6 us
    pallas_call x1, Pallas kernels, attention_backward(): pl.pallas_call(functools.partial(bwd_kernel, n_blocks, block, rows, min(5...  44.6 us
    pallas_call x1, Pallas kernels, attention_forward(): pl.pallas_call(functools.partial(fwd_kernel, n_blocks, block, rows, min(5...  43.2 us
    all_gather x1, blocking collectives, gather_halves(): lax.all_gather(shard, 'fsdp', axis=0, tiled=True, axis_index_groups=a_gro...  34.7 us
  transfers between devices with their start and end apart: 44, of which 20 were waited for; matrix products, arithmetic and copies ran while one was open for 15% of the time, Pallas kernels for 4%

profile of v1, /device:TPU:8, one launch (start us, length us, event | category | flops | bytes accessed | tf_op | source)
XLA Modules:
  0.0 1058.0 jit_solution(7145386997447961479)
XLA Ops:
  17.5 45.6 %all-gather = f32[32,64,2]{1,2,0:T(2,128)S(1)} all-gather(f32[1,64,2]{1,2,0:T(2,128)S(1)} %maximum_bitcast_fusion.2), channel_id=1, replica_groups=mesh['fsdp'=8,'tp'=4] {'fsdp','tp'}, dimensions={0}, use_global_device_ids=true | all-gather | bytes 16896 | tf_op jit(solution)/shard_map/all_gather | solution.py:263
  65.4 2.7 collective-permute-done.1
  70.2 26.3 %collective-permute-done.2 = bf16[1024,640]{1,0:T(8,128)(2,1)} collective-permute-done((bf16[1024,640]{1,0:T(8,128)(2,1)}, bf16[1024,640]{1,0:T(8,128)(2,1)}, u32[]{:S(2)}, u32[]{:S(2)}) %collective-permute-start.2) | collective-permute-done | bytes 1310752 | tf_op jit(solution)/shard_map/ppermute | solution.py:37
  96.5 2.6 fusion.25
  101.2 34.7 %all_gather.20 = bf16[1024,384]{0,1:T(8,128)(2,1)S(1)} all-gather(bf16[256,384]{0,1:T(8,128)(2,1)S(1)} %bitcast.143), channel_id=1, replica_groups={{0,8,16,24},{4,12,20,28},{1,9,17,25},{5,13,21,29},{2,10,18,26},{6,14,22..., dimensions={0}, use_global_device_ids=true | all-gather | bytes 983040 | tf_op jit(solution)/shard_map/all_gather | solution.py:46
  137.5 3.4 reshape.523
  144.2 12.3 %collective-permute-done.3 = bf16[1024,384]{0,1:T(8,128)(2,1)} collective-permute-done((bf16[1024,384]{0,1:T(8,128)(2,1)S(1)}, bf16[1024,384]{0,1:T(8,128)(2,1)}, u32[]{:S(2)}, u32[]{:S(2)}) %collective-permute-start.3) | collective-permute-done | bytes 786464 | tf_op jit(solution)/shard_map/ppermute | solution.py:37
  160.7 43.2 %attn_fwd.1 = (bf16[512,768]{1,0:T(8,128)(2,1)S(1)}, f32[8,1,768]{2,1,0:T(1,128)S(1)}) custom-call(s32[3,12]{1,0:T(4,128)S(1)} %concatenate.94.tab_ref, bf16[512,768]{1,0:T(8,128)(2,1)S(1)} %bitcast.105, bf16[2048,384]{1,0:T(8,128)(2,1)S(1)} %copy-done.1, bf16[384,2048]{1,0:T(8,128)(2,1)S(1)} %bitcast.103), custom_call_target="tpu_custom_call" | custom-call | flops 12884901888 | bytes 3145728 | tf_op jit(solution)/shard_map/attn_fwd/pallas_call | solution.py:175
  215.0 2.4 copy_select_fusion
  228.2 22.9 %all-gather.12.cloned.1.call-done = bf16[1024,1408]{0,1:T(8,128)(2,1)} async-done(((bf16[256,1408]{0,1:T(8,128)(2,1)}), bf16[1024,1408]{0,1:T(8,128)(2,1)}) %all-gather.12.cloned.1.call-update) | async-done | bytes 2883600 | tf_op jit(solution)/shard_map/all_gather | solution.py:46
  261.3 14.7 %collective-permute-done.9 = bf16[3,64,2048]{2,1,0:T(8,128)(2,1)S(1)} collective-permute-done((bf16[3,64,2048]{2,1,0:T(8,128)(2,1)S(1)}, bf16[3,64,2048]{2,1,0:T(8,128)(2,1)S(1)}, u32[]{:S(2)}, u32[]{:S(2)}) %collective-permute-start.9) | collective-permute-done | bytes 786464 | tf_op jit(solution)/shard_map/ppermute | solution.py:60
  277.7 124.8 %collective-permute-done.14 = bf16[1024,1408]{0,1:T(8,128)(2,1)S(1)} collective-permute-done((bf16[1024,1408]{0,1:T(8,128)(2,1)}, bf16[1024,1408]{0,1:T(8,128)(2,1)S(1)}, u32[]{:S(2)}, u32[]{:S(2)}) %collective-permute-start.14) | collective-permute-done | bytes 2883616 | tf_op jit(solution)/shard_map/ppermute | solution.py:37
  402.5 4.5 fusion.15
  407.4 10.9 %fusion.20 = f32[768,2816]{1,0:T(8,128)} fusion(bf16[1024,2816]{1,0:T(8,128)(2,1)} %collective-permute-done.11, bf16[768,2048]{1,0:T(8,128)(2,1)S(1)} %bitcast.114), kind=kOutput, calls=%fused_computation.80 | convolution fusion | flops 4429185024 | bytes 15990784 | tf_op jit(solution)/shard_map/dot_general | solution.py:32
  418.3 9.4 convolution_add_fusion
  427.7 7.3 multiply_convert_fusion.1
  435.0 2.6 fusion.81
  437.9 6.7 fusion.69
  445.2 7.8 fusion.68
  453.2 5.1 fusion.82
  464.7 15.0 %collective-permute-done.20 = bf16[3,64,1024]{2,1,0:T(8,128)(2,1)S(1)} collective-permute-done((bf16[3,64,1024]{2,1,0:T(8,128)(2,1)S(1)}, bf16[3,64,1024]{2,1,0:T(8,128)(2,1)S(1)}, u32[]{:S(2)}, u32[]{:S(2)}) %collective-permute-start.20) | collective-permute-done | bytes 393248 | tf_op jit(solution)/shard_map/ppermute | solution.py:60
  479.9 8.3 collective-permute-done.22
  488.9 6.8 collective-permute-done.16
  498.3 18.3 %collective-permute-done.23 = bf16[3,64,2048]{2,1,0:T(8,128)(2,1)S(1)} collective-permute-done((bf16[3,64,2048]{2,1,0:T(8,128)(2,1)S(1)}, bf16[3,64,2048]{2,1,0:T(8,128)(2,1)S(1)}, u32[]{:S(2)}, u32[]{:S(2)}) %collective-permute-start.23) | collective-permute-done | bytes 786464 | tf_op jit(solution)/shard_map/ppermute | solution.py:60
  516.9 3.4 collective-permute-done.24
  520.6 3.1 fusion.10
  524.8 44.6 %attn_bwd.1 = (f32[512,768]{1,0:T(8,128)S(1)}, bf16[2048,384]{1,0:T(8,128)(2,1)S(1)}) custom-call(s32[3,12]{1,0:T(4,128)S(1)} %concatenate.94.tab_ref, bf16[512,768]{1,0:T(8,128)(2,1)S(1)} %bitcast.106, bf16[2048,384]{1,0:T(8,128)(2,1)} %copy.83.kv_ref, bf16[384,2048]{1,0:T(8,128)(2,1)} %bitcast.104, bf16[512,768]{1,0:T(8,128)(2,1)S(1)} %fusion.36.go_ref, ...), custom_call_target="tpu_custom_call" | custom-call | flops 32212254720 | bytes 6291456 | tf_op jit(solution)/shard_map/attn_bwd/pallas_call | solution.py:203
  570.7 18.4 %collective-permute-done.25 = bf16[1024,384]{1,0:T(8,128)(2,1)S(1)} collective-permute-done((bf16[1024,384]{1,0:T(8,128)(2,1)S(1)}, bf16[1024,384]{1,0:T(8,128)(2,1)S(1)}, u32[]{:S(2)}, u32[]{:S(2)}) %collective-permute-start.25) | collective-permute-done | bytes 786464 | tf_op jit(solution)/shard_map/ppermute | solution.py:37
  590.5 6.4 convolution_convert_fusion.1
  601.4 11.3 %reduce-scatter.9.cloned.1.call-done = bf16[256,384]{1,0:T(8,128)(2,1)} async-done(((bf16[1024,384]{1,0:T(8,128)(2,1)}), bf16[256,384]{1,0:T(8,128)(2,1)}) %reduce-scatter.9.cloned.1.call-update) | async-done | bytes 196624 | tf_op jit(solution)/shard_map/reduce_scatter | solution.py:53
  614.6 2.7 fusion.71
  620.0 2.9 fusion.70
  626.0 57.4 %collective-permute-done.31 = bf16[1024,512]{1,0:T(8,128)(2,1)} collective-permute-done((bf16[1024,512]{1,0:T(8,128)(2,1)}, bf16[1024,512]{1,0:T(8,128)(2,1)}, u32[]{:S(2)}, u32[]{:S(2)}) %collective-permute-start.31) | collective-permute-done | bytes 1048608 | tf_op jit(solution)/shard_map/ppermute | solution.py:37
  683.4 3.2 add_convert_fusion.3
  692.3 8.5 collective-permute-done.27
  700.9 5.8 collective-permute-done.29
  709.0 7.2 add_convert_fusion.1
  716.3 10.1 convolution_convert_fusion
  729.9 153.9 %collective-permute-done.30 = bf16[1024,640]{1,0:T(8,128)(2,1)S(1)} collective-permute-done((bf16[1024,640]{1,0:T(8,128)(2,1)S(1)}, bf16[1024,640]{1,0:T(8,128)(2,1)S(1)}, u32[]{:S(2)}, u32[]{:S(2)}) %collective-permute-start.30) | collective-permute-done | bytes 1310752 | tf_op jit(solution)/shard_map/ppermute | solution.py:37
  883.8 2.5 add_convert_fusion.2
  886.7 11.6 %add_convert_fusion = bf16[1024,2816]{1,0:T(8,128)(2,1)} fusion(bf16[1024,2816]{1,0:T(8,128)(2,1)} %collective-permute-done.32, bf16[768,2048]{1,0:T(8,128)(2,1)} %bitcast.117, bf16[768,1408]{1,0:T(8,128)(2,1)} %copy-done.49, bf16[768,1408]{1,0:T(8,128)(2,1)} %copy-done.48), kind=kOutput, calls=%fused_computation | convolution fusion | flops 4446486528 | bytes 17432576 | tf_op jit(solution)/shard_map/dot_general | solution.py:32
  898.3 2.7 slice_select_fusion.3
  906.4 2.5 copy.84
  908.9 3.6 reshape.522
  918.9 2.4 reshape.534
  926.1 16.4 %reduce-scatter.11.cloned.1.call-done = bf16[256,640]{1,0:T(8,128)(2,1)} async-done(((bf16[1024,640]{1,0:T(8,128)(2,1)}), bf16[256,640]{1,0:T(8,128)(2,1)}) %reduce-scatter.11.cloned.1.call-update) | async-done | bytes 327696 | tf_op jit(solution)/shard_map/reduce_scatter | solution.py:53
  946.8 100.8 %reduce-scatter.15.cloned.1.call-done = bf16[256,2816]{1,0:T(8,128)(2,1)} async-done(((bf16[1024,2816]{1,0:T(8,128)(2,1)}), bf16[256,2816]{1,0:T(8,128)(2,1)}) %reduce-scatter.15.cloned.1.call-update) | async-done | bytes 1441808 | tf_op jit(solution)/shard_map/reduce_scatter | solution.py:53
  1047.6 3.1 fusion.74
  (341 shorter events, 119.1 us)
Async XLA Ops:
  7.2 58.1 %all-gather.6.cloned.1.call-start = ((), (), s32[]{:S(2)}) async-start(), calls=%async_computation.6 | async-start | bytes 1638400 | tf_op jit(solution)/shard_map/all_gather | solution.py:46
  10.9 130.6 %all-gather.8.cloned.1.call-start = ((), (), s32[]{:S(2)}) async-start(), calls=%async_computation.7 | async-start | bytes 1310720 | tf_op jit(solution)/shard_map/all_gather | solution.py:46
  11.7 202.2 %all-gather.10.cloned.1.call-start = ((), (), s32[]{:S(2)}) async-start(), calls=%async_computation.8 | async-start | bytes 7208960 | tf_op jit(solution)/shard_map/all_gather | solution.py:46
  12.9 238.1 %all-gather.12.cloned.1.call-start = ((), (), s32[]{:S(2)}) async-start(), calls=%async_computation.9 | async-start | bytes 3604480 | tf_op jit(solution)/shard_map/all_gather | solution.py:46
  15.8 47.4 %collective-permute-start = (bf16[3,64,2048]{2,1,0:T(8,128)(2,1)S(1)}, bf16[3,64,2048]{2,1,0:T(8,128)(2,1)S(1)}, u32[]{:S(2)}, u32[]{:S(2)}) collective-permute-start(bf16[3,64,2048]{2,1,0:T(8,128)(2,1)S(1)} %constant_dynamic-update-slice_fusion), channel_id=1, source_target_pairs={{0,2},{1,3},{2,0},{3,1},{4,6},{5,7},{6,4},{7,5},{8,10},{9,11},{10,... | collective-permute-start | bytes 2359304 | tf_op jit(solution)/shard_map/ppermute | solution.py:60
  17.4 595.3 %reduce-scatter.9.cloned.1.call-start = ((), (), s32[]{:S(2)}) async-start(), calls=%async_computation.10 | async-start | bytes 983040 | tf_op jit(solution)/shard_map/reduce_scatter | solution.py:53
  64.4 3.6 collective-permute-start.1
  65.2 75.8 %copy-start.37 = (f32[768]{0:T(1024)}, f32[768]{0:T(1024)S(1)}, u32[]{:S(2)}) copy-start(f32[768]{0:T(1024)S(1)} %convert_element_type.189) | copy-start | bytes 9220
  65.2 75.8 %copy-start.40 = (f32[32]{0:T(128)}, f32[32]{0:T(128)S(1)}, u32[]{:S(2)}) copy-start(f32[32]{0:T(128)S(1)} %negate_power_fusion) | copy-start | bytes 388
  65.3 31.2 %collective-permute-start.2 = (bf16[1024,640]{1,0:T(8,128)(2,1)}, bf16[1024,640]{1,0:T(8,128)(2,1)}, u32[]{:S(2)}, u32[]{:S(2)}) collective-permute-start(bf16[1024,640]{1,0:T(8,128)(2,1)} %all-gather.6.cloned.1.call-done), channel_id=1, source_target_pairs={{0,4},{4,0},{8,12},{12,8},{16,20},{20,16},{24,28},{28,24},{1,5},{5... | collective-permute-start | bytes 3932168 | tf_op jit(solution)/shard_map/ppermute | solution.py:37
  135.9 20.5 %collective-permute-start.3 = (bf16[1024,384]{0,1:T(8,128)(2,1)S(1)}, bf16[1024,384]{0,1:T(8,128)(2,1)}, u32[]{:S(2)}, u32[]{:S(2)}) collective-permute-start(bf16[1024,384]{0,1:T(8,128)(2,1)S(1)} %all_gather.20), channel_id=1, source_target_pairs={{0,4},{4,0},{8,12},{12,8},{16,20},{20,16},{24,28},{28,24},{1,5},{5... | collective-permute-start | bytes 2359304 | tf_op jit(solution)/shard_map/ppermute | solution.py:37
  141.5 65.4 %collective-permute-start.6 = (bf16[1024,512]{0,1:T(8,128)(2,1)}, bf16[1024,512]{0,1:T(8,128)(2,1)}, u32[]{:S(2)}, u32[]{:S(2)}) collective-permute-start(bf16[1024,512]{0,1:T(8,128)(2,1)} %all-gather.8.cloned.1.call-done), channel_id=1, source_target_pairs={{0,4},{4,0},{8,12},{12,8},{16,20},{20,16},{24,28},{28,24},{1,5},{5... | collective-permute-start | bytes 3145736 | tf_op jit(solution)/shard_map/ppermute | solution.py:37
  206.0 13.4 %collective-permute-start.4 = (bf16[3,128,1024]{2,1,0:T(8,128)(2,1)}, bf16[3,128,1024]{2,1,0:T(8,128)(2,1)}, u32[]{:S(2)}, u32[]{:S(2)}) collective-permute-start(bf16[3,128,1024]{2,1,0:T(8,128)(2,1)} %slice.562), channel_id=1, source_target_pairs={{0,1},{1,0},{2,3},{3,2},{4,5},{5,4},{6,7},{7,6},{8,9},{9,8},{10,11... | collective-permute-start | bytes 2359304 | tf_op jit(solution)/shard_map/ppermute | solution.py:60
  211.7 10.6 %collective-permute-start.7 = (bf16[3,128,1024]{2,1,0:T(8,128)(2,1)}, bf16[3,128,1024]{2,1,0:T(8,128)(2,1)}, u32[]{:S(2)}, u32[]{:S(2)}) collective-permute-start(bf16[3,128,1024]{2,1,0:T(8,128)(2,1)} %slice.561), channel_id=1, source_target_pairs={{0,1},{1,0},{2,3},{3,2},{4,5},{5,4},{6,7},{7,6},{8,9},{9,8},{10,11... | collective-permute-start | bytes 2359304 | tf_op jit(solution)/shard_map/ppermute | solution.py:60
  213.8 193.6 %collective-permute-start.11 = (bf16[1024,2816]{1,0:T(8,128)(2,1)}, bf16[1024,2816]{1,0:T(8,128)(2,1)}, u32[]{:S(2)}, u32[]{:S(2)}) collective-permute-start(bf16[1024,2816]{1,0:T(8,128)(2,1)} %all-gather.10.cloned.1.call-done), channel_id=1, source_target_pairs={{0,4},{4,0},{8,12},{12,8},{16,20},{20,16},{24,28},{28,24},{1,5},{5... | collective-permute-start | bytes 17301512 | tf_op jit(solution)/shard_map/ppermute | solution.py:37
  222.3 30.3 %collective-permute-start.5 = (bf16[3,64,1024]{2,1,0:T(8,128)(2,1)}, bf16[3,64,1024]{2,1,0:T(8,128)(2,1)}, u32[]{:S(2)}, u32[]{:S(2)}) collective-permute-start(bf16[3,64,1024]{2,1,0:T(8,128)(2,1)} %slice.570), channel_id=1, source_target_pairs={{0,2},{1,3},{2,0},{3,1},{4,6},{5,7},{6,4},{7,5},{8,10},{9,11},{10,... | collective-permute-start | bytes 1179656 | tf_op jit(solution)/shard_map/ppermute | solution.py:60
  224.7 29.3 %collective-permute-start.8 = (bf16[3,64,1024]{2,1,0:T(8,128)(2,1)}, bf16[3,64,1024]{2,1,0:T(8,128)(2,1)}, u32[]{:S(2)}, u32[]{:S(2)}) collective-permute-start(bf16[3,64,1024]{2,1,0:T(8,128)(2,1)} %slice.569), channel_id=1, source_target_pairs={{0,2},{1,3},{2,0},{3,1},{4,6},{5,7},{6,4},{7,5},{8,10},{9,11},{10,... | collective-permute-start | bytes 1179656 | tf_op jit(solution)/shard_map/ppermute | solution.py:60
  228.1 31.8 %collective-permute-start.17 = (bf16[3,64,2048]{2,1,0:T(8,128)(2,1)S(1)}, bf16[3,64,2048]{2,1,0:T(8,128)(2,1)}, u32[]{:S(2)}, u32[]{:S(2)}) collective-permute-start(bf16[3,64,2048]{2,1,0:T(8,128)(2,1)S(1)} %convert_element_type.200), channel_id=1, source_target_pairs={{0,2},{1,3},{2,0},{3,1},{4,6},{5,7},{6,4},{7,5},{8,10},{9,11},{10,... | collective-permute-start | bytes 2359304 | tf_op jit(solution)/shard_map/ppermute | solution.py:60
  251.0 151.5 %collective-permute-start.14 = (bf16[1024,1408]{0,1:T(8,128)(2,1)}, bf16[1024,1408]{0,1:T(8,128)(2,1)S(1)}, u32[]{:S(2)}, u32[]{:S(2)}) collective-permute-start(bf16[1024,1408]{0,1:T(8,128)(2,1)} %all-gather.12.cloned.1.call-done), channel_id=1, source_target_pairs={{0,4},{4,0},{8,12},{12,8},{16,20},{20,16},{24,28},{28,24},{1,5},{5... | collective-permute-start | bytes 8650760 | tf_op jit(solution)/shard_map/ppermute | solution.py:37
  256.0 19.9 %collective-permute-start.9 = (bf16[3,64,2048]{2,1,0:T(8,128)(2,1)S(1)}, bf16[3,64,2048]{2,1,0:T(8,128)(2,1)S(1)}, u32[]{:S(2)}, u32[]{:S(2)}) collective-permute-start(bf16[3,64,2048]{2,1,0:T(8,128)(2,1)S(1)} %multiply_convert_fusion.3), channel_id=1, source_target_pairs={{0,2},{1,3},{2,0},{3,1},{4,6},{5,7},{6,4},{7,5},{8,10},{9,11},{10,... | collective-permute-start | bytes 2359304 | tf_op jit(solution)/shard_map/ppermute | solution.py:60
  261.2 15.0 %collective-permute-start.18 = (bf16[3,128,2048]{2,1,0:T(8,128)(2,1)S(1)}, bf16[3,128,2048]{2,1,0:T(8,128)(2,1)S(1)}, u32[]{:S(2)}, u32[]{:S(2)}) collective-permute-start(bf16[3,128,2048]{2,1,0:T(8,128)(2,1)S(1)} %pad_maximum_fusion.7), channel_id=1, source_target_pairs={{0,1},{1,0},{2,3},{3,2},{4,5},{5,4},{6,7},{7,6},{8,9},{9,8},{10,11... | collective-permute-start | bytes 4718600 | tf_op jit(solution)/shard_map/ppermute | solution.py:60
  276.1 130.9 %collective-permute-start.10 = (bf16[3,128,2048]{2,1,0:T(8,128)(2,1)S(1)}, bf16[3,128,2048]{2,1,0:T(8,128)(2,1)S(1)}, u32[]{:S(2)}, u32[]{:S(2)}) collective-permute-start(bf16[3,128,2048]{2,1,0:T(8,128)(2,1)S(1)} %pad_maximum_fusion.5), channel_id=1, source_target_pairs={{0,1},{1,0},{2,3},{3,2},{4,5},{5,4},{6,7},{7,6},{8,9},{9,8},{10,11... | collective-permute-start | bytes 4718600 | tf_op jit(solution)/shard_map/ppermute | solution.py:60
  277.7 150.1 %copy-start.17 = (bf16[3,256,2048]{2,1,0:T(8,128)(2,1)}, bf16[3,256,2048]{2,1,0:T(8,128)(2,1)S(1)}, u32[]{:S(2)}) copy-start(bf16[3,256,2048]{2,1,0:T(8,128)(2,1)S(1)} %pad_maximum_fusion.2) | copy-start | bytes 9437188
  437.8 21.2 %collective-permute-start.12 = (bf16[3,128,1024]{2,1,0:T(8,128)(2,1)S(1)}, bf16[3,128,1024]{2,1,0:T(8,128)(2,1)S(1)}, u32[]{:S(2)}, u32[]{:S(2)}) collective-permute-start(bf16[3,128,1024]{2,1,0:T(8,128)(2,1)S(1)} %slice.560), channel_id=1, source_target_pairs={{0,1},{1,0},{2,3},{3,2},{4,5},{5,4},{6,7},{7,6},{8,9},{9,8},{10,11... | collective-permute-start | bytes 2359304 | tf_op jit(solution)/shard_map/ppermute | solution.py:60
  444.7 14.7 %collective-permute-start.19 = (bf16[3,128,1024]{2,1,0:T(8,128)(2,1)S(1)}, bf16[3,128,1024]{2,1,0:T(8,128)(2,1)S(1)}, u32[]{:S(2)}, u32[]{:S(2)}) collective-permute-start(bf16[3,128,1024]{2,1,0:T(8,128)(2,1)S(1)} %slice.558), channel_id=1, source_target_pairs={{0,1},{1,0},{2,3},{3,2},{4,5},{5,4},{6,7},{7,6},{8,9},{9,8},{10,11... | collective-permute-start | bytes 2359304 | tf_op jit(solution)/shard_map/ppermute | solution.py:60
  453.1 8.7 collective-permute-start.21
  458.4 3.9 collective-permute-start.15
  459.3 29.5 %collective-permute-start.13 = (bf16[3,64,1024]{2,1,0:T(8,128)(2,1)S(1)}, bf16[3,64,1024]{2,1,0:T(8,128)(2,1)S(1)}, u32[]{:S(2)}, u32[]{:S(2)}) collective-permute-start(bf16[3,64,1024]{2,1,0:T(8,128)(2,1)S(1)} %slice.568), channel_id=1, source_target_pairs={{0,2},{1,3},{2,0},{3,1},{4,6},{5,7},{6,4},{7,5},{8,10},{9,11},{10,... | collective-permute-start | bytes 1179656 | tf_op jit(solution)/shard_map/ppermute | solution.py:60
  459.8 20.0 %collective-permute-start.20 = (bf16[3,64,1024]{2,1,0:T(8,128)(2,1)S(1)}, bf16[3,64,1024]{2,1,0:T(8,128)(2,1)S(1)}, u32[]{:S(2)}, u32[]{:S(2)}) collective-permute-start(bf16[3,64,1024]{2,1,0:T(8,128)(2,1)S(1)} %slice.566), channel_id=1, source_target_pairs={{0,2},{1,3},{2,0},{3,1},{4,6},{5,7},{6,4},{7,5},{8,10},{9,11},{10,... | collective-permute-start | bytes 1179656 | tf_op jit(solution)/shard_map/ppermute | solution.py:60
  462.2 26.0 %collective-permute-start.22 = (bf16[3,64,1024]{2,1,0:T(8,128)(2,1)S(1)}, bf16[3,64,1024]{2,1,0:T(8,128)(2,1)S(1)}, u32[]{:S(2)}, u32[]{:S(2)}) collective-permute-start(bf16[3,64,1024]{2,1,0:T(8,128)(2,1)S(1)} %slice.565), channel_id=1, source_target_pairs={{0,2},{1,3},{2,0},{3,1},{4,6},{5,7},{6,4},{7,5},{8,10},{9,11},{10,... | collective-permute-start | bytes 1179656 | tf_op jit(solution)/shard_map/ppermute | solution.py:60
  462.7 33.0 %collective-permute-start.16 = (bf16[3,64,1024]{2,1,0:T(8,128)(2,1)S(1)}, bf16[3,64,1024]{2,1,0:T(8,128)(2,1)S(1)}, u32[]{:S(2)}, u32[]{:S(2)}) collective-permute-start(bf16[3,64,1024]{2,1,0:T(8,128)(2,1)S(1)} %slice.567), channel_id=1, source_target_pairs={{0,2},{1,3},{2,0},{3,1},{4,6},{5,7},{6,4},{7,5},{8,10},{9,11},{10,... | collective-permute-start | bytes 1179656 | tf_op jit(solution)/shard_map/ppermute | solution.py:60
  498.0 18.6 %collective-permute-start.23 = (bf16[3,64,2048]{2,1,0:T(8,128)(2,1)S(1)}, bf16[3,64,2048]{2,1,0:T(8,128)(2,1)S(1)}, u32[]{:S(2)}, u32[]{:S(2)}) collective-permute-start(bf16[3,64,2048]{2,1,0:T(8,128)(2,1)S(1)} %get-tuple-element.58), channel_id=1, source_target_pairs={{0,2},{1,3},{2,0},{3,1},{4,6},{5,7},{6,4},{7,5},{8,10},{9,11},{10,... | collective-permute-start | bytes 2359304 | tf_op jit(solution)/shard_map/ppermute | solution.py:60
  516.8 3.5 collective-permute-start.24
  569.5 19.7 %collective-permute-start.25 = (bf16[1024,384]{1,0:T(8,128)(2,1)S(1)}, bf16[1024,384]{1,0:T(8,128)(2,1)S(1)}, u32[]{:S(2)}, u32[]{:S(2)}) collective-permute-start(bf16[1024,384]{1,0:T(8,128)(2,1)S(1)} %slice.327), channel_id=1, source_target_pairs={{0,4},{4,0},{8,12},{12,8},{16,20},{20,16},{24,28},{28,24},{1,5},{5... | collective-permute-start | bytes 2359304 | tf_op jit(solution)/shard_map/ppermute | solution.py:37
  590.2 322.3 %reduce-scatter.13.cloned.1.call-start = ((), (), s32[]{:S(2)}) async-start(), calls=%async_computation.12 | async-start | bytes 1310720 | tf_op jit(solution)/shard_map/reduce_scatter | solution.py:53
  596.9 112.1 %collective-permute-start.33 = (bf16[1024,1408]{1,0:T(8,128)(2,1)}, bf16[1024,1408]{1,0:T(8,128)(2,1)}, u32[]{:S(2)}, u32[]{:S(2)}) collective-permute-start(bf16[1024,1408]{1,0:T(8,128)(2,1)} %convolution_convert_fusion.1), channel_id=1, source_target_pairs={{0,4},{4,0},{8,12},{12,8},{16,20},{20,16},{24,28},{28,24},{1,5},{5... | collective-permute-start | bytes 8650760 | tf_op jit(solution)/shard_map/ppermute | solution.py:37
  600.1 83.3 %collective-permute-start.31 = (bf16[1024,512]{1,0:T(8,128)(2,1)}, bf16[1024,512]{1,0:T(8,128)(2,1)}, u32[]{:S(2)}, u32[]{:S(2)}) collective-permute-start(bf16[1024,512]{1,0:T(8,128)(2,1)} %convolution_convert_fusion.3), channel_id=1, source_target_pairs={{0,4},{4,0},{8,12},{12,8},{16,20},{20,16},{24,28},{28,24},{1,5},{5... | collective-permute-start | bytes 3145736 | tf_op jit(solution)/shard_map/ppermute | solution.py:37
  620.0 63.4 %copy-start.20 = (bf16[3,256,2048]{2,1,0:T(8,128)(2,1)S(1)}, bf16[3,256,2048]{2,1,0:T(8,128)(2,1)}, u32[]{:S(2)}) copy-start(bf16[3,256,2048]{2,1,0:T(8,128)(2,1)} %copy-done.18) | copy-start | bytes 9437188
  620.0 66.7 %collective-permute-start.26 = (bf16[3,128,1024]{2,1,0:T(8,128)(2,1)}, bf16[3,128,1024]{2,1,0:T(8,128)(2,1)}, u32[]{:S(2)}, u32[]{:S(2)}) collective-permute-start(bf16[3,128,1024]{2,1,0:T(8,128)(2,1)} %slice.556), channel_id=1, source_target_pairs={{0,1},{1,0},{2,3},{3,2},{4,5},{5,4},{6,7},{7,6},{8,9},{9,8},{10,11... | collective-permute-start | bytes 2359304 | tf_op jit(solution)/shard_map/ppermute | solution.py:60
  625.6 63.8 %collective-permute-start.28 = (bf16[3,128,1024]{2,1,0:T(8,128)(2,1)}, bf16[3,128,1024]{2,1,0:T(8,128)(2,1)}, u32[]{:S(2)}, u32[]{:S(2)}) collective-permute-start(bf16[3,128,1024]{2,1,0:T(8,128)(2,1)} %slice.555), channel_id=1, source_target_pairs={{0,1},{1,0},{2,3},{3,2},{4,5},{5,4},{6,7},{7,6},{8,9},{9,8},{10,11... | collective-permute-start | bytes 2359304 | tf_op jit(solution)/shard_map/ppermute | solution.py:60
  686.6 234.6 %reduce-scatter.19.cloned.1.call-start = ((), (), s32[]{:S(2)}) async-start(), calls=%async_computation.15 | async-start | bytes 1081344
  688.8 12.1 %collective-permute-start.27 = (bf16[3,64,1024]{2,1,0:T(8,128)(2,1)S(1)}, bf16[3,64,1024]{2,1,0:T(8,128)(2,1)S(1)}, u32[]{:S(2)}, u32[]{:S(2)}) collective-permute-start(bf16[3,64,1024]{2,1,0:T(8,128)(2,1)S(1)} %slice.564), channel_id=1, source_target_pairs={{0,2},{1,3},{2,0},{3,1},{4,6},{5,7},{6,4},{7,5},{8,10},{9,11},{10,... | collective-permute-start | bytes 1179656 | tf_op jit(solution)/shard_map/ppermute | solution.py:60
  690.8 15.9 %collective-permute-start.29 = (bf16[3,64,1024]{2,1,0:T(8,128)(2,1)S(1)}, bf16[3,64,1024]{2,1,0:T(8,128)(2,1)S(1)}, u32[]{:S(2)}, u32[]{:S(2)}) collective-permute-start(bf16[3,64,1024]{2,1,0:T(8,128)(2,1)S(1)} %slice.563), channel_id=1, source_target_pairs={{0,2},{1,3},{2,0},{3,1},{4,6},{5,7},{6,4},{7,5},{8,10},{9,11},{10,... | collective-permute-start | bytes 1179656 | tf_op jit(solution)/shard_map/ppermute | solution.py:60
  708.7 214.6 %reduce-scatter.17.cloned.1.call-start = ((), (), s32[]{:S(2)}) async-start(), calls=%async_computation.14 | async-start | bytes 3604480 | tf_op jit(solution)/shard_map/reduce_scatter | solution.py:53
  716.2 226.3 %reduce-scatter.11.cloned.1.call-start = ((), (), s32[]{:S(2)}) async-start(), calls=%async_computation.11 | async-start | bytes 1638400 | tf_op jit(solution)/shard_map/reduce_scatter | solution.py:53
  726.4 160.3 %collective-permute-start.32 = (bf16[1024,2816]{1,0:T(8,128)(2,1)}, bf16[1024,2816]{1,0:T(8,128)(2,1)}, u32[]{:S(2)}, u32[]{:S(2)}) collective-permute-start(bf16[1024,2816]{1,0:T(8,128)(2,1)} %convolution_convert_fusion), channel_id=1, source_target_pairs={{0,4},{4,0},{8,12},{12,8},{16,20},{20,16},{24,28},{28,24},{1,5},{5... | collective-permute-start | bytes 17301512 | tf_op jit(solution)/shard_map/ppermute | solution.py:37
  729.0 154.8 %collective-permute-start.30 = (bf16[1024,640]{1,0:T(8,128)(2,1)S(1)}, bf16[1024,640]{1,0:T(8,128)(2,1)S(1)}, u32[]{:S(2)}, u32[]{:S(2)}) collective-permute-start(bf16[1024,640]{1,0:T(8,128)(2,1)S(1)} %convolution_convert_fusion.2), channel_id=1, source_target_pairs={{0,4},{4,0},{8,12},{12,8},{16,20},{20,16},{24,28},{28,24},{1,5},{5... | collective-permute-start | bytes 3932168 | tf_op jit(solution)/shard_map/ppermute | solution.py:37
  886.4 161.3 %reduce-scatter.15.cloned.1.call-start = ((), (), s32[]{:S(2)}) async-start(), calls=%async_computation.13 | async-start | bytes 7208960 | tf_op jit(solution)/shard_map/reduce_scatter | solution.py:53
  (50 other events, 582.8 us)
Sparse Core Ops, SparseCore 0:
  11.0 33.2 all-gather.5
  45.8 30.5 all-gather.7
  78.6 113.5 all-gather.9
  193.6 57.3 all-gather.11
  590.4 22.2 reduce-scatter.8
  686.8 25.8 reduce-scatter.12
  715.4 121.2 reduce-scatter.18
  839.0 70.6 reduce-scatter.16
  912.5 29.9 reduce-scatter.10
  944.7 102.8 reduce-scatter.14

commit v2 on v1

--- a/solution.py
+++ b/solution.py
@@ -75,6 +75,281 @@
         got = swap_tp(part[:, half:].astype(BF16), 2)
         out.append(part[:, :half] + got.astype(F32))
     return jnp.concatenate(out, axis=-1)
+
+
+MESH_ID = pl.DeviceIdType.MESH
+HBM_SPEC = pl.BlockSpec(memory_space=pl.ANY)
+VMEM_SPEC = pl.BlockSpec(memory_space=pltpu.VMEM)
+
+
+def remote(src, dst, send, recv, fsdp, tp):
+    return pltpu.make_async_remote_copy(
+        src_ref=src,
+        dst_ref=dst,
+        send_sem=send,
+        recv_sem=recv,
+        device_id=(fsdp, tp),
+        device_id_type=MESH_ID,
+    )
+
+
+def greet(peers):
+    barrier = pltpu.get_barrier_semaphore()
+    for fsdp, tp in peers:
+        pl.semaphore_signal(barrier, inc=1, device_id=(fsdp, tp), device_id_type=MESH_ID)
+    pl.semaphore_wait(barrier, len(peers))
+
+
+def coords(n_a):
+    fsdp, tp = lax.axis_index("fsdp"), lax.axis_index("tp")
+    return fsdp // 2, fsdp % 2, tp
+
+
+class FsdpGather:
+    def __init__(self, n_a, own, out, sems):
+        self.n_a, self.own, self.out = n_a, own, out
+        self.z_send, self.z_recv, self.x_send, self.x_recv, self.local = sems
+
+    def z_copy(self, d):
+        a, b, tp = coords(self.n_a)
+        to = lax.rem(a + d, self.n_a)
+        return remote(
+            self.own, self.out.at[0, a], self.z_send.at[d], self.z_recv.at[d], to * 2 + b, tp
+        )
+
+    def x_copy(self, d):
+        a, b, tp = coords(self.n_a)
+        at = lax.rem(a + self.n_a - d, self.n_a)
+        src = self.own if d == 0 else self.out.at[0, at]
+        return remote(
+            src, self.out.at[1, at], self.x_send.at[d], self.x_recv.at[d], a * 2 + 1 - b, tp
+        )
+
+    def start(self):
+        a, _, _ = coords(self.n_a)
+        self.x_copy(0).start()
+        for d in range(1, self.n_a):
+            self.z_copy(d).start()
+        pltpu.make_async_copy(self.own, self.out.at[0, a], self.local).start()
+
+    def forward(self):
+        for d in range(1, self.n_a):
+            self.z_copy(d).wait_recv()
+            self.x_copy(d).start()
+
+    def finish(self):
+        a, _, _ = coords(self.n_a)
+        for d in range(1, self.n_a):
+            self.z_copy(d).wait_send()
+        for d in range(self.n_a):
+            self.x_copy(d).wait()
+        pltpu.make_async_copy(self.own, self.out.at[0, a], self.local).wait()
+
+
+def gather_sems(n_a):
+    dma = pltpu.SemaphoreType.DMA
+    return [dma((n_a,)), dma((n_a,)), dma((n_a,)), dma((n_a,)), dma(())]
+
+
+def fsdp_peers(n_a):
+    a, b, tp = coords(n_a)
+    peers = [(a * 2 + 1 - b, tp)]
+    return peers + [(lax.rem(a + d, n_a) * 2 + b, tp) for d in range(1, n_a)]
+
+
+def prologue_kernel(
+    n_a, w_ref, x_ref, g_ref, wall_ref, xall_ref, gall_ref,
+    s0, s1, s2, s3, s4, tp_send, tp_recv, tp_local, g_send, g_recv,
+):
+    a, b, tp = coords(n_a)
+    fsdp = a * 2 + b
+    n_dev = n_a * 8
+    me = fsdp * 4 + tp
+    barrier = pltpu.get_barrier_semaphore()
+
+    def peer(k):
+        p = lax.rem(me + k, n_dev)
+        return p // 4, p % 4
+
+    @pl.loop(1, n_dev)
+    def _(k):
+        pl.semaphore_signal(barrier, inc=1, device_id=peer(k), device_id_type=MESH_ID)
+
+    pl.semaphore_wait(barrier, n_dev - 1)
+
+    def gain_copy(k):
+        f, t = peer(k)
+        return remote(g_ref, gall_ref.at[me], g_send.at[k], g_recv.at[k], f, t)
+
+    gather = FsdpGather(n_a, w_ref, wall_ref, (s0, s1, s2, s3, s4))
+    y_tp = lax.rem(tp + 2, 4)
+    c_tp = tp + 1 - 2 * (tp % 2)
+    to_y = remote(x_ref, xall_ref.at[:, 1], tp_send.at[0], tp_recv.at[0], fsdp, y_tp)
+    to_c = remote(x_ref, xall_ref.at[:, 2], tp_send.at[1], tp_recv.at[1], fsdp, c_tp)
+    fwd = remote(
+        xall_ref.at[:, 1], xall_ref.at[:, 3], tp_send.at[2], tp_recv.at[2], fsdp, c_tp
+    )
+    mine = pltpu.make_async_copy(x_ref, xall_ref.at[:, 0], tp_local)
+
+    @pl.loop(1, n_dev)
+    def _(k):
+        gain_copy(k).start()
+
+    gather.start()
+    to_y.start()
+    to_c.start()
+    mine.start()
+    gall_ref[me] = g_ref[...]
+    to_y.wait_recv()
+    fwd.start()
+    gather.forward()
+
+    @pl.loop(1, n_dev)
+    def _(k):
+        gain_copy(k).wait()
+
+    to_y.wait_send()
+    to_c.wait()
+    fwd.wait()
+    mine.wait()
+    gather.finish()
+
+
+def prologue(w, x, gains):
+    n_a = lax.axis_size("fsdp") // 2
+    n_dev = n_a * 8
+    dma = pltpu.SemaphoreType.DMA
+    seqs, rows, width = x.shape
+    return pl.pallas_call(
+        functools.partial(prologue_kernel, n_a),
+        name="prologue",
+        out_shape=(
+            jax.ShapeDtypeStruct((2, n_a) + w.shape, w.dtype),
+            jax.ShapeDtypeStruct((seqs, 4, rows, width), x.dtype),
+            jax.ShapeDtypeStruct((n_dev,) + gains.shape, gains.dtype),
+        ),
+        in_specs=[VMEM_SPEC] * 3,
+        out_specs=(HBM_SPEC, HBM_SPEC, VMEM_SPEC),
+        scratch_shapes=gather_sems(n_a)
+        + [dma((3,)), dma((3,)), dma(()), dma((n_dev,)), dma((n_dev,))],
+        compiler_params=pltpu.CompilerParams(collective_id=1, has_side_effects=True),
+        cost_estimate=pl.CostEstimate(flops=0, bytes_accessed=40 << 20, transcendentals=0),
+    )(w, x, gains)
+
+
+def gather_kernel(n_a, own_ref, out_ref, *sems):
+    greet(fsdp_peers(n_a))
+    gather = FsdpGather(n_a, own_ref, out_ref, sems)
+    gather.start()
+    gather.forward()
+    gather.finish()
+
+
+def gather_blocks(own):
+    n_a = lax.axis_size("fsdp") // 2
+    return pl.pallas_call(
+        functools.partial(gather_kernel, n_a),
+        name="kv_gather",
+        out_shape=jax.ShapeDtypeStruct((2, n_a) + own.shape, own.dtype),
+        in_specs=[VMEM_SPEC],
+        out_specs=HBM_SPEC,
+        scratch_shapes=gather_sems(n_a),
+        compiler_params=pltpu.CompilerParams(collective_id=2, has_side_effects=True),
+        cost_estimate=pl.CostEstimate(flops=0, bytes_accessed=40 << 20, transcendentals=0),
+    )(own)
+
+
+def scatter_kernel(n_a, part_ref, out_ref, got, send, recv):
+    a, b, tp = coords(n_a)
+    peers = [
+        (e, d, lax.rem(a + d, n_a), lax.rem(b + e, 2))
+        for d in range(n_a)
+        for e in range(2)
+        if (d, e) != (0, 0)
+    ]
+    greet([(pa * 2 + pb, tp) for _, _, pa, pb in peers])
+    copies = [
+        remote(
+            part_ref.at[e, pa], got.at[2 * d + e - 1], send.at[2 * d + e - 1],
+            recv.at[2 * d + e - 1], pa * 2 + pb, tp,
+        )
+        for e, d, pa, pb in peers
+    ]
+    for copy in copies:
+        copy.start()
+    total = part_ref[0, a].astype(F32)
+    for i, copy in enumerate(copies):
+        copy.wait_recv()
+        total = total + got[i].astype(F32)
+    out_ref[...] = total
+    for copy in copies:
+        copy.wait_send()
+
+
+def scatter_blocks(part):
+    n_a = part.shape[1]
+    n = 2 * n_a - 1
+    dma = pltpu.SemaphoreType.DMA
+    return pl.pallas_call(
+        functools.partial(scatter_kernel, n_a),
+        name="kv_scatter",
+        out_shape=jax.ShapeDtypeStruct(part.shape[2:], F32),
+        in_specs=[VMEM_SPEC],
+        out_specs=VMEM_SPEC,
+        scratch_shapes=[pltpu.VMEM((n,) + part.shape[2:], part.dtype), dma((n,)), dma((n,))],
+        compiler_params=pltpu.CompilerParams(
+            collective_id=3, has_side_effects=True, vmem_limit_bytes=48 << 20
+        ),
+        cost_estimate=pl.CostEstimate(flops=0, bytes_accessed=40 << 20, transcendentals=0),
+    )(part)
+
+
+def gain_kernel(n_a, part_ref, out_ref, got, send, recv):
+    a, b, tp = coords(n_a)
+    n_dev = n_a * 8
+    me = (a * 2 + b) * 4 + tp
+    barrier = pltpu.get_barrier_semaphore()
+
+    def peer(k):
+        return lax.rem(me + k, n_dev)
+
+    @pl.loop(1, n_dev)
+    def _(k):
+        p = peer(k)
+        pl.semaphore_signal(barrier, inc=1, device_id=(p // 4, p % 4), device_id_type=MESH_ID)
+
+    pl.semaphore_wait(barrier, n_dev - 1)
+
+    def copy(k):
+        p = peer(k)
+        return remote(part_ref.at[p], got.at[k], send.at[k], recv.at[k], p // 4, p % 4)
+
+    @pl.loop(1, n_dev)
+    def _(k):
+        copy(k).start()
+
+    got[0] = part_ref[me]
+
+    @pl.loop(1, n_dev)
+    def _(k):
+        copy(k).wait()
+
+    out_ref[...] = jnp.sum(got[...], axis=0)
+
+
+def scatter_gains(part):
+    n_a = lax.axis_size("fsdp") // 2
+    dma = pltpu.SemaphoreType.DMA
+    n = part.shape[0]
+    return pl.pallas_call(
+        functools.partial(gain_kernel, n_a),
+        name="gain_scatter",
+        out_shape=jax.ShapeDtypeStruct(part.shape[1:], F32),
+        in_specs=[VMEM_SPEC],
+        out_specs=VMEM_SPEC,
+        scratch_shapes=[pltpu.VMEM(part.shape, F32), dma((n,)), dma((n,))],
+        compiler_params=pltpu.CompilerParams(collective_id=4, has_side_effects=True),
+    )(part)
 
 
 def row_offsets(idx, rows, y, c):
@@ -260,11 +535,19 @@
         even, odd = jnp.where(first, lo, hi), jnp.where(first, hi, lo)
         return jnp.stack([even, odd], axis=-2).reshape(v.shape[:-1] + (width,))
 
-    gains = lax.all_gather(
-        jnp.stack([gain_attn, gain_mlp]), ("fsdp", "tp"), axis=1, tiled=True
-    )
-    gains = to_rel(gains)
-    gain_first, gain_second = gains[0], gains[1]
+    x_rel = to_rel(hidden_in)
+    piece = gain_attn.shape[0]
+    fill = -2 * piece % 128
+    gain_row = jnp.pad(jnp.concatenate([gain_attn, gain_mlp]), (0, fill))
+    gain_row = jnp.broadcast_to(gain_row[None], (8, 2 * piece + fill))
+    qkv_w, x_all, gains = prologue(
+        jnp.concatenate([w_query, w_key, w_value], axis=1), x_rel, gain_row
+    )
+    gains = gains[:, 0]
+    gain_first = to_rel(gains[:, :piece].reshape(width))
+    gain_second = to_rel(gains[:, piece : 2 * piece].reshape(width))
+    qkv_a = qkv_w[0].reshape(half, -1)
+    qkv_b = qkv_w[1].reshape(half, -1)
     own_block = jnp.sum(
         jnp.where(jnp.arange(n_fsdp)[None, :] == fsdp_index, block_order, 0), axis=1
     )
@@ -305,13 +588,11 @@
             [u1 * cos_t + u2 * sin_t, u2 * cos_t - u1 * sin_t], axis=1
         ).reshape(-1, tokens)
 
-    qkv_a, qkv_b = gather_halves(jnp.concatenate([w_query, w_key, w_value], axis=1))
     out_a, out_b = gather_halves(w_out.T)
     gu_a, gu_b = gather_halves(jnp.concatenate([w_gate, w_up], axis=1))
     down_a, down_b = gather_halves(w_down.T)
 
-    x_rel = to_rel(hidden_in)
-    x_all = spread_rows(x_rel).astype(F32)
+    x_all = x_all.reshape(seqs, block, width).astype(F32)
     h_first = (x_all * inverse_rms(x_all) * gain_first).astype(BF16).reshape(tokens, width)
     gm = spread_rows(to_rel(cotangent).astype(BF16)).reshape(tokens, width)
     qkv_t = dot(qkv_a, h_first[:, :half], 0, 1) + dot(qkv_b, h_first[:, half:], 0, 1)
@@ -322,7 +603,7 @@
     kv_own = (
         kv_t.reshape(2 * HD, seqs, block).transpose(2, 1, 0).reshape(block, seqs * 2 * HD)
     )
-    kv = jnp.concatenate(gather_halves(kv_own), axis=0)
+    kv = gather_blocks(kv_own).reshape(n_fsdp * block, -1)
     kv_all_t = kv.T
     o_t, lse = attention_forward(tab, q_t, kv, kv_all_t, n_fsdp, block, rows)
 
@@ -371,10 +652,7 @@
         tab, q_t, kv, kv_all_t, go_t, o_t, lse, n_fsdp, block, rows
     )
     out_g = scatter_halves(dot(ga[:, half:], o_t, 0, 1), lambda: dot(ga[:, :half], o_t, 0, 1))
-    seq_half = n_a * block
-    dkv_own = scatter_halves(
-        dkv[seq_half:], lambda: dkv[:seq_half].astype(F32)
-    ).astype(F32)
+    dkv_own = scatter_blocks(dkv.reshape(2, n_a, block, -1))
     dkv_t = dkv_own.reshape(block, seqs, 2 * HD).transpose(2, 1, 0).reshape(2 * HD, tokens)
     gq_t = rotate_back_t(dq_t * (HD**-0.5)).astype(BF16)
     gk_t = rotate_back_t(dkv_t[:HD]).astype(BF16)
@@ -385,23 +663,29 @@
     g_h1 = collect_rows([rows3(dot(g_qkv_t, qkv_a, 0, 1)), rows3(dot(g_qkv_t, qkv_b, 0, 1))])
     g_in_norm, gain_first_sum = norm_back(g_h1, x_own, gain_first, rms_first)
     g_in = g_mid + g_in_norm
-    gain_sums = lax.psum_scatter(
-        from_rel(jnp.stack([gain_first_sum, gain_second_sum])),
-        ("fsdp", "tp"),
-        scatter_dimension=1,
-        tiled=True,
-    )
+    gain_parts = jnp.concatenate(
+        [
+            from_rel(gain_first_sum).reshape(-1, piece),
+            from_rel(gain_second_sum).reshape(-1, piece),
+        ],
+        axis=1,
+    )
+    gain_parts = jnp.pad(gain_parts, ((0, 0), (0, fill)))
+    gain_parts = jnp.broadcast_to(
+        gain_parts[:, None], (n_fsdp * 4, 8, 2 * piece + fill)
+    )
+    gain_sums = scatter_gains(gain_parts)[0]
     qkv_g = qkv_g.astype(F32)
     gu_g = gu_g.astype(F32)
     return (
         from_rel(layer_out),
         from_rel(g_in),
-        gain_sums[0],
+        gain_sums[:piece],
         qkv_g[:, :q_width],
         qkv_g[:, q_width : q_width + HD],
         qkv_g[:, q_width + HD :],
         out_g.astype(F32).T,
-        gain_sums[1],
+        gain_sums[piece : 2 * piece],
         gu_g[:, :ff],
         gu_g[:, ff:],
         down_g.astype(F32).T,

time: 1070 us -> 990 us (0.925)
  Pallas kernels: 87.8 us -> 263 us
  waiting for transfers between devices: 631 us -> 479 us
  blocking collectives: 80.3 us -> 0 us
  matrix products: 116 us -> 105 us
    pallas_call x0 -> x4, Pallas kernels: none -> 175 us  [the longest x1 64 us: prologue(): pl.pallas_call(functools.partial(prologue_kernel, n_a), name='prologue',...]
    reduce_scatter x5 -> x4, waiting for transfers between devices: 129 us -> 37.5 us  [scatter_halves(): lax.psum_scatter(total, 'fsdp', scatter_dimension=0, tiled=True, axis_ind...]
    all_gather x2 -> x0, blocking collectives: 80.3 us -> none  [the longest x1 45.6 us: on_device(): lax.all_gather(jnp.stack([gain_attn, gain_mlp]), ('fsdp', 'tp'), axis=1,...]
    ppermute x10 -> x7, waiting for transfers between devices: 393 us -> 337 us  [swap_b(): return lax.ppermute(v, 'fsdp', [(i, i ^ 1) for i in range(n)])]
    all_gather x4 -> x3, waiting for transfers between devices: 22.9 us -> 1.92 us  [gather_halves(): lax.all_gather(shard, 'fsdp', axis=0, tiled=True, axis_index_groups=a_gro...]
    ppermute x24 -> x22, waiting for transfers between devices: 85.8 us -> 101 us  [swap_tp(): return lax.ppermute(v, 'tp', [(i, i ^ bit) for i in range(n)])]
  transfers between devices with their start and end apart: 44 -> 36, of which waited for: 20 -> 19; matrix products, arithmetic and copies ran while one was open for 15% -> 14% of each run, Pallas kernels for 4% -> 18%
where the time goes in v2:
time: 990 us; the launch traced here: 985 us
  waiting for transfers between devices  479 us (48%)
  Pallas kernels  263 us (27%)
  matrix products  105 us (11%)
  local copies, waits for them, and re-layouts  58.7 us (6%)
  other arithmetic  39.4 us (4%)
  starting transfers between devices  23.7 us (2%)
  between operations  15.9 us (2%)
    ppermute x7, waiting for transfers between devices, swap_b(): return lax.ppermute(v, 'fsdp', [(i, i ^ 1) for i in range(n)])  337 us
    dot_general x24, matrix products, dot(): lax.dot_general(a, b, (((ca,), (cb,)), ((), ())), preferred_element_type=...  105 us
    ppermute x22, waiting for transfers between devices, swap_tp(): return lax.ppermute(v, 'tp', [(i, i ^ bit) for i in range(n)])  101 us
    pallas_call x1, Pallas kernels, prologue(): pl.pallas_call(functools.partial(prologue_kernel, n_a), name='prologue',...  64 us
    pallas_call x1, Pallas kernels, gather_blocks(): pl.pallas_call(functools.partial(gather_kernel, n_a), name='kv_gather', o...  55.8 us
    pallas_call x1, Pallas kernels, attention_backward(): pl.pallas_call(functools.partial(bwd_kernel, n_blocks, block, rows, min(5...  44.8 us
    pallas_call x1, Pallas kernels, attention_forward(): pl.pallas_call(functools.partial(fwd_kernel, n_blocks, block, rows, min(5...  43.2 us
    pallas_call x1, Pallas kernels, scatter_blocks(): pl.pallas_call(functools.partial(scatter_kernel, n_a), name='kv_scatter',...  40.8 us
  transfers between devices with their start and end apart: 36, of which 19 were waited for; matrix products, arithmetic and copies ran while one was open for 14% of the time, Pallas kernels for 18%

profile of v2, /device:TPU:8, one launch (start us, length us, event | category | flops | bytes accessed | tf_op | source)
XLA Modules:
  0.0 984.9 jit_solution(12630876930422574332)
XLA Ops:
  8.0 2.6 pad_maximum_fusion.11
  16.1 64.0 %prologue.1 = (bf16[2,4,256,640]{3,2,1,0:T(8,128)(2,1)}, bf16[3,4,64,2048]{3,2,1,0:T(8,128)(2,1)}, f32[32,8,128]{2,1,0:T(8,128)}) custom-call(bf16[256,640]{1,0:T(8,128)(2,1)} %pad_maximum_fusion.14.w_ref, bf16[3,64,2048]{2,1,0:T(8,128)(2,1)} %copy-done.2, f32[8,128]{1,0:T(8,128)} %broadcast_in_dim.30.g_ref), custom_call_target="tpu_custom_call" | custom-call | bytes 41943040 | tf_op jit(solution)/shard_map/prologue/pallas_call | solution.py:223
  81.4 2.6 multiply_reduce_fusion
  84.4 2.6 copy-done.8
  93.7 55.8 %kv_gather.1 = bf16[2,4,256,384]{3,2,1,0:T(8,128)(2,1)} custom-call(bf16[256,384]{1,0:T(8,128)(2,1)} %copy.61.own_ref), custom_call_target="tpu_custom_call" | custom-call | bytes 41943040 | tf_op jit(solution)/shard_map/kv_gather/pallas_call | solution.py:250
  149.5 2.6 copy.83
  155.0 43.2 %attn_fwd.1 = (bf16[512,768]{1,0:T(8,128)(2,1)S(1)}, f32[8,1,768]{2,1,0:T(1,128)S(1)}) custom-call(s32[3,12]{1,0:T(4,128)S(1)} %concatenate.93.tab_ref, bf16[512,768]{1,0:T(8,128)(2,1)S(1)} %bitcast.110, bf16[2048,384]{1,0:T(8,128)(2,1)S(1)} %bitcast.106, bf16[384,2048]{1,0:T(8,128)(2,1)S(1)} %bitcast.108), custom_call_target="tpu_custom_call" | custom-call | flops 12884901888 | bytes 3145728 | tf_op jit(solution)/shard_map/attn_fwd/pallas_call | solution.py:450
  198.1 2.8 reshape.543
  225.4 5.6 collective-permute-done.1
  231.1 8.3 collective-permute-done.4
  246.7 9.7 collective-permute-done.13
  258.0 14.6 %collective-permute-done.5 = bf16[3,64,2048]{2,1,0:T(8,128)(2,1)} collective-permute-done((bf16[3,64,2048]{2,1,0:T(8,128)(2,1)}, bf16[3,64,2048]{2,1,0:T(8,128)(2,1)}, u32[]{:S(2)}, u32[]{:S(2)}) %collective-permute-start.5) | collective-permute-done | bytes 786464 | tf_op jit(solution)/shard_map/ppermute | solution.py:60
  279.1 125.2 %collective-permute-done.10 = bf16[1024,1408]{0,1:T(8,128)(2,1)S(1)} collective-permute-done((bf16[1024,1408]{0,1:T(8,128)(2,1)}, bf16[1024,1408]{0,1:T(8,128)(2,1)S(1)}, u32[]{:S(2)}, u32[]{:S(2)}) %collective-permute-start.10) | collective-permute-done | bytes 2883616 | tf_op jit(solution)/shard_map/ppermute | solution.py:37
  404.3 4.3 fusion.15
  408.6 9.6 fusion.20
  418.2 9.5 convolution_add_fusion
  427.7 8.5 multiply_convert_fusion.1
  436.2 5.0 fusion.72
  441.5 4.6 fusion.62
  446.8 8.0 fusion.61
  455.1 2.6 fusion.73
  463.9 15.2 %collective-permute-done.16 = bf16[3,64,1024]{2,1,0:T(8,128)(2,1)S(1)} collective-permute-done((bf16[3,64,1024]{2,1,0:T(8,128)(2,1)S(1)}, bf16[3,64,1024]{2,1,0:T(8,128)(2,1)S(1)}, u32[]{:S(2)}, u32[]{:S(2)}) %collective-permute-start.16) | collective-permute-done | bytes 393248 | tf_op jit(solution)/shard_map/ppermute | solution.py:60
  479.3 8.3 collective-permute-done.18
  488.3 6.8 collective-permute-done.12
  495.2 2.3 fusion.63
  498.9 17.1 %collective-permute-done.19 = bf16[3,64,2048]{2,1,0:T(8,128)(2,1)S(1)} collective-permute-done((bf16[3,64,2048]{2,1,0:T(8,128)(2,1)S(1)}, bf16[3,64,2048]{2,1,0:T(8,128)(2,1)S(1)}, u32[]{:S(2)}, u32[]{:S(2)}) %collective-permute-start.19) | collective-permute-done | bytes 786464 | tf_op jit(solution)/shard_map/ppermute | solution.py:60
  516.3 3.4 collective-permute-done.20
  522.0 2.3 fusion.10
  525.4 44.8 %attn_bwd.1 = (f32[512,768]{1,0:T(8,128)S(1)}, bf16[2048,384]{1,0:T(8,128)(2,1)S(1)}) custom-call(s32[3,12]{1,0:T(4,128)S(1)} %concatenate.93.tab_ref, bf16[512,768]{1,0:T(8,128)(2,1)S(1)} %bitcast.111, bf16[2048,384]{1,0:T(8,128)(2,1)} %bitcast.105, bf16[384,2048]{1,0:T(8,128)(2,1)} %bitcast.107, bf16[512,768]{1,0:T(8,128)(2,1)S(1)} %fusion.32.go_ref, ...), custom_call_target="tpu_custom_call" | custom-call | flops 32212254720 | bytes 6291456 | tf_op jit(solution)/shard_map/attn_bwd/pallas_call | solution.py:478
  570.2 40.8 %kv_scatter.1 = f32[256,384]{1,0:T(8,128)S(1)} custom-call(bf16[2,4,256,384]{3,2,1,0:T(8,128)(2,1)S(1)} %bitcast.109), custom_call_target="tpu_custom_call" | custom-call | bytes 41943040 | tf_op jit(solution)/shard_map/kv_scatter/pallas_call | solution.py:293
  615.8 21.6 %collective-permute-done.26 = bf16[1024,512]{1,0:T(8,128)(2,1)} collective-permute-done((bf16[1024,512]{1,0:T(8,128)(2,1)}, bf16[1024,512]{1,0:T(8,128)(2,1)}, u32[]{:S(2)}, u32[]{:S(2)}) %collective-permute-start.26) | collective-permute-done | bytes 1048608 | tf_op jit(solution)/shard_map/ppermute | solution.py:37
  637.4 3.7 add_convert_fusion.3
  641.4 3.3 convolution_convert_fusion.2
  646.2 4.0 convolution_convert_fusion.1
  650.8 25.6 %collective-permute-done.25 = bf16[1024,640]{1,0:T(8,128)(2,1)S(1)} collective-permute-done((bf16[1024,640]{1,0:T(8,128)(2,1)S(1)}, bf16[1024,640]{1,0:T(8,128)(2,1)S(1)}, u32[]{:S(2)}, u32[]{:S(2)}) %collective-permute-start.25) | collective-permute-done | bytes 1310752 | tf_op jit(solution)/shard_map/ppermute | solution.py:37
  676.3 2.5 add_convert_fusion.2
  679.0 9.0 convolution_convert_fusion
  689.5 48.8 %collective-permute-done.28 = bf16[1024,1408]{1,0:T(8,128)(2,1)} collective-permute-done((bf16[1024,1408]{1,0:T(8,128)(2,1)}, bf16[1024,1408]{1,0:T(8,128)(2,1)}, u32[]{:S(2)}, u32[]{:S(2)}) %collective-permute-start.28) | collective-permute-done | bytes 2883616 | tf_op jit(solution)/shard_map/ppermute | solution.py:37
  738.2 5.4 add_convert_fusion.1
  743.7 116.3 %collective-permute-done.27 = bf16[1024,2816]{1,0:T(8,128)(2,1)} collective-permute-done((bf16[1024,2816]{1,0:T(8,128)(2,1)}, bf16[1024,2816]{1,0:T(8,128)(2,1)}, u32[]{:S(2)}, u32[]{:S(2)}) %collective-permute-start.27) | collective-permute-done | bytes 5767200 | tf_op jit(solution)/shard_map/ppermute | solution.py:37
  860.0 9.9 %add_convert_fusion = bf16[1024,2816]{1,0:T(8,128)(2,1)} fusion(bf16[1024,2816]{1,0:T(8,128)(2,1)} %collective-permute-done.27, bf16[768,2048]{1,0:T(8,128)(2,1)S(1)} %bitcast.121, bf16[768,1408]{1,0:T(8,128)(2,1)} %get-tuple-element.56, bf16[768,1408]{1,0:T(8,128)(2,1)} %copy-done.53), kind=kOutput, calls=%fused_computation | convolution fusion | flops 4446486528 | bytes 17432576 | tf_op jit(solution)/shard_map/dot_general | solution.py:32
  889.4 2.4 reshape.542
  891.8 3.2 collective-permute-done.22
  896.1 6.8 collective-permute-done.24
  905.6 14.3 %gain_scatter.1 = f32[8,128]{1,0:T(8,128)} custom-call(f32[32,8,128]{2,1,0:T(8,128)} %broadcast_in_dim.31.part_ref), custom_call_target="tpu_custom_call" | custom-call | tf_op jit(solution)/shard_map/gain_scatter/pallas_call | solution.py:344
  924.3 2.4 reshape.552
  937.1 37.5 %reduce-scatter.9.cloned.1.call-done = bf16[256,2816]{1,0:T(8,128)(2,1)} async-done(((bf16[1024,2816]{1,0:T(8,128)(2,1)}), bf16[256,2816]{1,0:T(8,128)(2,1)}) %reduce-scatter.9.cloned.1.call-update) | async-done | bytes 1441808 | tf_op jit(solution)/shard_map/reduce_scatter | solution.py:53
  974.7 3.1 fusion.66
  (337 shorter events, 116.4 us)
Async XLA Ops:
  7.2 145.8 %all-gather.4.cloned.1.call-start = ((), (), s32[]{:S(2)}) async-start(), calls=%async_computation.4 | async-start | bytes 1310720 | tf_op jit(solution)/shard_map/all_gather | solution.py:46
  7.9 207.6 %all-gather.6.cloned.1.call-start = ((), (), s32[]{:S(2)}) async-start(), calls=%async_computation.5 | async-start | bytes 7208960 | tf_op jit(solution)/shard_map/all_gather | solution.py:46
  10.6 234.4 %all-gather.8.cloned.1.call-start = ((), (), s32[]{:S(2)}) async-start(), calls=%async_computation.6 | async-start | bytes 3604480 | tf_op jit(solution)/shard_map/all_gather | solution.py:46
  11.3 916.7 %reduce-scatter.7.cloned.1.call-start = ((), (), s32[]{:S(2)}) async-start(), calls=%async_computation.8 | async-start | bytes 1310720 | tf_op jit(solution)/shard_map/reduce_scatter | solution.py:53
  11.4 80.7 %copy-start.45 = (f32[32]{0:T(128)}, f32[32]{0:T(128)S(1)}, u32[]{:S(2)}) copy-start(f32[32]{0:T(128)S(1)} %negate_power_fusion) | copy-start | bytes 388
  93.7 58.7 %copy-start.47 = (s32[3]{0:T(128)S(1)}, s32[3]{0:T(128)}, u32[]{:S(2)}) copy-start(s32[3]{0:T(128)} %param.24) | copy-start | bytes 40
  152.9 52.1 %collective-permute-start.2 = (bf16[1024,512]{0,1:T(8,128)(2,1)}, bf16[1024,512]{0,1:T(8,128)(2,1)}, u32[]{:S(2)}, u32[]{:S(2)}) collective-permute-start(bf16[1024,512]{0,1:T(8,128)(2,1)} %all-gather.4.cloned.1.call-done), channel_id=1, source_target_pairs={{0,4},{4,0},{8,12},{12,8},{16,20},{20,16},{24,28},{28,24},{1,5},{5... | collective-permute-start | bytes 3145736 | tf_op jit(solution)/shard_map/ppermute | solution.py:37
  204.3 12.7 %collective-permute-start = (bf16[3,128,1024]{2,1,0:T(8,128)(2,1)}, bf16[3,128,1024]{2,1,0:T(8,128)(2,1)}, u32[]{:S(2)}, u32[]{:S(2)}) collective-permute-start(bf16[3,128,1024]{2,1,0:T(8,128)(2,1)} %slice.622), channel_id=1, source_target_pairs={{0,1},{1,0},{2,3},{3,2},{4,5},{5,4},{6,7},{7,6},{8,9},{9,8},{10,11... | collective-permute-start | bytes 2359304 | tf_op jit(solution)/shard_map/ppermute | solution.py:60
  210.0 10.5 %collective-permute-start.3 = (bf16[3,128,1024]{2,1,0:T(8,128)(2,1)}, bf16[3,128,1024]{2,1,0:T(8,128)(2,1)}, u32[]{:S(2)}, u32[]{:S(2)}) collective-permute-start(bf16[3,128,1024]{2,1,0:T(8,128)(2,1)} %slice.621), channel_id=1, source_target_pairs={{0,1},{1,0},{2,3},{3,2},{4,5},{5,4},{6,7},{7,6},{8,9},{9,8},{10,11... | collective-permute-start | bytes 2359304 | tf_op jit(solution)/shard_map/ppermute | solution.py:60
  215.5 193.0 %collective-permute-start.7 = (bf16[1024,2816]{1,0:T(8,128)(2,1)}, bf16[1024,2816]{1,0:T(8,128)(2,1)}, u32[]{:S(2)}, u32[]{:S(2)}) collective-permute-start(bf16[1024,2816]{1,0:T(8,128)(2,1)} %all-gather.6.cloned.1.call-done), channel_id=1, source_target_pairs={{0,4},{4,0},{8,12},{12,8},{16,20},{20,16},{24,28},{28,24},{1,5},{5... | collective-permute-start | bytes 17301512 | tf_op jit(solution)/shard_map/ppermute | solution.py:37
  219.0 12.1 %collective-permute-start.1 = (bf16[3,64,1024]{2,1,0:T(8,128)(2,1)S(1)}, bf16[3,64,1024]{2,1,0:T(8,128)(2,1)S(1)}, u32[]{:S(2)}, u32[]{:S(2)}) collective-permute-start(bf16[3,64,1024]{2,1,0:T(8,128)(2,1)S(1)} %slice.630), channel_id=1, source_target_pairs={{0,2},{1,3},{2,0},{3,1},{4,6},{5,7},{6,4},{7,5},{8,10},{9,11},{10,... | collective-permute-start | bytes 1179656 | tf_op jit(solution)/shard_map/ppermute | solution.py:60
  222.0 17.4 %collective-permute-start.4 = (bf16[3,64,1024]{2,1,0:T(8,128)(2,1)S(1)}, bf16[3,64,1024]{2,1,0:T(8,128)(2,1)S(1)}, u32[]{:S(2)}, u32[]{:S(2)}) collective-permute-start(bf16[3,64,1024]{2,1,0:T(8,128)(2,1)S(1)} %slice.629), channel_id=1, source_target_pairs={{0,2},{1,3},{2,0},{3,1},{4,6},{5,7},{6,4},{7,5},{8,10},{9,11},{10,... | collective-permute-start | bytes 1179656 | tf_op jit(solution)/shard_map/ppermute | solution.py:60
  223.9 15.6 %copy-start.3 = (bf16[3,64,2048]{2,1,0:T(8,128)(2,1)S(1)}, bf16[3,64,2048]{2,1,0:T(8,128)(2,1)}, u32[]{:S(2)}) copy-start(bf16[3,64,2048]{2,1,0:T(8,128)(2,1)} %copy-done.2) | copy-start | bytes 2359300
  223.9 32.5 %collective-permute-start.13 = (bf16[3,64,2048]{2,1,0:T(8,128)(2,1)}, bf16[3,64,2048]{2,1,0:T(8,128)(2,1)}, u32[]{:S(2)}, u32[]{:S(2)}) collective-permute-start(bf16[3,64,2048]{2,1,0:T(8,128)(2,1)} %convert_element_type.191), channel_id=1, source_target_pairs={{0,2},{1,3},{2,0},{3,1},{4,6},{5,7},{6,4},{7,5},{8,10},{9,11},{10,... | collective-permute-start | bytes 2359304 | tf_op jit(solution)/shard_map/ppermute | solution.py:60
  241.6 30.9 %collective-permute-start.5 = (bf16[3,64,2048]{2,1,0:T(8,128)(2,1)}, bf16[3,64,2048]{2,1,0:T(8,128)(2,1)}, u32[]{:S(2)}, u32[]{:S(2)}) collective-permute-start(bf16[3,64,2048]{2,1,0:T(8,128)(2,1)} %multiply_convert_fusion.3), channel_id=1, source_target_pairs={{0,2},{1,3},{2,0},{3,1},{4,6},{5,7},{6,4},{7,5},{8,10},{9,11},{10,... | collective-permute-start | bytes 2359304 | tf_op jit(solution)/shard_map/ppermute | solution.py:60
  245.0 159.3 %collective-permute-start.10 = (bf16[1024,1408]{0,1:T(8,128)(2,1)}, bf16[1024,1408]{0,1:T(8,128)(2,1)S(1)}, u32[]{:S(2)}, u32[]{:S(2)}) collective-permute-start(bf16[1024,1408]{0,1:T(8,128)(2,1)} %all-gather.8.cloned.1.call-done), channel_id=1, source_target_pairs={{0,4},{4,0},{8,12},{12,8},{16,20},{20,16},{24,28},{28,24},{1,5},{5... | collective-permute-start | bytes 8650760 | tf_op jit(solution)/shard_map/ppermute | solution.py:37
  257.9 16.2 %collective-permute-start.14 = (bf16[3,128,2048]{2,1,0:T(8,128)(2,1)S(1)}, bf16[3,128,2048]{2,1,0:T(8,128)(2,1)S(1)}, u32[]{:S(2)}, u32[]{:S(2)}) collective-permute-start(bf16[3,128,2048]{2,1,0:T(8,128)(2,1)S(1)} %pad_maximum_fusion.6), channel_id=1, source_target_pairs={{0,1},{1,0},{2,3},{3,2},{4,5},{5,4},{6,7},{7,6},{8,9},{9,8},{10,11... | collective-permute-start | bytes 4718600 | tf_op jit(solution)/shard_map/ppermute | solution.py:60
  274.0 3.5 collective-permute-start.6
  275.7 152.0 %copy-start.15 = (bf16[3,256,2048]{2,1,0:T(8,128)(2,1)}, bf16[3,256,2048]{2,1,0:T(8,128)(2,1)S(1)}, u32[]{:S(2)}) copy-start(bf16[3,256,2048]{2,1,0:T(8,128)(2,1)S(1)} %pad_maximum_fusion.2) | copy-start | bytes 9437188
  279.1 139.1 %copy-start.13 = (bf16[3,256,2048]{2,1,0:T(8,128)(2,1)}, bf16[3,256,2048]{2,1,0:T(8,128)(2,1)S(1)}, u32[]{:S(2)}) copy-start(bf16[3,256,2048]{2,1,0:T(8,128)(2,1)S(1)} %pad_maximum_fusion.1) | copy-start | bytes 9437188
  404.3 13.9 %slice-start = ((s8[5767168]{0:T(1024)(128)(4,1)}), s8[4194304]{0:T(1024)(128)(4,1)S(1)}, s32[]{:S(2)}) async-start(s8[5767168]{0:T(1024)(128)(4,1)} %bitcast.165), calls=%async_computation.11 | async-start | bytes 8388608
  441.4 17.0 %collective-permute-start.8 = (bf16[3,128,1024]{2,1,0:T(8,128)(2,1)S(1)}, bf16[3,128,1024]{2,1,0:T(8,128)(2,1)S(1)}, u32[]{:S(2)}, u32[]{:S(2)}) collective-permute-start(bf16[3,128,1024]{2,1,0:T(8,128)(2,1)S(1)} %slice.620), channel_id=1, source_target_pairs={{0,1},{1,0},{2,3},{3,2},{4,5},{5,4},{6,7},{7,6},{8,9},{9,8},{10,11... | collective-permute-start | bytes 2359304 | tf_op jit(solution)/shard_map/ppermute | solution.py:60
  446.3 13.9 %collective-permute-start.15 = (bf16[3,128,1024]{2,1,0:T(8,128)(2,1)S(1)}, bf16[3,128,1024]{2,1,0:T(8,128)(2,1)S(1)}, u32[]{:S(2)}, u32[]{:S(2)}) collective-permute-start(bf16[3,128,1024]{2,1,0:T(8,128)(2,1)S(1)} %slice.618), channel_id=1, source_target_pairs={{0,1},{1,0},{2,3},{3,2},{4,5},{5,4},{6,7},{7,6},{8,9},{9,8},{10,11... | collective-permute-start | bytes 2359304 | tf_op jit(solution)/shard_map/ppermute | solution.py:60
  455.0 6.1 collective-permute-start.17
  457.8 5.1 collective-permute-start.11
  458.7 29.5 %collective-permute-start.9 = (bf16[3,64,1024]{2,1,0:T(8,128)(2,1)S(1)}, bf16[3,64,1024]{2,1,0:T(8,128)(2,1)S(1)}, u32[]{:S(2)}, u32[]{:S(2)}) collective-permute-start(bf16[3,64,1024]{2,1,0:T(8,128)(2,1)S(1)} %slice.628), channel_id=1, source_target_pairs={{0,2},{1,3},{2,0},{3,1},{4,6},{5,7},{6,4},{7,5},{8,10},{9,11},{10,... | collective-permute-start | bytes 1179656 | tf_op jit(solution)/shard_map/ppermute | solution.py:60
  460.5 18.7 %collective-permute-start.16 = (bf16[3,64,1024]{2,1,0:T(8,128)(2,1)S(1)}, bf16[3,64,1024]{2,1,0:T(8,128)(2,1)S(1)}, u32[]{:S(2)}, u32[]{:S(2)}) collective-permute-start(bf16[3,64,1024]{2,1,0:T(8,128)(2,1)S(1)} %slice.626), channel_id=1, source_target_pairs={{0,2},{1,3},{2,0},{3,1},{4,6},{5,7},{6,4},{7,5},{8,10},{9,11},{10,... | collective-permute-start | bytes 1179656 | tf_op jit(solution)/shard_map/ppermute | solution.py:60
  461.4 26.2 %collective-permute-start.18 = (bf16[3,64,1024]{2,1,0:T(8,128)(2,1)S(1)}, bf16[3,64,1024]{2,1,0:T(8,128)(2,1)S(1)}, u32[]{:S(2)}, u32[]{:S(2)}) collective-permute-start(bf16[3,64,1024]{2,1,0:T(8,128)(2,1)S(1)} %slice.625), channel_id=1, source_target_pairs={{0,2},{1,3},{2,0},{3,1},{4,6},{5,7},{6,4},{7,5},{8,10},{9,11},{10,... | collective-permute-start | bytes 1179656 | tf_op jit(solution)/shard_map/ppermute | solution.py:60
  463.3 31.7 %collective-permute-start.12 = (bf16[3,64,1024]{2,1,0:T(8,128)(2,1)S(1)}, bf16[3,64,1024]{2,1,0:T(8,128)(2,1)S(1)}, u32[]{:S(2)}, u32[]{:S(2)}) collective-permute-start(bf16[3,64,1024]{2,1,0:T(8,128)(2,1)S(1)} %slice.627), channel_id=1, source_target_pairs={{0,2},{1,3},{2,0},{3,1},{4,6},{5,7},{6,4},{7,5},{8,10},{9,11},{10,... | collective-permute-start | bytes 1179656 | tf_op jit(solution)/shard_map/ppermute | solution.py:60
  497.5 18.6 %collective-permute-start.19 = (bf16[3,64,2048]{2,1,0:T(8,128)(2,1)S(1)}, bf16[3,64,2048]{2,1,0:T(8,128)(2,1)S(1)}, u32[]{:S(2)}, u32[]{:S(2)}) collective-permute-start(bf16[3,64,2048]{2,1,0:T(8,128)(2,1)S(1)} %get-tuple-element.51), channel_id=1, source_target_pairs={{0,2},{1,3},{2,0},{3,1},{4,6},{5,7},{6,4},{7,5},{8,10},{9,11},{10,... | collective-permute-start | bytes 2359304 | tf_op jit(solution)/shard_map/ppermute | solution.py:60
  516.2 3.5 collective-permute-start.20
  611.9 25.5 %collective-permute-start.26 = (bf16[1024,512]{1,0:T(8,128)(2,1)}, bf16[1024,512]{1,0:T(8,128)(2,1)}, u32[]{:S(2)}, u32[]{:S(2)}) collective-permute-start(bf16[1024,512]{1,0:T(8,128)(2,1)} %convolution_convert_fusion.3), channel_id=1, source_target_pairs={{0,4},{4,0},{8,12},{12,8},{16,20},{20,16},{24,28},{28,24},{1,5},{5... | collective-permute-start | bytes 3145736 | tf_op jit(solution)/shard_map/ppermute | solution.py:37
  641.1 288.9 %reduce-scatter.5.cloned.1.call-start = ((), (), s32[]{:S(2)}) async-start(), calls=%async_computation.7 | async-start | bytes 1638400 | tf_op jit(solution)/shard_map/reduce_scatter | solution.py:53
  641.3 35.0 %copy-start.31 = (bf16[640,768]{0,1:T(8,128)(2,1)}, bf16[640,768]{0,1:T(8,128)(2,1)S(1)}, u32[]{:S(2)}) copy-start(bf16[640,768]{0,1:T(8,128)(2,1)S(1)} %pad_maximum_fusion.12) | copy-start | bytes 2949124
  644.6 31.7 %copy-start.21 = (bf16[768,2048]{1,0:T(8,128)(2,1)S(1)}, bf16[768,2048]{1,0:T(8,128)(2,1)}, u32[]{:S(2)}) copy-start(bf16[768,2048]{1,0:T(8,128)(2,1)} %copy-done.20) | copy-start | bytes 9437188
  644.6 31.7 %collective-permute-start.25 = (bf16[1024,640]{1,0:T(8,128)(2,1)S(1)}, bf16[1024,640]{1,0:T(8,128)(2,1)S(1)}, u32[]{:S(2)}, u32[]{:S(2)}) collective-permute-start(bf16[1024,640]{1,0:T(8,128)(2,1)S(1)} %convolution_convert_fusion.2), channel_id=1, source_target_pairs={{0,4},{4,0},{8,12},{12,8},{16,20},{20,16},{24,28},{28,24},{1,5},{5... | collective-permute-start | bytes 3932168 | tf_op jit(solution)/shard_map/ppermute | solution.py:37
  650.2 28.7 %copy-start.14 = (bf16[3,256,2048]{2,1,0:T(8,128)(2,1)S(1)}, bf16[3,256,2048]{2,1,0:T(8,128)(2,1)}, u32[]{:S(2)}) copy-start(bf16[3,256,2048]{2,1,0:T(8,128)(2,1)} %copy-done.13) | copy-start | bytes 9437188
  650.2 88.0 %collective-permute-start.28 = (bf16[1024,1408]{1,0:T(8,128)(2,1)}, bf16[1024,1408]{1,0:T(8,128)(2,1)}, u32[]{:S(2)}, u32[]{:S(2)}) collective-permute-start(bf16[1024,1408]{1,0:T(8,128)(2,1)} %convolution_convert_fusion.1), channel_id=1, source_target_pairs={{0,4},{4,0},{8,12},{12,8},{16,20},{20,16},{24,28},{28,24},{1,5},{5... | collective-permute-start | bytes 8650760 | tf_op jit(solution)/shard_map/ppermute | solution.py:37
  678.9 255.5 %reduce-scatter.11.cloned.1.call-start = ((), (), s32[]{:S(2)}) async-start(), calls=%async_computation.10 | async-start | bytes 3604480 | tf_op jit(solution)/shard_map/reduce_scatter | solution.py:53
  679.0 59.3 %copy-start.17 = (bf16[3,256,2048]{2,1,0:T(8,128)(2,1)S(1)}, bf16[3,256,2048]{2,1,0:T(8,128)(2,1)}, u32[]{:S(2)}) copy-start(bf16[3,256,2048]{2,1,0:T(8,128)(2,1)} %copy-done.15) | copy-start | bytes 9437188
  679.0 59.3 %copy-start.57 = (bf16[768,1408]{1,0:T(8,128)(2,1)S(1)}, bf16[768,1408]{1,0:T(8,128)(2,1)}, u32[]{:S(2)}) copy-start(bf16[768,1408]{1,0:T(8,128)(2,1)} %get-tuple-element.57) | copy-start | bytes 6488068
  688.0 172.1 %collective-permute-start.27 = (bf16[1024,2816]{1,0:T(8,128)(2,1)}, bf16[1024,2816]{1,0:T(8,128)(2,1)}, u32[]{:S(2)}, u32[]{:S(2)}) collective-permute-start(bf16[1024,2816]{1,0:T(8,128)(2,1)} %convolution_convert_fusion), channel_id=1, source_target_pairs={{0,4},{4,0},{8,12},{12,8},{16,20},{20,16},{24,28},{28,24},{1,5},{5... | collective-permute-start | bytes 17301512 | tf_op jit(solution)/shard_map/ppermute | solution.py:37
  743.7 231.0 %reduce-scatter.9.cloned.1.call-start = ((), (), s32[]{:S(2)}) async-start(), calls=%async_computation.9 | async-start | bytes 7208960 | tf_op jit(solution)/shard_map/reduce_scatter | solution.py:53
  874.1 6.7 collective-permute-start.21
  879.1 5.2 collective-permute-start.23
  882.9 12.2 %collective-permute-start.22 = (bf16[3,64,1024]{2,1,0:T(8,128)(2,1)S(1)}, bf16[3,64,1024]{2,1,0:T(8,128)(2,1)}, u32[]{:S(2)}, u32[]{:S(2)}) collective-permute-start(bf16[3,64,1024]{2,1,0:T(8,128)(2,1)S(1)} %slice.624), channel_id=1, source_target_pairs={{0,2},{1,3},{2,0},{3,1},{4,6},{5,7},{6,4},{7,5},{8,10},{9,11},{10,... | collective-permute-start | bytes 1179656 | tf_op jit(solution)/shard_map/ppermute | solution.py:60
  887.2 15.8 %collective-permute-start.24 = (bf16[3,64,1024]{2,1,0:T(8,128)(2,1)}, bf16[3,64,1024]{2,1,0:T(8,128)(2,1)}, u32[]{:S(2)}, u32[]{:S(2)}) collective-permute-start(bf16[3,64,1024]{2,1,0:T(8,128)(2,1)} %slice.623), channel_id=1, source_target_pairs={{0,2},{1,3},{2,0},{3,1},{4,6},{5,7},{6,4},{7,5},{8,10},{9,11},{10,... | collective-permute-start | bytes 1179656 | tf_op jit(solution)/shard_map/ppermute | solution.py:60
  891.8 12.5 %copy-start.37 = (f32[2048]{0:T(1024)S(1)}, f32[2048]{0:T(1024)}, u32[]{:S(2)}) copy-start(f32[2048]{0:T(1024)} %copy-done.36) | copy-start | bytes 24580
  (48 other events, 175.0 us)
Sparse Core Ops, SparseCore 0:
  9.5 51.5 all-gather.3
  63.3 121.6 all-gather.5
  186.5 58.4 all-gather.7
  641.2 25.3 reduce-scatter.6
  679.0 29.6 reduce-scatter.4
  743.8 55.7 reduce-scatter.10
  870.1 104.5 reduce-scatter.8

commit v3 on v2

v3 whole, which is shorter than its diff:
```python
import functools

import jax
import jax.numpy as jnp
from jax import lax
from jax.experimental import pallas as pl
from jax.experimental.pallas import tpu as pltpu
from jax.sharding import PartitionSpec as P

HD = 64
EPS = 1e-05
THETA = 10000.0
NEG = -1000000000.0
F32 = jnp.float32
BF16 = jnp.bfloat16


def inverse_rms(values):
    return lax.rsqrt(jnp.mean(values * values, axis=-1, keepdims=True) + EPS)


def norm_back(upstream, values, gain_vec, inv_rms):
    weighted = upstream * gain_vec
    inner_mean = jnp.mean(weighted * values, axis=-1, keepdims=True)
    return (
        inv_rms * weighted - values * (inv_rms * inv_rms * inv_rms) * inner_mean,
        jnp.sum(upstream * values * inv_rms, axis=0),
    )


def dot(a, b, ca, cb):
    return lax.dot_general(a, b, (((ca,), (cb,)), ((), ())), preferred_element_type=F32)


def swap_b(v):
    n = lax.axis_size("fsdp")
    return lax.ppermute(v, "fsdp", [(i, i ^ 1) for i in range(n)])


def swap_tp(v, bit):
    n = lax.axis_size("tp")
    return lax.ppermute(v, "tp", [(i, i ^ bit) for i in range(n)])


def a_groups():
    n = lax.axis_size("fsdp")
    return [[b + 2 * a for a in range(n // 2)] for b in range(2)]


def gather_a(shard):
    return lax.all_gather(shard, "fsdp", axis=0, tiled=True, axis_index_groups=a_groups())


def scatter_a(part):
    return lax.psum_scatter(
        part, "fsdp", scatter_dimension=0, tiled=True, axis_index_groups=a_groups()
    )


MESH_ID = pl.DeviceIdType.MESH
HBM_SPEC = pl.BlockSpec(memory_space=pl.ANY)
VMEM_SPEC = pl.BlockSpec(memory_space=pltpu.VMEM)
DMA = pltpu.SemaphoreType.DMA


def coords(n_a):
    fsdp, tp = lax.axis_index("fsdp"), lax.axis_index("tp")
    return fsdp // 2, fsdp % 2, tp


def remote(src, dst, sems, i, device):
    return pltpu.make_async_remote_copy(
        src_ref=src,
        dst_ref=dst,
        send_sem=sems[0].at[i],
        recv_sem=sems[1].at[i],
        device_id=device,
        device_id_type=MESH_ID,
    )


def greet(peers):
    barrier = pltpu.get_barrier_semaphore()
    for peer in peers:
        pl.semaphore_signal(barrier, inc=1, device_id=peer, device_id_type=MESH_ID)
    pl.semaphore_wait(barrier, len(peers))


def x_peer(n_a):
    a, b, tp = coords(n_a)
    return (a * 2 + 1 - b, tp)


def y_peer(n_a):
    a, b, tp = coords(n_a)
    return (a * 2 + b, lax.rem(tp + 2, 4))


def c_peer(n_a):
    a, b, tp = coords(n_a)
    return (a * 2 + b, tp + 1 - 2 * (tp % 2))


def a_peers(n_a):
    a, b, tp = coords(n_a)
    return [(lax.rem(a + d, n_a) * 2 + b, tp) for d in range(1, n_a)]


class FsdpGather:
    def __init__(self, n_a, own, out, slot, sems):
        self.n_a, self.own, self.out, self.slot = n_a, own, out, slot
        self.z, self.x, self.local = sems[:2], sems[2:4], sems[4]

    def at(self, e, a):
        i, j = self.slot(e, a)
        return self.out.at[i, j]

    def z_copy(self, d):
        a, _, _ = coords(self.n_a)
        return remote(self.own, self.at(0, a), self.z, d, a_peers(self.n_a)[d - 1])

    def x_copy(self, d):
        a, _, _ = coords(self.n_a)
        at = lax.rem(a + self.n_a - d, self.n_a)
        src = self.own if d == 0 else self.at(0, at)
        return remote(src, self.at(1, at), self.x, d, x_peer(self.n_a))

    def mine(self):
        a, _, _ = coords(self.n_a)
        return pltpu.make_async_copy(self.own, self.at(0, a), self.local)

    def start(self):
        self.x_copy(0).start()
        for d in range(1, self.n_a):
            self.z_copy(d).start()
        self.mine().start()

    def forward(self):
        for d in range(1, self.n_a):
            self.z_copy(d).wait_recv()
            self.x_copy(d).start()

    def finish(self):
        for d in range(1, self.n_a):
            self.z_copy(d).wait_send()
        for d in range(self.n_a):
            self.x_copy(d).wait()
        self.mine().wait()

    @staticmethod
    def scratch(n_a):
        return [DMA((n_a,)), DMA((n_a,)), DMA((n_a,)), DMA((n_a,)), DMA(())]


class TpGather:
    def __init__(self, n_a, own, out, sems):
        self.to_y = remote(own, out.at[:, 1], sems[:2], 0, y_peer(n_a))
        self.to_c = remote(own, out.at[:, 2], sems[:2], 1, c_peer(n_a))
        self.fwd = remote(out.at[:, 1], out.at[:, 3], sems[:2], 2, c_peer(n_a))
        self.mine = pltpu.make_async_copy(own, out.at[:, 0], sems[2])

    def start(self):
        self.to_y.start()
        self.to_c.start()
        self.mine.start()

    def forward(self):
        self.to_y.wait_recv()
        self.fwd.start()

    def finish(self):
        self.to_y.wait_send()
        self.to_c.wait()
        self.fwd.wait()
        self.mine.wait()

    @staticmethod
    def scratch():
        return [DMA((3,)), DMA((3,)), DMA(())]


class PlaneGather:
    def __init__(self, n_a, own, out, sems):
        half = own.shape[0] // 2
        h = [pl.ds(0, half), pl.ds(half, half)]
        x, y, c = x_peer(n_a), y_peer(n_a), c_peer(n_a)
        pair = sems[:2]

        def to(src, slot, i, peer, part=None):
            dst = out.at[slot] if part is None else out.at[slot, h[part]]
            return remote(src, dst, pair, i, peer)

        self.x0 = to(own.at[h[0]], 4, 0, x, 0)
        self.x1 = to(own.at[h[1]], 4, 1, x, 1)
        self.y0 = to(own.at[h[0]], 2, 2, y, 0)
        self.y1 = to(own.at[h[1]], 2, 3, y, 1)
        self.xd = to(out.at[2, h[0]], 6, 4, x, 0)
        self.yd = to(out.at[4, h[1]], 6, 5, y, 1)
        self.c = [to(own, 1, 6, c)] + [to(out.at[k], k + 1, 6 + k // 2, c) for k in (2, 4, 6)]
        self.mine = pltpu.make_async_copy(own, out.at[0], sems[2])

    def start(self):
        for copy in (self.x1, self.y0, self.x0, self.y1, self.c[0], self.mine):
            copy.start()

    def forward(self):
        self.y0.wait_recv()
        self.xd.start()
        self.x1.wait_recv()
        self.yd.start()
        self.y1.wait_recv()
        self.c[1].start()
        self.x0.wait_recv()
        self.c[2].start()
        self.xd.wait_recv()
        self.yd.wait_recv()
        self.c[3].start()

    def finish(self):
        for copy in (self.x0, self.x1, self.y0, self.y1, self.xd, self.yd):
            copy.wait_send()
        for copy in self.c:
            copy.wait()
        self.mine.wait()

    @staticmethod
    def scratch():
        return [DMA((10,)), DMA((10,)), DMA(())]


def comm_call(kernel, name, cid, out_shape, n_in, out_specs, scratch):
    return pl.pallas_call(
        kernel,
        name=name,
        out_shape=out_shape,
        in_specs=[VMEM_SPEC] * n_in,
        out_specs=out_specs,
        scratch_shapes=scratch,
        compiler_params=pltpu.CompilerParams(
            collective_id=cid, has_side_effects=True, vmem_limit_bytes=48 << 20
        ),
        cost_estimate=pl.CostEstimate(flops=0, bytes_accessed=64 << 20, transcendentals=0),
    )


def prologue_kernel(n_a, w_ref, x_ref, g_ref, m_ref, wall_ref, xall_ref, gall_ref, mgot_ref, *sems):
    a, b, tp = coords(n_a)
    n_dev = n_a * 8
    me = (a * 2 + b) * 4 + tp
    barrier = pltpu.get_barrier_semaphore()
    gather = FsdpGather(n_a, w_ref, wall_ref, lambda e, at: (at, b), sems[:5])
    rows = TpGather(n_a, x_ref, xall_ref, sems[5:8])
    g_sems = sems[8:10]
    swap = remote(m_ref, mgot_ref, sems[10:12], 0, x_peer(n_a))

    def peer(k):
        p = lax.rem(me + k, n_dev)
        return p // 4, p % 4

    @pl.loop(1, n_dev)
    def _(k):
        pl.semaphore_signal(barrier, inc=1, device_id=peer(k), device_id_type=MESH_ID)

    pl.semaphore_wait(barrier, n_dev - 1)

    def gain_copy(k):
        return remote(g_ref, gall_ref.at[me], g_sems, k, peer(k))

    @pl.loop(1, n_dev)
    def _(k):
        gain_copy(k).start()

    gather.start()
    rows.start()
    swap.start()
    gall_ref[me] = g_ref[...]
    rows.forward()
    gather.forward()

    @pl.loop(1, n_dev)
    def _(k):
        gain_copy(k).wait()

    rows.finish()
    gather.finish()
    swap.wait()


def prologue(w, x, gains, mlp):
    n_a = lax.axis_size("fsdp") // 2
    n_dev = n_a * 8
    seqs, rows, width = x.shape
    return comm_call(
        functools.partial(prologue_kernel, n_a),
        "prologue",
        1,
        (
            jax.ShapeDtypeStruct((n_a, 2) + w.shape, w.dtype),
            jax.ShapeDtypeStruct((seqs, 4, rows, width), x.dtype),
            jax.ShapeDtypeStruct((n_dev,) + gains.shape, gains.dtype),
            jax.ShapeDtypeStruct(mlp.shape, mlp.dtype),
        ),
        4,
        (HBM_SPEC, HBM_SPEC, VMEM_SPEC, HBM_SPEC),
        FsdpGather.scratch(n_a)
        + TpGather.scratch()
        + [DMA((n_dev,)), DMA((n_dev,)), DMA((1,)), DMA((1,))],
    )(w, x, gains, mlp)


def kv_gather_kernel(n_a, own_ref, gm_ref, out_ref, gmall_ref, *sems):
    greet([x_peer(n_a), y_peer(n_a), c_peer(n_a)] + a_peers(n_a))
    gather = FsdpGather(n_a, own_ref, out_ref, lambda e, a: (e, a), sems[:5])
    plane = PlaneGather(n_a, gm_ref, gmall_ref, sems[5:8])
    gather.start()
    plane.start()
    gather.forward()
    plane.forward()
    gather.finish()
    plane.finish()


def kv_gather(own, gm):
    n_a = lax.axis_size("fsdp") // 2
    return comm_call(
        functools.partial(kv_gather_kernel, n_a),
        "kv_gather",
        2,
        (
            jax.ShapeDtypeStruct((2, n_a) + own.shape, own.dtype),
            jax.ShapeDtypeStruct((8,) + gm.shape, gm.dtype),
        ),
        2,
        (HBM_SPEC, HBM_SPEC),
        FsdpGather.scratch(n_a) + PlaneGather.scratch(),
    )(own, gm)


def plane_gather_kernel(n_a, own_ref, out_ref, *sems):
    greet([x_peer(n_a), y_peer(n_a), c_peer(n_a)])
    plane = PlaneGather(n_a, own_ref, out_ref, sems)
    plane.start()
    plane.forward()
    plane.finish()


def plane_gather(own):
    n_a = lax.axis_size("fsdp") // 2
    return comm_call(
        functools.partial(plane_gather_kernel, n_a),
        "plane_gather",
        5,
        jax.ShapeDtypeStruct((8,) + own.shape, own.dtype),
        1,
        HBM_SPEC,
        PlaneGather.scratch(),
    )(own)


def tp_gather_kernel(n_a, own_ref, out_ref, *sems):
    greet([y_peer(n_a), c_peer(n_a)])
    rows = TpGather(n_a, own_ref, out_ref, sems)
    rows.start()
    rows.forward()
    rows.finish()


def tp_gather(own):
    n_a = lax.axis_size("fsdp") // 2
    seqs, rows, width = own.shape
    return comm_call(
        functools.partial(tp_gather_kernel, n_a),
        "tp_gather",
        6,
        jax.ShapeDtypeStruct((seqs, 4, rows, width), own.dtype),
        1,
        HBM_SPEC,
        TpGather.scratch(),
    )(own)


def tp_scatter_kernel(n_a, part_ref, out_ref, got_c, mid, got_y, c_send, c_recv, y_send, y_recv):
    greet([y_peer(n_a), c_peer(n_a)])
    seqs = part_ref.shape[0]
    to_c = [
        remote(part_ref.at[s, pl.ds(2, 2)], got_c.at[s], (c_send, c_recv), s, c_peer(n_a))
        for s in range(seqs)
    ]
    to_y = [
        remote(mid.at[s], got_y.at[s], (y_send, y_recv), s, y_peer(n_a)) for s in range(seqs)
    ]
    for copy in to_c:
        copy.start()
    for s in range(seqs):
        to_c[s].wait_recv()
        mid[s] = (part_ref[s, 1].astype(F32) + got_c[s, 1].astype(F32)).astype(BF16)
        out_ref[s] = part_ref[s, 0].astype(F32) + got_c[s, 0].astype(F32)
        to_y[s].start()
    for s in range(seqs):
        to_y[s].wait_recv()
        out_ref[s] = out_ref[s] + got_y[s].astype(F32)
    for copy in to_c + to_y:
        copy.wait_send()


def tp_scatter(part, name, cid):
    n_a = lax.axis_size("fsdp") // 2
    seqs, _, rows, width = part.shape
    return comm_call(
        functools.partial(tp_scatter_kernel, n_a),
        name,
        cid,
        jax.ShapeDtypeStruct((seqs, rows, width), F32),
        1,
        VMEM_SPEC,
        [
            pltpu.VMEM((seqs, 2, rows, width), BF16),
            pltpu.VMEM((seqs, rows, width), BF16),
            pltpu.VMEM((seqs, rows, width), BF16),
        ]
        + [DMA((seqs,))] * 4,
    )(part)


def plane_scatter_kernel(n_a, part_ref, out_ref, got_c, mid, got_x, got_y, got_d, send, recv):
    rows = part_ref.shape[1]
    half = rows // 2
    h0, h1 = pl.ds(0, half), pl.ds(half, half)
    x, y, c = x_peer(n_a), y_peer(n_a), c_peer(n_a)
    greet([x, y, c])
    sems = (send, recv)
    to_c = [remote(part_ref.at[2 * k + 1], got_c.at[k], sems, k, c) for k in range(4)]
    xd = remote(mid.at[3, h0], got_d.at[h0], sems, 4, x)
    yd = remote(mid.at[3, h1], got_d.at[h1], sems, 5, y)
    x0 = remote(mid.at[2, h0], got_x.at[h0], sems, 6, x)
    x1 = remote(mid.at[2, h1], got_x.at[h1], sems, 7, x)
    y0 = remote(mid.at[1, h0], got_y.at[h0], sems, 8, y)
    y1 = remote(mid.at[1, h1], got_y.at[h1], sems, 9, y)
    for k in (3, 2, 1, 0):
        to_c[k].start()

    def fold(k):
        to_c[k].wait_recv()
        mid[k] = (part_ref[2 * k].astype(F32) + got_c[k].astype(F32)).astype(BF16)

    fold(3)
    xd.start()
    yd.start()
    fold(2)
    x0.start()
    fold(1)
    y1.start()
    to_c[0].wait_recv()
    out_ref[...] = part_ref[0].astype(F32) + got_c[0].astype(F32)
    xd.wait_recv()
    mid[1, h0] = (mid[1, h0].astype(F32) + got_d[h0].astype(F32)).astype(BF16)
    y0.start()
    yd.wait_recv()
    mid[2, h1] = (mid[2, h1].astype(F32) + got_d[h1].astype(F32)).astype(BF16)
    x1.start()
    x0.wait_recv()
    y1.wait_recv()
    y0.wait_recv()
    x1.wait_recv()
    out_ref[...] = out_ref[...] + got_x[...].astype(F32) + got_y[...].astype(F32)
    for copy in to_c + [xd, yd, x0, x1, y0, y1]:
        copy.wait_send()


def plane_scatter(part):
    n_a = lax.axis_size("fsdp") // 2
    _, rows, width = part.shape
    return comm_call(
        functools.partial(plane_scatter_kernel, n_a),
        "plane_scatter",
        7,
        jax.ShapeDtypeStruct((rows, width), F32),
        1,
        VMEM_SPEC,
        [
            pltpu.VMEM((4, rows, width), BF16),
            pltpu.VMEM((4, rows, width), BF16),
            pltpu.VMEM((rows, width), BF16),
            pltpu.VMEM((rows, width), BF16),
            pltpu.VMEM((rows, width), BF16),
            DMA((10,)),
            DMA((10,)),
        ],
    )(part)


def plane_scatter_lazy(part):
    _, rows, width = part.shape
    part = part.reshape(4, 2, rows, width)
    part = part[:, 0].astype(F32) + swap_tp(part[:, 1], 1).astype(F32)
    part = part[:2] + swap_b(part[2:].astype(BF16)).astype(F32)
    return part[0] + swap_tp(part[1].astype(BF16), 2).astype(F32)


def kv_scatter_kernel(n_a, part_ref, out_ref, got, send, recv):
    a, b, tp = coords(n_a)
    peers = [
        (e, d, lax.rem(a + d, n_a), lax.rem(b + e, 2))
        for d in range(n_a)
        for e in range(2)
        if (d, e) != (0, 0)
    ]
    greet([(pa * 2 + pb, tp) for _, _, pa, pb in peers])
    copies = [
        remote(
            part_ref.at[e, pa], got.at[2 * d + e - 1], (send, recv), 2 * d + e - 1,
            (pa * 2 + pb, tp),
        )
        for e, d, pa, pb in peers
    ]
    for copy in copies:
        copy.start()
    total = part_ref[0, a].astype(F32)
    for i, copy in enumerate(copies):
        copy.wait_recv()
        total = total + got[i].astype(F32)
    out_ref[...] = total
    for copy in copies:
        copy.wait_send()


def kv_scatter(part):
    n_a = part.shape[1]
    n = 2 * n_a - 1
    return comm_call(
        functools.partial(kv_scatter_kernel, n_a),
        "kv_scatter",
        3,
        jax.ShapeDtypeStruct(part.shape[2:], F32),
        1,
        VMEM_SPEC,
        [pltpu.VMEM((n,) + part.shape[2:], part.dtype), DMA((n,)), DMA((n,))],
    )(part)


def gain_kernel(n_a, part_ref, out_ref, got, send, recv):
    a, b, tp = coords(n_a)
    n_dev = n_a * 8
    me = (a * 2 + b) * 4 + tp
    barrier = pltpu.get_barrier_semaphore()

    def peer(k):
        return lax.rem(me + k, n_dev)

    @pl.loop(1, n_dev)
    def _(k):
        p = peer(k)
        pl.semaphore_signal(barrier, inc=1, device_id=(p // 4, p % 4), device_id_type=MESH_ID)

    pl.semaphore_wait(barrier, n_dev - 1)

    def copy(k):
        p = peer(k)
        return remote(part_ref.at[p], got.at[k], (send, recv), k, (p // 4, p % 4))

    @pl.loop(1, n_dev)
    def _(k):
        copy(k).start()

    got[0] = part_ref[me]

    @pl.loop(1, n_dev)
    def _(k):
        copy(k).wait()

    out_ref[...] = jnp.sum(got[...], axis=0)


def scatter_gains(part):
    n_a = lax.axis_size("fsdp") // 2
    n = part.shape[0]
    return comm_call(
        functools.partial(gain_kernel, n_a),
        "gain_scatter",
        4,
        jax.ShapeDtypeStruct(part.shape[1:], F32),
        1,
        VMEM_SPEC,
        [pltpu.VMEM(part.shape, F32), DMA((n,)), DMA((n,))],
    )(part)


def row_offsets(idx, rows, y, c):
    ec = idx // (2 * rows)
    ey = (idx // rows) % 2
    return ((ey ^ y) * 2 + (ec ^ c)) * rows + idx % rows


def fill_bias(bias_ref, tab_ref, s, n_blocks, block, rows):
    y = tab_ref[s, n_blocks + 2]
    c = tab_ref[s, n_blocks + 3]
    prefix = tab_ref[s, n_blocks + 1]
    koff = row_offsets(lax.broadcasted_iota(jnp.int32, (block, block), 0), rows, y, c)
    qoff = row_offsets(lax.broadcasted_iota(jnp.int32, (block, block), 1), rows, y, c)
    qpos = qoff + tab_ref[s, n_blocks] * block
    for kb in range(n_blocks):
        kpos = koff + tab_ref[s, kb] * block
        ok = (kpos <= qpos) | (kpos < prefix)
        bias_ref[kb * block : (kb + 1) * block, :] = jnp.where(ok, 0.0, NEG)


def fwd_kernel(n_blocks, block, rows, step, tab_ref, q_ref, kv_ref, vt_ref, o_ref, lse_ref, bias_ref):
    s = pl.program_id(0)

    @pl.when(pl.program_id(1) == 0)
    def _():
        fill_bias(bias_ref, tab_ref, s, n_blocks, block, rows)

    q = q_ref[...]
    qz = jnp.concatenate([q, jnp.zeros_like(q)], axis=0)
    seq = n_blocks * block
    m = jnp.full((1, block), -jnp.inf, F32)
    l = jnp.zeros((1, block), F32)
    acc = jnp.zeros((HD, block), F32)
    for k0 in range(0, seq, step):
        sc = dot(kv_ref[k0 : k0 + step, :], qz, 1, 0) + bias_ref[k0 : k0 + step, :]
        m_new = jnp.maximum(m, jnp.max(sc, axis=0, keepdims=True))
        alpha = jnp.exp(m - m_new)
        p = jnp.exp(sc - m_new)
        l = l * alpha + jnp.sum(p, axis=0, keepdims=True)
        acc = acc * alpha + dot(vt_ref[:, k0 : k0 + step], p.astype(BF16), 1, 0)
        m = m_new
    o_ref[...] = (acc / l).astype(BF16)
    lse_ref[0] = m + jnp.log(l)


def bwd_kernel(
    n_blocks, block, rows, step, tab_ref, q_ref, kv_ref, kt_ref, go_ref, o_ref, lse_ref,
    dq_ref, dkv_ref, bias_ref, dkv_acc,
):
    s = pl.program_id(0)
    h = pl.program_id(1)

    @pl.when(h == 0)
    def _():
        fill_bias(bias_ref, tab_ref, s, n_blocks, block, rows)
        dkv_acc[...] = jnp.zeros_like(dkv_acc)

    q = q_ref[...]
    go = go_ref[...]
    zero = jnp.zeros_like(q)
    qz = jnp.concatenate([q, zero], axis=0)
    gz = jnp.concatenate([zero, go], axis=0)
    lse = lse_ref[0]
    delta = jnp.sum(go.astype(F32) * o_ref[...].astype(F32), axis=0, keepdims=True)
    seq = n_blocks * block
    dq = jnp.zeros((HD, block), F32)
    for k0 in range(0, seq, step):
        ks = slice(k0, k0 + step)
        kv = kv_ref[ks, :]
        p = jnp.exp(dot(kv, qz, 1, 0) + bias_ref[ks, :] - lse)
        ds = (p * (dot(kv, gz, 1, 0) - delta)).astype(BF16)
        dkv_acc[HD:, ks] += dot(go, p.astype(BF16), 1, 1)
        dkv_acc[:HD, ks] += dot(q, ds, 1, 1)
        dq = dq + dot(kt_ref[:, ks], ds, 1, 0)
    dq_ref[...] = dq

    @pl.when(h == pl.num_programs(1) - 1)
    def _():
        dkv_ref[...] = dkv_acc[...].T.astype(BF16)


def attention_specs(n_blocks, block):
    seq = n_blocks * block
    q_spec = pl.BlockSpec((HD, block), lambda s, h, t: (h, s))
    kv_spec = pl.BlockSpec((seq, 2 * HD), lambda s, h, t: (0, s))
    lse_spec = pl.BlockSpec((1, 1, block), lambda s, h, t: (h, 0, s))

    def half_spec(which):
        return pl.BlockSpec((HD, seq), lambda s, h, t: (2 * s + which, 0))

    return q_spec, kv_spec, lse_spec, half_spec


def attention_forward(tab, q_t, kv, kv_t, n_blocks, block, rows):
    heads, seqs, seq = q_t.shape[0] // HD, q_t.shape[1] // block, n_blocks * block
    q_spec, kv_spec, lse_spec, half_spec = attention_specs(n_blocks, block)
    return pl.pallas_call(
        functools.partial(fwd_kernel, n_blocks, block, rows, min(512, seq)),
        name="attn_fwd",
        out_shape=(
            jax.ShapeDtypeStruct(q_t.shape, BF16),
            jax.ShapeDtypeStruct((heads, 1, seqs * block), F32),
        ),
        grid_spec=pltpu.PrefetchScalarGridSpec(
            num_scalar_prefetch=1,
            grid=(seqs, heads),
            in_specs=[q_spec, kv_spec, half_spec(1)],
            out_specs=[q_spec, lse_spec],
            scratch_shapes=[pltpu.VMEM((seq, block), F32)],
        ),
        compiler_params=pltpu.CompilerParams(
            dimension_semantics=("arbitrary", "arbitrary"), vmem_limit_bytes=48 << 20
        ),
        cost_estimate=pl.CostEstimate(
            flops=16 * heads * seqs * block * seq * HD,
            bytes_accessed=4 * seqs * seq * 2 * HD,
            transcendentals=heads * seqs * block * seq,
        ),
    )(tab, q_t, kv, kv_t)


def attention_backward(tab, q_t, kv, kv_t, go_t, o_t, lse, n_blocks, block, rows):
    heads, seqs, seq = q_t.shape[0] // HD, q_t.shape[1] // block, n_blocks * block
    q_spec, kv_spec, lse_spec, half_spec = attention_specs(n_blocks, block)
    return pl.pallas_call(
        functools.partial(bwd_kernel, n_blocks, block, rows, min(512, seq)),
        name="attn_bwd",
        out_shape=(
            jax.ShapeDtypeStruct(q_t.shape, F32),
            jax.ShapeDtypeStruct((seq, seqs * 2 * HD), BF16),
        ),
        grid_spec=pltpu.PrefetchScalarGridSpec(
            num_scalar_prefetch=1,
            grid=(seqs, heads),
            in_specs=[q_spec, kv_spec, half_spec(0), q_spec, q_spec, lse_spec],
            out_specs=[q_spec, kv_spec],
            scratch_shapes=[pltpu.VMEM((seq, block), F32), pltpu.VMEM((2 * HD, seq), F32)],
        ),
        compiler_params=pltpu.CompilerParams(
            dimension_semantics=("arbitrary", "arbitrary"), vmem_limit_bytes=48 << 20
        ),
        cost_estimate=pl.CostEstimate(
            flops=40 * heads * seqs * block * seq * HD,
            bytes_accessed=8 * seqs * seq * 2 * HD,
            transcendentals=heads * seqs * block * seq,
        ),
    )(tab, q_t, kv, kv_t, go_t, o_t, lse)


def on_device(
    hidden_in, cotangent, gain_attn, w_query, w_key, w_value, w_out, gain_mlp, w_gate, w_up,
    w_down, prefix, block_order,
):
    seqs, rows, width = hidden_in.shape
    n_tp = lax.axis_size("tp")
    n_fsdp = lax.axis_size("fsdp")
    if n_tp != 4 or n_fsdp % 2 or w_key.shape[1] != HD:
        raise ValueError("unsupported mesh")
    n_a = n_fsdp // 2
    block = rows * n_tp
    tokens = seqs * block
    own = seqs * rows
    chunk = width // n_fsdp
    q_width = w_query.shape[1]
    ff = w_gate.shape[1] // 2
    fsdp_index = lax.axis_index("fsdp")
    b_idx = fsdp_index % 2
    tp_index = lax.axis_index("tp")
    y_idx, c_idx = tp_index // 2, tp_index % 2
    first = b_idx == 0

    def order(mine, other, axis):
        return jnp.concatenate(
            [jnp.where(first, mine, other), jnp.where(first, other, mine)], axis=axis
        )

    own_block = jnp.sum(
        jnp.where(jnp.arange(n_fsdp)[None, :] == fsdp_index, block_order, 0), axis=1
    )
    by_b = block_order.reshape(seqs, n_a, 2)
    even, odd = by_b[:, :, 0], by_b[:, :, 1]
    key_blocks = jnp.concatenate(
        [jnp.where(first, even, odd), jnp.where(first, odd, even)], axis=1
    )
    tab = jnp.concatenate(
        [
            key_blocks,
            own_block[:, None],
            prefix[:, None],
            jnp.broadcast_to(y_idx, (seqs, 1)),
            jnp.broadcast_to(c_idx, (seqs, 1)),
        ],
        axis=1,
    ).astype(jnp.int32)
    lane = jnp.arange(block, dtype=jnp.int32)
    offs = row_offsets(lane, rows, y_idx, c_idx)
    pos = (own_block[:, None] * block + offs[None, :]).reshape(tokens)
    frequency = THETA ** (-(jnp.arange(HD // 2, dtype=F32) * 2.0 / HD))
    angles = frequency[:, None] * pos.astype(F32)[None, :]
    cos_t = jnp.cos(angles)[None]
    sin_t = jnp.sin(angles)[None]

    def rotate_t(v):
        v = v.reshape(-1, HD, tokens)
        u1, u2 = v[:, : HD // 2], v[:, HD // 2 :]
        return jnp.concatenate(
            [u1 * cos_t - u2 * sin_t, u2 * cos_t + u1 * sin_t], axis=1
        ).reshape(-1, tokens)

    def rotate_back_t(v):
        v = v.reshape(-1, HD, tokens)
        u1, u2 = v[:, : HD // 2], v[:, HD // 2 :]
        return jnp.concatenate(
            [u1 * cos_t + u2 * sin_t, u2 * cos_t - u1 * sin_t], axis=1
        ).reshape(-1, tokens)

    piece = gain_attn.shape[0]
    fill = -2 * piece % 128
    gain_row = jnp.pad(jnp.concatenate([gain_attn, gain_mlp]), (0, fill))
    gain_row = jnp.broadcast_to(gain_row[None], (8, 2 * piece + fill))
    mlp_w = jnp.stack([w_gate, w_up, w_down.T])
    mlp_lo, mlp_hi = mlp_w[..., :ff], mlp_w[..., ff:]
    out_own = gather_a(w_out.T)
    qkv_w, x_all, gains, mlp_got = prologue(
        jnp.concatenate([w_query, w_key, w_value], axis=1),
        hidden_in,
        gain_row,
        jnp.where(first, mlp_hi, mlp_lo),
    )
    out_other = swap_b(out_own)
    out_w = order(
        out_own.reshape(n_a, 1, chunk, -1), out_other.reshape(n_a, 1, chunk, -1), 1
    ).reshape(width, -1)
    mlp_pair = order(jnp.where(first, mlp_lo, mlp_hi), mlp_got, 1)
    gate_w = gather_a(mlp_pair[0])
    up_w = gather_a(mlp_pair[1])
    down_w = gather_a(mlp_pair[2])
    gains = gains[:, 0]
    gain_first = gains[:, :piece].reshape(width)
    gain_second = gains[:, piece : 2 * piece].reshape(width)
    qkv_w = qkv_w.reshape(width, -1)
    cot = cotangent.reshape(own, width)

    x_all = x_all.reshape(seqs * block, width).astype(F32)
    h_first = (x_all * inverse_rms(x_all) * gain_first).astype(BF16)
    qkv_t = dot(qkv_w, h_first, 0, 1)
    q_t = (rotate_t(qkv_t[:q_width]).astype(BF16) * (HD**-0.5)).astype(BF16)
    kv_t = jnp.concatenate(
        [rotate_t(qkv_t[q_width : q_width + HD]), qkv_t[q_width + HD :]], axis=0
    ).astype(BF16)
    kv_own = (
        kv_t.reshape(2 * HD, seqs, block).transpose(2, 1, 0).reshape(block, seqs * 2 * HD)
    )
    kv, gm = kv_gather(kv_own, cot.astype(BF16))
    kv = kv.reshape(n_fsdp * block, -1)
    gm = gm.reshape(8 * own, width)
    kv_all_t = kv.T
    o_t, lse = attention_forward(tab, q_t, kv, kv_all_t, n_fsdp, block, rows)

    x_own = hidden_in.astype(F32).reshape(own, width)
    rms_first = inverse_rms(x_own)
    part = dot(o_t, out_w, 0, 1).astype(BF16).reshape(seqs, 4, rows, width)
    middle = x_own + tp_scatter(part, "out_scatter", 8).reshape(own, width)
    rms_second = inverse_rms(middle)
    h_second = plane_gather((middle * rms_second * gain_second).astype(BF16)).reshape(
        8 * own, width
    )

    gate = dot(h_second, gate_w, 1, 0)
    up = dot(h_second, up_w, 1, 0)
    sig = jax.nn.sigmoid(gate)
    hidden = (gate * sig * up).astype(BF16)
    down_g = scatter_a(dot(gm, hidden, 0, 0).astype(BF16))
    g_hidden = dot(gm, down_w, 1, 0)
    g_gate = (g_hidden * up * sig * (1.0 + gate * (1.0 - sig))).astype(BF16)
    g_up = (g_hidden * gate * sig).astype(BF16)
    g_h2 = (dot(g_gate, gate_w, 1, 1) + dot(g_up, up_w, 1, 1)).astype(BF16)
    g_h2 = plane_scatter(g_h2.reshape(8, own, width))
    gate_g = scatter_a(dot(h_second, g_gate, 0, 0).astype(BF16))
    up_g = scatter_a(dot(h_second, g_up, 0, 0).astype(BF16))
    layer_out = middle + plane_scatter_lazy(
        dot(hidden, down_w, 1, 1).astype(BF16).reshape(8, own, width)
    )
    g_mid_norm, gain_second_sum = norm_back(g_h2, middle, gain_second, rms_second)
    g_mid = cot + g_mid_norm

    ga = tp_gather(g_mid.astype(BF16).reshape(seqs, rows, width)).reshape(tokens, width)
    go_t = dot(out_w, ga, 0, 1).astype(BF16)
    dq_t, dkv = attention_backward(
        tab, q_t, kv, kv_all_t, go_t, o_t, lse, n_fsdp, block, rows
    )
    out_g = scatter_a(dot(ga, o_t, 0, 1).astype(BF16))
    dkv_own = kv_scatter(dkv.reshape(2, n_a, block, -1))
    dkv_t = dkv_own.reshape(block, seqs, 2 * HD).transpose(2, 1, 0).reshape(2 * HD, tokens)
    gq_t = rotate_back_t(dq_t * (HD**-0.5)).astype(BF16)
    gk_t = rotate_back_t(dkv_t[:HD]).astype(BF16)
    g_qkv_t = jnp.concatenate([gq_t, gk_t, dkv_t[HD:].astype(BF16)], axis=0)
    qkv_g = scatter_a(dot(h_first, g_qkv_t, 0, 1).astype(BF16))
    part = dot(g_qkv_t, qkv_w, 0, 1).astype(BF16).reshape(seqs, 4, rows, width)
    g_h1 = tp_scatter(part, "in_scatter", 9).reshape(own, width)
    g_in_norm, gain_first_sum = norm_back(g_h1, x_own, gain_first, rms_first)
    g_in = g_mid + g_in_norm
    gain_parts = jnp.concatenate(
        [
            gain_first_sum.reshape(-1, piece),
            gain_second_sum.reshape(-1, piece),
        ],
        axis=1,
    )
    gain_parts = jnp.pad(gain_parts, ((0, 0), (0, fill)))
    gain_parts = jnp.broadcast_to(
        gain_parts[:, None], (n_fsdp * 4, 8, 2 * piece + fill)
    )
    gain_sums = scatter_gains(gain_parts)[0]

    def split(part):
        lo, hi = part[..., :chunk, :], part[..., chunk:, :]
        return jnp.where(first, lo, hi), swap_b(jnp.where(first, hi, lo))

    def settle(part):
        mine, got = split(part)
        return mine.astype(F32) + got.astype(F32)

    out_g = settle(out_g)
    qkv_g = settle(qkv_g)
    mlp_g = order(*split(jnp.stack([gate_g, up_g, down_g])), 2).astype(F32)
    return (
        layer_out.reshape(hidden_in.shape),
        g_in.reshape(hidden_in.shape),
        gain_sums[:piece],
        qkv_g[:, :q_width],
        qkv_g[:, q_width : q_width + HD],
        qkv_g[:, q_width + HD :],
        out_g.T,
        gain_sums[piece : 2 * piece],
        mlp_g[0],
        mlp_g[1],
        mlp_g[2].T,
    )


def solution(mesh):
    rows = P(None, ("fsdp", "tp"), None)
    gain = P(("fsdp", "tp"))
    col = P("fsdp", "tp")
    row = P("tp", "fsdp")
    return jax.shard_map(
        on_device,
        mesh=mesh,
        in_specs=(rows, rows, gain, col, col, col, row, gain, col, col, row, P(), P()),
        out_specs=(rows, rows, gain, col, col, col, row, gain, col, col, row),
        check_vma=False,
    )
```

time: 990 us -> 707 us (0.71)
  waiting for transfers between devices: 479 us -> 26.8 us
  Pallas kernels: 263 us -> 435 us
  starting transfers between devices: 23.7 us -> 6.44 us
  other arithmetic: 39.4 us -> 55.2 us
    ppermute x7 -> x5, waiting for transfers between devices: 337 us -> 21.7 us  [swap_b(): return lax.ppermute(v, 'fsdp', [(i, i ^ 1) for i in range(n)])]
    pallas_call x4 -> x9, Pallas kernels: 175 us -> 347 us  [the longest x1 65.1 us: kv_gather(): comm_call(functools.partial(kv_gather_kernel, n_a), 'kv_gather', 2, (jax....]
    ppermute x22 -> x2, waiting for transfers between devices: 101 us -> 3.1 us  [swap_tp(): return lax.ppermute(v, 'tp', [(i, i ^ bit) for i in range(n)])]
    reduce_scatter x4 -> x5, waiting for transfers between devices: 37.5 us -> 0.01 us  [scatter_a(): lax.psum_scatter(part, 'fsdp', scatter_dimension=0, tiled=True, axis_inde...]
    ppermute x22 -> x2, starting transfers between devices: 14.5 us -> 1.75 us  [swap_tp(): return lax.ppermute(v, 'tp', [(i, i ^ bit) for i in range(n)])]
    unnamed x129 -> x107, local copies, waits for them, and re-layouts: 18.2 us -> 24.1 us
    dot_general x24 -> x15, matrix products: 105 us -> 102 us  [dot(): lax.dot_general(a, b, (((ca,), (cb,)), ((), ())), preferred_element_type=...]
  transfers between devices with their start and end apart: 36 -> 16, of which waited for: 19 -> 4; matrix products, arithmetic and copies ran while one was open for 14% -> 25% of each run, Pallas kernels for 18% -> 62%
where the time goes in v3:
time: 707 us; the launch traced here: 698 us
  Pallas kernels  435 us (62%)
  matrix products  102 us (14%)
  local copies, waits for them, and re-layouts  56.8 us (8%)
  other arithmetic  55.2 us (8%)
  waiting for transfers between devices  26.8 us (4%)
  between operations  15.3 us (2%)
    dot_general x15, matrix products, dot(): lax.dot_general(a, b, (((ca,), (cb,)), ((), ())), preferred_element_type=...  102 us
    pallas_call x1, Pallas kernels, kv_gather(): comm_call(functools.partial(kv_gather_kernel, n_a), 'kv_gather', 2, (jax....  65.1 us
    pallas_call x1, Pallas kernels, prologue(): comm_call(functools.partial(prologue_kernel, n_a), 'prologue', 1, (jax.Sh...  63.6 us
    pallas_call x1, Pallas kernels, kv_scatter(): comm_call(functools.partial(kv_scatter_kernel, n_a), 'kv_scatter', 3, jax...  61.7 us
    pallas_call x1, Pallas kernels, attention_backward(): pl.pallas_call(functools.partial(bwd_kernel, n_blocks, block, rows, min(5...  44.9 us
    pallas_call x2, Pallas kernels, tp_scatter(): comm_call(functools.partial(tp_scatter_kernel, n_a), name, cid, jax.Shape...  43.9 us
    pallas_call x1, Pallas kernels, attention_forward(): pl.pallas_call(functools.partial(fwd_kernel, n_blocks, block, rows, min(5...  43.2 us
    pallas_call x1, Pallas kernels, plane_scatter(): comm_call(functools.partial(plane_scatter_kernel, n_a), 'plane_scatter',...  33 us
  transfers between devices with their start and end apart: 16, of which 4 were waited for; matrix products, arithmetic and copies ran while one was open for 25% of the time, Pallas kernels for 62%

profile of v3, /device:TPU:8, one launch (start us, length us, event | category | flops | bytes accessed | tf_op | source)
XLA Modules:
  0.0 697.6 jit_solution(5157643172862567068)
XLA Ops:
  14.4 63.6 %prologue.1 = (bf16[4,2,256,640]{3,2,1,0:T(8,128)(2,1)}, bf16[3,4,64,2048]{3,2,1,0:T(8,128)(2,1)}, f32[32,8,128]{2,1,0:T(8,128)S(1)}, bf16[3,256,704]{2,1,0:T(8,128)(2,1)S(1)}) custom-call(bf16[256,640]{1,0:T(8,128)(2,1)S(1)} %pad_maximum_fusion.8.w_ref, bf16[3,64,2048]{2,1,0:T(8,128)(2,1)S(1)} %copy-done, f32[8,128]{1,0:T(8,128)S(1)} %broadcast_in_dim.30.g_ref, ...), custom_call_target="tpu_custom_call" | custom-call | bytes 67108864 | tf_op jit(solution)/shard_map/prologue/pallas_call | solution.py:293
  81.9 2.6 multiply_reduce_fusion
  85.3 2.8 multiply_convert_fusion
  88.1 2.2 fusion.59
  96.9 65.1 %kv_gather.1 = (bf16[2,4,256,384]{3,2,1,0:T(8,128)(2,1)S(1)}, bf16[8,192,2048]{2,1,0:T(8,128)(2,1)}) custom-call(bf16[256,384]{1,0:T(8,128)(2,1)S(1)} %copy.111.own_ref, bf16[192,2048]{1,0:T(8,128)(2,1)S(1)} %bitcast_convert_fusion.gm_ref), custom_call_target="tpu_custom_call" | custom-call | bytes 67108864 | tf_op jit(solution)/shard_map/kv_gather/pallas_call | solution.py:325
  167.4 43.2 %attn_fwd.1 = (bf16[512,768]{1,0:T(8,128)(2,1)S(1)}, f32[8,1,768]{2,1,0:T(1,128)S(1)}) custom-call(s32[3,12]{1,0:T(4,128)S(1)} %concatenate.49.tab_ref, bf16[512,768]{1,0:T(8,128)(2,1)S(1)} %bitcast.162, bf16[2048,384]{1,0:T(8,128)(2,1)S(1)} %bitcast.157, bf16[384,2048]{1,0:T(8,128)(2,1)S(1)} %bitcast.160), custom_call_target="tpu_custom_call" | custom-call | flops 12884901888 | bytes 3145728 | tf_op jit(solution)/shard_map/attn_fwd/pallas_call | solution.py:683
  217.6 1.8 convolution_convert_fusion.1
  219.5 21.9 %out_scatter.1 = f32[3,64,2048]{2,1,0:T(8,128)S(1)} custom-call(bf16[3,4,64,2048]{3,2,1,0:T(8,128)(2,1)S(1)} %bitcast.152), custom_call_target="tpu_custom_call" | custom-call | bytes 67108864 | tf_op jit(solution)/shard_map/out_scatter/pallas_call | solution.py:409
  244.0 30.8 %plane_gather.1 = bf16[8,192,2048]{2,1,0:T(8,128)(2,1)} custom-call(bf16[192,2048]{1,0:T(8,128)(2,1)S(1)} %get-tuple-element.83.own_ref), custom_call_target="tpu_custom_call" | custom-call | bytes 67108864 | tf_op jit(solution)/shard_map/plane_gather/pallas_call | solution.py:349
  274.9 10.5 %fusion.6 = f32[1536,704]{0,1:T(8,128)} fusion(bf16[1536,2048]{1,0:T(8,128)(2,1)} %bitcast.164, bf16[1,2048,704]{2,1,0:T(8,128)(2,1)} %all-gather.12.cloned.1.call-done), kind=kOutput, calls=%fused_computation.26 | convolution fusion | flops 4429185024 | bytes 13500416 | tf_op jit(solution)/shard_map/dot_general | solution.py:32
  285.3 10.9 %fusion.10 = f32[1536,704]{0,1:T(8,128)} fusion(bf16[1536,2048]{1,0:T(8,128)(2,1)} %bitcast.165, bf16[1,2048,704]{2,1,0:T(8,128)(2,1)} %all-gather.10.cloned.1.call-done), kind=kOutput, calls=%fused_computation.30 | convolution fusion | flops 4429185024 | bytes 13500416 | tf_op jit(solution)/shard_map/dot_general | solution.py:32
  296.2 12.8 %multiply_convert_fusion.1 = (bf16[1536,704]{0,1:T(8,128)(2,1)}, bf16[1536,704]{0,1:T(8,128)(2,1)}, bf16[1536,704]{0,1:T(8,128)(2,1)S(1)}) fusion(f32[1536,704]{0,1:T(8,128)} %fusion.10, f32[1536,704]{0,1:T(8,128)} %fusion.6, bf16[1536,2048]{1,0:T(8,128)(2,1)} %bitcast.202, bf16[1,2048,704]{2,1,0:T(8,128)(2,1)} %all-gather.14.cloned.1.call-done), kind=kOutput, calls=%fused_computation.8 | convolution fusion | flops 4446486528 | bytes 24313856 | tf_op jit(solution)/shard_map/dot_general | solution.py:32
  310.3 7.9 %convolution_convert_fusion.3 = bf16[2048,704]{0,1:T(8,128)(2,1)S(1)} fusion(bf16[1536,704]{0,1:T(8,128)(2,1)S(1)} %get-tuple-element.87, bf16[1536,2048]{1,0:T(8,128)(2,1)} %bitcast.203), kind=kOutput, calls=%fused_computation.14 | convolution fusion | flops 4430626816 | bytes 11337728 | tf_op jit(solution)/shard_map/dot_general | solution.py:32
  318.2 2.9 copy.124
  321.1 8.1 %convolution_convert_fusion.5 = bf16[2048,704]{0,1:T(8,128)(2,1)S(1)} fusion(bf16[1536,704]{0,1:T(8,128)(2,1)} %get-tuple-element.86, bf16[1536,2048]{1,0:T(8,128)(2,1)} %bitcast.166), kind=kOutput, calls=%fused_computation.16 | convolution fusion | flops 4430626816 | bytes 11337728 | tf_op jit(solution)/shard_map/dot_general | solution.py:32
  329.2 2.8 copy.122
  332.1 1.8 copy-done.42
  333.9 7.2 %convolution_convert_fusion = bf16[1536,2048]{1,0:T(8,128)(2,1)S(1)} fusion(bf16[1536,704]{0,1:T(8,128)(2,1)} %copy-done.46, bf16[1,2048,704]{2,1,0:T(8,128)(2,1)S(1)} %copy-done.42), kind=kOutput, calls=%fused_computation.1 | convolution fusion | flops 4432330752 | bytes 11337728 | tf_op jit(solution)/shard_map/dot_general | solution.py:32
  341.2 2.0 slice_bitcast_fusion
  343.2 2.2 copy-done.13
  345.8 2.5 fusion.1
  348.3 3.1 collective-permute-done.1
  351.4 6.8 convert_add_fusion
  358.2 3.4 slice.318
  363.0 5.0 convolution_convert_fusion.4
  367.9 2.8 copy.123
  370.8 1.8 copy-done.41
  372.6 9.9 %fusion.8 = f32[1536,2048]{1,0:T(8,128)} fusion(bf16[1536,704]{0,1:T(8,128)(2,1)} %get-tuple-element.86, bf16[1,2048,704]{2,1,0:T(8,128)(2,1)S(1)} %copy-done.41), kind=kOutput, calls=%fused_computation.28 | convolution fusion | flops 4429185024 | bytes 17629184 | tf_op jit(solution)/shard_map/dot_general | solution.py:32
  382.5 16.1 %collective-permute-done.2 = bf16[2,192,2048]{2,1,0:T(8,128)(2,1)} collective-permute-done((bf16[2,192,2048]{2,1,0:T(8,128)(2,1)}, bf16[2,192,2048]{2,1,0:T(8,128)(2,1)}, u32[]{:S(2)}, u32[]{:S(2)}) %collective-permute-start.2) | collective-permute-done | bytes 1572896 | tf_op jit(solution)/shard_map/ppermute | solution.py:37
  398.6 3.0 slice_add_fusion
  403.1 9.9 %add_convert_fusion = bf16[1536,2048]{1,0:T(8,128)(2,1)} fusion(f32[1536,2048]{1,0:T(8,128)} %fusion.8, bf16[1536,704]{0,1:T(8,128)(2,1)S(1)} %copy-done.45, bf16[1,2048,704]{2,1,0:T(8,128)(2,1)S(1)} %copy-done.40), kind=kOutput, calls=%fused_computation | convolution fusion | flops 4435476480 | bytes 23920640 | tf_op jit(solution)/shard_map/dot_general | solution.py:32
  413.0 33.0 %plane_scatter.1 = f32[192,2048]{1,0:T(8,128)S(1)} custom-call(bf16[8,192,2048]{2,1,0:T(8,128)(2,1)} %bitcast.174), custom_call_target="tpu_custom_call" | custom-call | bytes 67108864 | tf_op jit(solution)/shard_map/plane_scatter/pallas_call | solution.py:473
  447.4 2.2 fusion.56
  449.7 22.2 %tp_gather.1 = bf16[3,4,64,2048]{3,2,1,0:T(8,128)(2,1)S(1)} custom-call(bf16[3,64,2048]{2,1,0:T(8,128)(2,1)S(1)} %bitcast.155), custom_call_target="tpu_custom_call" | custom-call | bytes 67108864 | tf_op jit(solution)/shard_map/tp_gather/pallas_call | solution.py:371
  471.8 3.2 convolution_convert_fusion.7
  475.0 4.3 convolution_convert_fusion.8.go_ref
  482.8 44.9 %attn_bwd.1 = (f32[512,768]{1,0:T(8,128)S(1)}, bf16[2048,384]{1,0:T(8,128)(2,1)S(1)}) custom-call(s32[3,12]{1,0:T(4,128)S(1)} %concatenate.49.tab_ref, bf16[512,768]{1,0:T(8,128)(2,1)S(1)} %bitcast.163, bf16[2048,384]{1,0:T(8,128)(2,1)} %bitcast.158, bf16[384,2048]{1,0:T(8,128)(2,1)} %bitcast.159, bf16[512,768]{1,0:T(8,128)(2,1)S(1)} %copy-done.10, ...), custom_call_target="tpu_custom_call" | custom-call | flops 32212254720 | bytes 6291456 | tf_op jit(solution)/shard_map/attn_bwd/pallas_call | solution.py:711
  527.7 61.7 %kv_scatter.1 = f32[256,384]{1,0:T(8,128)S(1)} custom-call(bf16[2,4,256,384]{3,2,1,0:T(8,128)(2,1)S(1)} %bitcast.161), custom_call_target="tpu_custom_call" | custom-call | bytes 67108864 | tf_op jit(solution)/shard_map/kv_scatter/pallas_call | solution.py:530
  592.4 4.0 convolution_convert_fusion.6
  598.4 4.6 convolution_convert_fusion.2
  603.1 21.9 %in_scatter.1 = f32[3,64,2048]{2,1,0:T(8,128)S(1)} custom-call(bf16[3,4,64,2048]{3,2,1,0:T(8,128)(2,1)S(1)} %bitcast.151), custom_call_target="tpu_custom_call" | custom-call | bytes 67108864 | tf_op jit(solution)/shard_map/in_scatter/pallas_call | solution.py:409
  626.1 3.3 pad_maximum_fusion
  634.8 26.7 %gain_scatter.1 = f32[8,128]{1,0:T(8,128)S(1)} custom-call(f32[32,8,128]{2,1,0:T(8,128)S(1)} %broadcast_in_dim.31.part_ref), custom_call_target="tpu_custom_call" | custom-call | bytes 67108864 | tf_op jit(solution)/shard_map/gain_scatter/pallas_call | solution.py:577
  662.1 3.2 fusion.16
  666.3 1.8 broadcast_select_fusion.1
  668.1 2.7 maximum_convert_fusion
  675.7 4.1 slice_bitcast_fusion.3
  683.0 5.1 collective-permute-done.4
  (227 shorter events, 66.3 us)
Async XLA Ops:
  7.2 5.8 copy-start.25
  7.2 5.8 copy-start.26
  7.2 158.5 %all-gather.8.cloned.1.call-start = ((), (), s32[]{:S(2)}) async-start(), calls=%async_computation.5 | async-start | bytes 1310720 | tf_op jit(solution)/shard_map/all_gather | solution.py:51
  7.9 266.9 %all-gather.12.cloned.1.call-start = ((), (), s32[]{:S(2)}) async-start(), calls=%async_computation.12 | async-start | bytes 3932160 | tf_op jit(solution)/shard_map/all_gather | solution.py:51
  80.0 205.3 %all-gather.10.cloned.1.call-start = ((), (), s32[]{:S(2)}) async-start(), calls=%async_computation.11 | async-start | bytes 3932160 | tf_op jit(solution)/shard_map/all_gather | solution.py:51
  80.7 215.5 %all-gather.14.cloned.1.call-start = ((), (), s32[]{:S(2)}) async-start(), calls=%async_computation.13 | async-start | bytes 3932160 | tf_op jit(solution)/shard_map/all_gather | solution.py:51
  81.3 544.8 %reduce-scatter.14.cloned.1.call-start = ((), (), s32[]{:S(2)}) async-start(), calls=%async_computation.10 | async-start | bytes 3932160 | tf_op jit(solution)/shard_map/reduce_scatter | solution.py:55
  84.5 3.6 copy-start.30
  85.3 2.8 copy-start.43
  90.4 3.7 copy-start.14
  92.8 4.0 copy-start.27
  95.3 68.4 %copy-start.21 = (f32[32,768]{1,0:T(8,128)}, f32[32,768]{1,0:T(8,128)S(1)}, u32[]{:S(2)}) copy-start(f32[32,768]{1,0:T(8,128)S(1)} %get-tuple-element.113) | copy-start | bytes 294916
  95.3 68.4 %copy-start.23 = (f32[32,768]{1,0:T(8,128)}, f32[32,768]{1,0:T(8,128)S(1)}, u32[]{:S(2)}) copy-start(f32[32,768]{1,0:T(8,128)S(1)} %get-tuple-element.114) | copy-start | bytes 294916
  162.1 3.9 copy-start.2
  163.7 1.8 copy-start.37
  165.5 45.1 %copy-start.4 = (bf16[8,64,768]{2,1,0:T(8,128)(2,1)}, bf16[8,64,768]{2,1,0:T(8,128)(2,1)S(1)}, u32[]{:S(2)}) copy-start(bf16[8,64,768]{2,1,0:T(8,128)(2,1)S(1)} %maximum_multiply_fusion) | copy-start | bytes 2359300
  165.7 45.9 %collective-permute-start = (bf16[1024,512]{0,1:T(8,128)(2,1)}, bf16[1024,512]{0,1:T(8,128)(2,1)}, u32[]{:S(2)}, u32[]{:S(2)}) collective-permute-start(bf16[1024,512]{0,1:T(8,128)(2,1)} %all-gather.8.cloned.1.call-done), channel_id=1, source_target_pairs={{0,4},{4,0},{8,12},{12,8},{16,20},{20,16},{24,28},{28,24},{1,5},{5... | collective-permute-start | bytes 3145736 | tf_op jit(solution)/shard_map/ppermute | solution.py:37
  167.4 44.1 %copy-start.29 = (f32[32,64]{1,0:T(8,128)S(1)}, f32[32,64]{1,0:T(8,128)}, u32[]{:S(2)}) copy-start(f32[32,64]{1,0:T(8,128)} %get-tuple-element.112) | copy-start | bytes 24580
  217.6 1.9 copy-start.20
  321.1 305.0 %reduce-scatter.10.cloned.1.call-start = ((), (), s32[]{:S(2)}) async-start(), calls=%async_computation.8 | async-start | bytes 3932160 | tf_op jit(solution)/shard_map/reduce_scatter | solution.py:55
  332.0 1.9 copy-start.42
  332.1 294.0 %reduce-scatter.12.cloned.1.call-start = ((), (), s32[]{:S(2)}) async-start(), calls=%async_computation.9 | async-start | bytes 3932160 | tf_op jit(solution)/shard_map/reduce_scatter | solution.py:55
  341.1 4.2 copy-start.13
  341.2 4.5 copy-start.31
  341.2 4.6 copy-start.11
  345.4 6.0 collective-permute-start.1
  345.8 17.2 %slice-start = ((s8[6291456]{0:T(1024)(128)(4,1)}), s8[4194304]{0:T(1024)(128)(4,1)S(1)}, s32[]{:S(2)}) async-start(s8[6291456]{0:T(1024)(128)(4,1)} %bitcast.167), calls=%async_computation.14 | async-start | bytes 8388608
  348.3 14.7 %slice-start.1 = ((s8[6291456]{0:T(1024)(128)(4,1)}), s8[2097152]{0:T(1024)(128)(4,1)S(1)}, s32[]{:S(2)}) async-start(s8[6291456]{0:T(1024)(128)(4,1)} %bitcast.167), calls=%async_computation.15 | async-start | bytes 4194304
  358.2 4.8 copy-start.44
  361.6 37.0 %collective-permute-start.2 = (bf16[2,192,2048]{2,1,0:T(8,128)(2,1)}, bf16[2,192,2048]{2,1,0:T(8,128)(2,1)}, u32[]{:S(2)}, u32[]{:S(2)}) collective-permute-start(bf16[2,192,2048]{2,1,0:T(8,128)(2,1)} %slice.318), channel_id=1, source_target_pairs={{0,4},{4,0},{8,12},{12,8},{16,20},{20,16},{24,28},{28,24},{1,5},{5... | collective-permute-start | bytes 4718600 | tf_op jit(solution)/shard_map/ppermute | solution.py:37
  370.7 1.9 copy-start.41
  370.7 300.0 %reduce-scatter.8.cloned.1.call-start = ((), (), s32[]{:S(2)}) async-start(), calls=%async_computation.7 | async-start | bytes 2621440 | tf_op jit(solution)/shard_map/reduce_scatter | solution.py:55
  382.5 20.6 %copy-start.40 = (bf16[1,2048,704]{2,1,0:T(8,128)(2,1)S(1)}, bf16[1,2048,704]{2,1,0:T(8,128)(2,1)}, u32[]{:S(2)}) copy-start(bf16[1,2048,704]{2,1,0:T(8,128)(2,1)} %all-gather.12.cloned.1.call-done) | copy-start | bytes 8650756
  382.5 20.6 %copy-start.45 = (bf16[1536,704]{0,1:T(8,128)(2,1)S(1)}, bf16[1536,704]{0,1:T(8,128)(2,1)}, u32[]{:S(2)}) copy-start(bf16[1536,704]{0,1:T(8,128)(2,1)} %get-tuple-element.85) | copy-start | bytes 6488068
  401.7 44.9 %collective-permute-start.3 = (bf16[192,2048]{1,0:T(8,128)(2,1)S(1)}, bf16[192,2048]{1,0:T(8,128)(2,1)S(1)}, u32[]{:S(2)}, u32[]{:S(2)}) collective-permute-start(bf16[192,2048]{1,0:T(8,128)(2,1)S(1)} %fusion.24), channel_id=1, source_target_pairs={{0,2},{1,3},{2,0},{3,1},{4,6},{5,7},{6,4},{7,5},{8,10},{9,11},{10,... | collective-permute-start | bytes 2359304 | tf_op jit(solution)/shard_map/ppermute | solution.py:42
  413.0 33.1 %copy-start.12 = (f32[192,2048]{1,0:T(8,128)S(1)}, f32[192,2048]{1,0:T(8,128)}, u32[]{:S(2)}) copy-start(f32[192,2048]{1,0:T(8,128)} %get-tuple-element.84) | copy-start | bytes 4718596
  449.7 22.2 %copy-start.8 = (bf16[512,768]{1,0:T(8,128)(2,1)S(1)}, bf16[512,768]{1,0:T(8,128)(2,1)}, u32[]{:S(2)}) copy-start(bf16[512,768]{1,0:T(8,128)(2,1)} %copy-done.6) | copy-start | bytes 2359300
  479.3 194.0 %reduce-scatter.6.cloned.1.call-start = ((), (), s32[]{:S(2)}) async-start(), calls=%async_computation.6 | async-start | bytes 3276800 | tf_op jit(solution)/shard_map/reduce_scatter | solution.py:55
  527.7 62.2 %copy-start.28 = (f32[768]{0:T(1024)S(1)}, f32[768]{0:T(1024)}, u32[]{:S(2)}) copy-start(f32[768]{0:T(1024)} %copy-done.27) | copy-start | bytes 9220
  527.7 62.2 %copy-start.38 = (f32[32]{0:T(128)S(1)}, f32[32]{0:T(128)}, u32[]{:S(2)}) copy-start(f32[32]{0:T(128)} %negate_power_fusion) | copy-start | bytes 388
  590.5 1.9 copy-start.17
  597.2 5.9 copy-start.32
  603.1 22.0 %copy-start.1 = (bf16[3,64,2048]{2,1,0:T(8,128)(2,1)S(1)}, bf16[3,64,2048]{2,1,0:T(8,128)(2,1)}, u32[]{:S(2)}) copy-start(bf16[3,64,2048]{2,1,0:T(8,128)(2,1)} %x_ref.1) | copy-start | bytes 2359300
  632.6 32.7 %collective-permute-start.6 = (bf16[3,256,704]{1,2,0:T(8,128)(2,1)}, bf16[3,256,704]{1,2,0:T(8,128)(2,1)S(1)}, u32[]{:S(2)}, u32[]{:S(2)}) collective-permute-start(bf16[3,256,704]{1,2,0:T(8,128)(2,1)} %copy.125), channel_id=1, source_target_pairs={{0,4},{4,0},{8,12},{12,8},{16,20},{20,16},{24,28},{28,24},{1,5},{5... | collective-permute-start | bytes 3244040 | tf_op jit(solution)/shard_map/ppermute | solution.py:37
  672.5 9.4 %collective-permute-start.5 = (bf16[256,512]{1,0:T(8,128)(2,1)}, bf16[256,512]{1,0:T(8,128)(2,1)S(1)}, u32[]{:S(2)}, u32[]{:S(2)}) collective-permute-start(bf16[256,512]{1,0:T(8,128)(2,1)} %broadcast_select_fusion.11), channel_id=1, source_target_pairs={{0,4},{4,0},{8,12},{12,8},{16,20},{20,16},{24,28},{28,24},{1,5},{5... | collective-permute-start | bytes 786440 | tf_op jit(solution)/shard_map/ppermute | solution.py:37
  674.5 13.6 %collective-permute-start.4 = (bf16[256,640]{1,0:T(8,128)(2,1)S(1)}, bf16[256,640]{1,0:T(8,128)(2,1)S(1)}, u32[]{:S(2)}, u32[]{:S(2)}) collective-permute-start(bf16[256,640]{1,0:T(8,128)(2,1)S(1)} %broadcast_select_fusion.10), channel_id=1, source_target_pairs={{0,4},{4,0},{8,12},{12,8},{16,20},{20,16},{24,28},{28,24},{1,5},{5... | collective-permute-start | bytes 983048 | tf_op jit(solution)/shard_map/ppermute | solution.py:37
  679.8 2.1 copy-start.19
  679.8 8.3 %copy-start.18 = (bf16[512,640]{1,0:T(8,128)(2,1)S(1)}, bf16[512,640]{1,0:T(8,128)(2,1)}, u32[]{:S(2)}) copy-start(bf16[512,640]{1,0:T(8,128)(2,1)} %reduce-scatter.6.cloned.1.call-done) | copy-start | bytes 1966084
  (17 other events, 21.6 us)
Sparse Core Ops, SparseCore 0:
  9.6 52.0 all-gather.7
  80.1 82.6 all-gather.11
  164.4 63.5 all-gather.9
  230.0 62.0 all-gather.13
  321.2 63.6 reduce-scatter.13
  387.1 60.2 reduce-scatter.9
  449.7 60.2 reduce-scatter.11
  512.4 69.6 reduce-scatter.7
  596.5 53.2 reduce-scatter.5
